TPU v7x, 32 devices: a whole 2x2x4 slice. The times are simulated.
32 devices in a mesh: dom: 4 (over y, core), slab: 8 (over z, x).
Axes of the slice: x: 2, y: 2, z: 4, core: 2. Of those that a mesh axis runs over, the one named last changes fastest.
Arguments:
- heat_level: float32 [524288], P(('dom', 'slab')), may hold values from -6 to 6
- emitting_vertex_position: int32 [32, 3, 3, 8192], P(('dom', 'slab')), may hold values from 0 to 16383
- corner_holder_shift: int32 [4, 32, 64, 512], P(None, 'dom', 'slab'), may hold values from 0 to 8, as said below
- corner_fetched_bucket: int32 [4, 32, 64, 512], P(None, 'dom', 'slab'), may hold values from 0 to 8191
- corner_factors: float32 [4, 32, 64, 512], P(None, 'dom', 'slab'), may hold values from 0.05 to 0.5
- diagonal_rigidity: float32 [32, 64, 512], P('dom', 'slab'), may hold values from 0.25 to 2
- boundary_vertex_position: int32 [32, 3, 3, 128], P(('dom', 'slab')), may hold values from 0 to 32767
- boundary_bucket_tally: int32 [32, 9], P(('dom', 'slab')), may hold values from 1 to 128, 576 in all within a row
- boundary_accepting_vertex: int32 [32, 3, 3, 128], P(('dom', 'slab')), may hold values from 0 to 16383
Outputs:
- displacement: float32 [3, 32, 64, 512], P(None, 'dom', 'slab')
- thermal_disp: float32 [3, 524288], P(None, ('dom', 'slab'))
Inputs may be any that keep to these rules, and one draw needn't show every extreme that they name: emitting_vertex_position stays below 16384. corner_holder_shift is 3 a + b for an offset (a, b) of the hex node's device that names a device inside the mesh.
All inputs are finite; a program needn't handle non-finite values.
Results may differ from a plain program's by a relative error of at most 0.0001.
Values sent between devices are 32-bit elements; how exact they have to be, the bound alone decides.
No kernel may reach another device: no remote copies, remote signals or barrier semaphores. Data moves between devices by JAX's collectives and lax.ppermute only.
A program may use at most 192 MiB of HBM per device.

v0:
```python
import math

import jax
import jax.numpy as jnp
from jax import lax
from jax.sharding import PartitionSpec as P

ITERS = 4


COEF = 0.5


def with_halo(shard, sides, width):
    for axis, dim in sides:
        peers, length = (lax.axis_size(axis), shard.shape[dim])
        up = [(i, (i + 1) % peers) for i in range(peers - 1)]
        down = [(j, i) for i, j in up]
        last = lax.slice_in_dim(shard, length - width, length, axis=dim)
        leading = lax.slice_in_dim(shard, 0, width, axis=dim)
        before = lax.ppermute(last, axis, up)
        after = lax.ppermute(leading, axis, down)
        shard = jnp.concatenate([before, shard, after], axis=dim)
    return shard


def fetch_entries(source_table, positions):
    entry_count = source_table.shape[0]
    lane_count = math.gcd(entry_count, 128)
    table_rows = source_table.reshape(entry_count // lane_count, lane_count)
    picked = table_rows[positions // lane_count]
    lane_ids = jnp.arange(lane_count, dtype=jnp.int32)
    chosen = lane_ids == (positions % lane_count)[..., None]
    return jnp.sum(jnp.where(chosen, picked, jnp.zeros_like(picked)), axis=-1)


def spread_entries(values, positions, entry_count):
    lane_count = math.gcd(entry_count, 128)
    row_count = entry_count // lane_count
    row_hot = (
        (positions // lane_count)[:, None] == jnp.arange(row_count, dtype=jnp.int32)[None, :]
    ).astype(jnp.float32)
    lane_hot = (
        (positions % lane_count)[:, None] == jnp.arange(lane_count, dtype=jnp.int32)[None, :]
    ).astype(jnp.float32)
    weighted = values[:, :, None] * lane_hot[None]
    summed = jnp.einsum("kh,ckl->chl", row_hot, weighted, precision=lax.Precision.HIGHEST)
    return summed.reshape(values.shape[0], entry_count)


def operate(bucket_entries, diagonal_rigidity, padded=None):
    padded = with_halo(bucket_entries, (("dom", 1), ("slab", 2)), 1)
    interior = padded[:, 1:-1, 1:-1, :]
    along_z = jnp.pad(interior, ((0, 0), (0, 0), (0, 0), (1, 1)))
    beside = padded[:, 2:, 1:-1, :] + padded[:, :-2, 1:-1, :]
    beside = beside + padded[:, 1:-1, 2:, :] + padded[:, 1:-1, :-2, :]
    beside = beside + along_z[:, :, :, 2:] + along_z[:, :, :, :-2]
    return (6.0 + diagonal_rigidity)[None] * bucket_entries - beside


def paired(residual, applied):
    return lax.psum((jnp.sum(residual * residual), jnp.sum(residual * applied)), ("dom", "slab"))


def gradients(padded):
    interior = padded[1:-1, 1:-1, :]
    along_z = jnp.pad(interior, ((0, 0), (0, 0), (1, 1)))
    return COEF * jnp.stack(
        [
            padded[2:, 1:-1, :] - padded[:-2, 1:-1, :],
            padded[1:-1, 2:, :] - padded[1:-1, :-2, :],
            along_z[:, :, 2:] - along_z[:, :, :-2],
        ]
    )


def on_device(
    heat_level,
    emitting_vertex_position,
    corner_holder_shift,
    corner_fetched_bucket,
    corner_factors,
    diagonal_rigidity,
    boundary_vertex_position,
    boundary_bucket_tally,
    boundary_accepting_vertex,
):
    departing_entries = fetch_entries(heat_level, emitting_vertex_position[0])
    slots = departing_entries.shape[2]
    gathered = with_halo(departing_entries, (("dom", 0), ("slab", 1)), 1)
    flat_slots = gathered[::2, ::2, :].reshape(-1)
    interp = jnp.zeros(diagonal_rigidity.shape, jnp.float32)
    for corner in range(4):
        column = corner_holder_shift[corner] * slots + corner_fetched_bucket[corner]
        interp = interp + corner_factors[corner] * fetch_entries(flat_slots, column)
    first_pad = None
    padded = with_halo(interp, (("dom", 0), ("slab", 1)), 1)
    thermal_load = gradients(padded)
    solution = jnp.zeros_like(thermal_load)
    residual = thermal_load
    applied = operate(residual, diagonal_rigidity, first_pad)
    norm_now, product = paired(residual, applied)
    step_size = norm_now / product
    direction = residual
    along = applied
    for iteration in range(ITERS):
        solution = solution + step_size * direction
        residual = residual - step_size * along
        if iteration + 1 < ITERS:
            applied = operate(residual, diagonal_rigidity)
            norm_next, product = paired(residual, applied)
            beta_ratio = norm_next / norm_now
            step_size = norm_next / (product - beta_ratio * norm_next / step_size)
            direction = residual + beta_ratio * direction
            along = applied + beta_ratio * along
            norm_now = norm_next
    flat_solution = solution.reshape(3, -1)
    surface_positions = boundary_vertex_position[0]
    surface_values = jnp.stack(
        [fetch_entries(flat_solution[component], surface_positions) for component in range(3)]
    )
    wslots = surface_values.shape[3]
    live_mask = (
        jnp.arange(wslots, dtype=jnp.int32)[None, None, :]
        < boundary_bucket_tally[0].reshape(3, 3)[:, :, None]
    )
    surface_values = jnp.where(live_mask[None], surface_values, jnp.zeros_like(surface_values))
    returned = with_halo(surface_values, (("dom", 1), ("slab", 2)), 1)
    arrived = returned[:, ::2, ::2, :]
    thermal_disp = spread_entries(
        arrived.reshape(3, -1), boundary_accepting_vertex[0].reshape(-1), heat_level.shape[0]
    )
    return (solution, thermal_disp)


def solution(mesh):
    in_specs = (
        P(("dom", "slab")),
        P(("dom", "slab"), None, None, None),
        P(None, "dom", "slab", None),
        P(None, "dom", "slab", None),
        P(None, "dom", "slab", None),
        P("dom", "slab", None),
        P(("dom", "slab"), None, None, None),
        P(("dom", "slab"), None),
        P(("dom", "slab"), None, None, None),
    )
    out_specs = (P(None, "dom", "slab", None), P(None, ("dom", "slab")))
    return jax.shard_map(
        on_device, mesh=mesh, in_specs=in_specs, out_specs=out_specs, check_vma=False
    )
```

profile of v0, /device:TPU:0, one launch (start us, length us, event | category | flops | bytes accessed | tf_op | source)
XLA Modules:
  0.0 1073.7 jit_solution(15727276044515979557)
XLA Ops:
  0.6 2.5 compare_select_fusion
  3.2 1.3 add_select_fusion
  4.5 244.2 %gather_fusion = f32[73728,128]{1,0:T(8,128)} fusion(f32[128,128]{1,0:T(8,128)S(1)} %bitcast.178, s32[73728]{0:T(1024)S(1)} %broadcast_clamp_fusion), kind=kCustom, calls=%fused_computation | custom fusion | bytes 75792384 | tf_op jit(solution)/shard_map/gather | solution.py:31
  248.7 26.3 %select_reduce_fusion = f32[3,3,8192]{2,1,0:T(4,128)S(1)} fusion(f32[3,3,8192,128]{3,2,1,0:T(8,128)} %bitcast.179, s32[3,3,8192]{2,1,0:T(4,128)S(1)} %add_select_fusion), kind=kLoop, calls=%fused_computation.8 | loop fusion | flops 28237824 | bytes 38338560 | tf_op jit(solution)/shard_map/reduce_sum | solution.py:34
  275.1 2.4 collective-permute-start
  277.5 1.3 collective-permute-start.1
  279.5 3.4 collective-permute-done.1
  283.2 3.4 collective-permute-start.2
  286.6 1.3 collective-permute-start.3
  289.4 4.4 collective-permute-done.3
  294.2 3.4 slice.255
  297.9 108.9 %gather_fusion.2 = f32[32768,128]{1,0:T(8,128)} fusion(f32[576,128]{1,0:T(8,128)S(1)} %reshape_reshape.2, s32[32768]{0:T(1024)S(1)} %broadcast_clamp_fusion.3), kind=kCustom, calls=%fused_computation.2 | custom fusion | bytes 33685504 | tf_op jit(solution)/shard_map/gather | solution.py:31
  406.8 108.9 %gather_fusion.1 = f32[32768,128]{1,0:T(8,128)} fusion(f32[576,128]{1,0:T(8,128)S(1)} %reshape_reshape.2, s32[32768]{0:T(1024)S(1)} %broadcast_clamp_fusion.4), kind=kCustom, calls=%fused_computation.1 | custom fusion | bytes 33685504 | tf_op jit(solution)/shard_map/gather | solution.py:31
  515.6 109.0 %gather_fusion.3 = f32[32768,128]{1,0:T(8,128)} fusion(f32[576,128]{1,0:T(8,128)S(1)} %reshape_reshape.2, s32[32768]{0:T(1024)S(1)} %broadcast_clamp_fusion.2), kind=kCustom, calls=%fused_computation.3 | custom fusion | bytes 33685504 | tf_op jit(solution)/shard_map/gather | solution.py:31
  624.7 109.0 %gather_fusion.4 = f32[32768,128]{1,0:T(8,128)} fusion(f32[576,128]{1,0:T(8,128)S(1)} %reshape_reshape.2, s32[32768]{0:T(1024)S(1)} %broadcast_clamp_fusion.1), kind=kCustom, calls=%fused_computation.4 | custom fusion | bytes 33685504 | tf_op jit(solution)/shard_map/gather | solution.py:31
  733.7 22.5 %select_reduce_fusion.3 = (f32[8,8,512]{2,1,0:T(8,128)S(1)}, f32[8,8,512]{2,1,0:T(8,128)S(1)}) fusion(f32[8,8,512,128]{3,2,1,0:T(8,128)} %bitcast.182, s32[8,8,512]{2,1,0:T(8,128)S(1)} %copy-done.10, f32[8,8,512,128]{3,2,1,0:T(8,128)} %bitcast.183, s32[8,8,512]{2,1,0:T(8,128)S(1)} %copy-done.9), kind=kLoop, calls=%fused_computation.14 | loop fusion | flops 25100288 | bytes 34078720 | tf_op jit(solution)/shard_map/reduce_sum | solution.py:34
  756.3 20.8 %select_reduce_fusion.1 = (f32[8,8,512]{2,1,0:T(8,128)S(1)}, f32[8,8,512]{2,1,0:T(8,128)S(1)}) fusion(f32[8,8,512,128]{3,2,1,0:T(8,128)S(1)} %bitcast.181, s32[8,8,512]{2,1,0:T(8,128)S(1)} %copy-done.7, f32[8,8,512,128]{3,2,1,0:T(8,128)S(1)} %bitcast.180, s32[8,8,512]{2,1,0:T(8,128)S(1)} %copy-done.8), kind=kLoop, calls=%fused_computation.10 | loop fusion | flops 25100288 | bytes 34078720 | tf_op jit(solution)/shard_map/reduce_sum | solution.py:34
  777.2 1.3 collective-permute-start.4
  778.5 4.6 collective-permute-start.5
  784.0 1.3 collective-permute-start.6
  785.3 5.0 collective-permute-start.7
  790.3 1.5 collective-permute-done.7
  792.0 1.3 collective-permute-start.8
  793.3 3.4 collective-permute-start.9
  799.0 5.2 collective-permute-start.11
  804.4 1.6 collective-permute-done.11
  807.0 48.2 %all-reduce.8 = (f32[]{:T(128)}, f32[]{:T(128)}) all-reduce(f32[]{:T(128)} %get-tuple-element.9, f32[]{:T(128)} %get-tuple-element.8), channel_id=1, replica_groups=mesh['dom'=4,'slab'=8] {'dom','slab'}, use_global_device_ids=true, to_apply=%region_6.7 | all-reduce | flops 2 | bytes 16 | tf_op jit(solution)/shard_map/psum | solution.py:62
  856.6 1.3 collective-permute-start.12
  857.9 3.0 collective-permute-start.13
  863.2 4.8 collective-permute-start.15
  868.3 1.7 collective-permute-done.15
  871.0 44.0 %all-reduce.7 = (f32[]{:T(128)}, f32[]{:T(128)}) all-reduce(f32[]{:T(128)} %get-tuple-element.7, f32[]{:T(128)} %get-tuple-element.6), channel_id=1, replica_groups=mesh['dom'=4,'slab'=8] {'dom','slab'}, use_global_device_ids=true, to_apply=%region_10.11 | all-reduce | flops 2 | bytes 16 | tf_op jit(solution)/shard_map/psum | solution.py:62
  919.9 1.3 collective-permute-start.16
  921.2 3.0 collective-permute-start.17
  926.9 4.8 collective-permute-start.19
  932.0 2.1 collective-permute-done.19
  935.1 44.1 %all-reduce.6 = (f32[]{:T(128)}, f32[]{:T(128)}) all-reduce(f32[]{:T(128)} %get-tuple-element.5, f32[]{:T(128)} %get-tuple-element.4), channel_id=1, replica_groups=mesh['dom'=4,'slab'=8] {'dom','slab'}, use_global_device_ids=true, to_apply=%region_14.15 | all-reduce | flops 2 | bytes 16 | tf_op jit(solution)/shard_map/psum | solution.py:62
  984.7 3.0 collective-permute-start.21
  988.7 1.3 collective-permute-start.22
  990.0 4.8 collective-permute-start.23
  995.1 2.2 collective-permute-done.23
  998.4 44.3 %all-reduce.5 = (f32[]{:T(128)}, f32[]{:T(128)}) all-reduce(f32[]{:T(128)} %get-tuple-element.3, f32[]{:T(128)} %get-tuple-element.2), channel_id=1, replica_groups=mesh['dom'=4,'slab'=8] {'dom','slab'}, use_global_device_ids=true, to_apply=%region_18.19 | all-reduce | flops 2 | bytes 16 | tf_op jit(solution)/shard_map/psum | solution.py:62
  1046.7 2.4 gather_fusion.5
  1049.2 2.4 gather_fusion.6
  1051.6 2.4 gather_fusion.7
  1057.5 4.4 collective-permute-done.25
  1061.9 3.8 collective-permute-start.26
  1067.1 4.2 collective-permute-done.27
  (121 shorter events, 26.4 us)
Async XLA Ops:
  0.6 3.9 copy-start
  248.7 30.1 %copy-start.4 = (s32[4,8,8,512]{3,2,1,0:T(8,128)S(1)}, s32[4,8,8,512]{3,2,1,0:T(8,128)}, u32[]{:S(2)}) copy-start(s32[4,8,8,512]{3,2,1,0:T(8,128)} %param.12) | copy-start | bytes 1572868
  248.7 30.1 %copy-start.5 = (s32[4,8,8,512]{3,2,1,0:T(8,128)S(1)}, s32[4,8,8,512]{3,2,1,0:T(8,128)}, u32[]{:S(2)}) copy-start(s32[4,8,8,512]{3,2,1,0:T(8,128)} %param.11) | copy-start | bytes 1572868
  275.1 4.4 collective-permute-start
  277.5 5.4 collective-permute-start.1
  283.2 6.2 collective-permute-start.2
  286.6 7.2 collective-permute-start.3
  624.7 109.0 %copy-start.9 = (s32[8,8,512]{2,1,0:T(8,128)S(1)}, s32[8,8,512]{2,1,0:T(8,128)}, u32[]{:S(2)}) copy-start(s32[8,8,512]{2,1,0:T(8,128)} %get-tuple-element.24) | copy-start | bytes 393220
  624.7 109.0 %copy-start.10 = (s32[8,8,512]{2,1,0:T(8,128)S(1)}, s32[8,8,512]{2,1,0:T(8,128)}, u32[]{:S(2)}) copy-start(s32[8,8,512]{2,1,0:T(8,128)} %get-tuple-element.25) | copy-start | bytes 393220
  733.7 22.5 %copy-start.2 = (f32[32768,128]{1,0:T(8,128)S(1)}, f32[32768,128]{1,0:T(8,128)}, u32[]{:S(2)}) copy-start(f32[32768,128]{1,0:T(8,128)} %gather_fusion.3) | copy-start | bytes 50331652
  733.7 22.6 %copy-start.3 = (f32[32768,128]{1,0:T(8,128)S(1)}, f32[32768,128]{1,0:T(8,128)}, u32[]{:S(2)}) copy-start(f32[32768,128]{1,0:T(8,128)} %gather_fusion.4) | copy-start | bytes 50331652
  733.7 22.6 %copy-start.7 = (s32[8,8,512]{2,1,0:T(8,128)S(1)}, s32[8,8,512]{2,1,0:T(8,128)}, u32[]{:S(2)}) copy-start(s32[8,8,512]{2,1,0:T(8,128)} %get-tuple-element.26) | copy-start | bytes 393220
  733.7 22.6 %copy-start.8 = (s32[8,8,512]{2,1,0:T(8,128)S(1)}, s32[8,8,512]{2,1,0:T(8,128)}, u32[]{:S(2)}) copy-start(s32[8,8,512]{2,1,0:T(8,128)} %get-tuple-element.27) | copy-start | bytes 393220
  756.3 20.8 %copy-start.11 = (f32[4,8,8,512]{3,2,1,0:T(8,128)S(1)}, f32[4,8,8,512]{3,2,1,0:T(8,128)}, u32[]{:S(2)}) copy-start(f32[4,8,8,512]{3,2,1,0:T(8,128)} %param.13) | copy-start | bytes 1572868
  756.3 47.8 %copy-start.12 = (f32[8,8,512]{2,1,0:T(8,128)S(1)}, f32[8,8,512]{2,1,0:T(8,128)}, u32[]{:S(2)}) copy-start(f32[8,8,512]{2,1,0:T(8,128)} %param.14) | copy-start | bytes 393220
  756.3 168.0 %copy-start.13 = (s32[1,3,3,128]{3,0,2,1:T(1,128)S(1)}, s32[1,3,3,128]{3,0,2,1:T(1,128)}, u32[]{:S(2)}) copy-start(s32[1,3,3,128]{3,0,2,1:T(1,128)} %param.15) | copy-start | bytes 13828
  756.3 168.5 %copy-start.15 = (s32[1,9]{1,0:T(1,128)S(1)}, s32[1,9]{1,0:T(1,128)}, u32[]{:S(2)}) copy-start(s32[1,9]{1,0:T(1,128)} %param.16) | copy-start | bytes 112
  756.3 231.5 %copy-start.14 = (s32[1,3,3,128]{3,0,2,1:T(1,128)S(1)}, s32[1,3,3,128]{3,0,2,1:T(1,128)}, u32[]{:S(2)}) copy-start(s32[1,3,3,128]{3,0,2,1:T(1,128)} %param.17) | copy-start | bytes 13828
  777.2 6.0 collective-permute-start.4
  778.5 5.5 collective-permute-start.5
  784.0 6.3 collective-permute-start.6
  785.3 6.4 collective-permute-start.7
  792.0 4.8 collective-permute-start.8
  793.3 4.3 collective-permute-start.9
  797.7 6.7 collective-permute-start.10
  799.0 7.0 collective-permute-start.11
  856.5 217.2 %copy-start.1 = (f32[16384]{0:T(1024)S(1)}, f32[16384]{0:T(1024)}, u32[]{:S(2)}) copy-start(f32[16384]{0:T(1024)} %param.9) | copy-start | bytes 196612
  856.6 4.3 collective-permute-start.12
  857.9 3.9 collective-permute-start.13
  861.9 6.4 collective-permute-start.14
  863.2 6.8 collective-permute-start.15
  919.9 5.6 collective-permute-start.16
  921.2 4.3 collective-permute-start.17
  925.6 6.4 collective-permute-start.18
  926.9 7.2 collective-permute-start.19
  983.4 4.5 collective-permute-start.20
  984.7 3.9 collective-permute-start.21
  988.7 6.4 collective-permute-start.22
  990.0 7.3 collective-permute-start.23
  1046.6 27.1 %copy-start.6 = (f32[3,8,8,512]{3,2,1,0:T(8,128)}, f32[3,8,8,512]{3,2,1,0:T(8,128)S(1)}, u32[]{:S(2)}) copy-start(f32[3,8,8,512]{3,2,1,0:T(8,128)S(1)} %multiply_add_fusion) | copy-start | bytes 1179652
  1054.9 2.6 collective-permute-start.24
  1056.2 5.8 collective-permute-start.25
  1061.9 5.2 collective-permute-start.26
  1065.8 5.5 collective-permute-start.27
where the time goes:
time: 1080 us; the launch traced here: 1070 us
  local copies, waits for them, and re-layouts  693 us (64%)
  blocking collectives  181 us (17%)
  other arithmetic  82.4 us (8%)
  starting transfers between devices  70.8 us (7%)
  waiting for transfers between devices  30.2 us (3%)
  between operations  15.3 us (1%)
    gather x8, local copies, waits for them, and re-layouts, fetch_entries(): picked = table_rows[positions // lane_count]  687 us
    psum x4, blocking collectives, paired(): lax.psum((jnp.sum(residual * residual), jnp.sum(residual * applied)), ('d...  181 us
    reduce_sum x4, other arithmetic, fetch_entries(): return jnp.sum(jnp.where(chosen, picked, jnp.zeros_like(picked)), axis=-1)  70.3 us
    ppermute x14, starting transfers between devices, with_halo(): before = lax.ppermute(last, axis, up)  52.7 us
  transfers between devices with their start and end apart: 28, of which 18 were waited for; matrix products, arithmetic and copies ran while one was open for 0% of the time, Pallas kernels for 0%

commit v1 on v0

v1 whole, which is shorter than its diff:
```python
import functools
import math

import jax
import jax.numpy as jnp
from jax import lax
from jax.experimental import pallas as pl
from jax.experimental.pallas import tpu as pltpu
from jax.sharding import PartitionSpec as P

ITERS = 4
COEF = 0.5
LANES = 128
SUB = 8
CENTRE = 7.125
HALF = 6.875
REACH = ITERS + 1
VMEM = pl.BlockSpec(memory_space=pltpu.VMEM)
SMEM = pl.BlockSpec(memory_space=pltpu.SMEM)


def params(mib):
    return pltpu.CompilerParams(vmem_limit_bytes=mib * 1024 * 1024)


def lookup(table, first, rows, lanes, bits):
    if rows == 1:
        row = jnp.broadcast_to(table[pl.ds(first, 1), :], lanes.shape)
        return jnp.take_along_axis(row, lanes, axis=1, mode="promise_in_bounds")
    half = rows // 2
    lower = lookup(table, first, half, lanes, bits[:-1])
    upper = lookup(table, first + half, half, lanes, bits[:-1])
    return jnp.where(bits[-1], upper, lower)


def lookup_all(table, indices, chunk):
    rows = table.shape[0]
    depth = int(math.log2(chunk))
    lanes = [index & (LANES - 1) for index in indices]
    high = [index >> 7 for index in indices]
    outer = [value >> depth for value in high]

    def step(block, found):
        base = pl.multiple_of(block * chunk, chunk)
        fresh = []
        for lane, value, top, old in zip(lanes, high, outer, found):
            bits = [((value >> bit) & 1) == 1 for bit in range(depth)]
            fresh.append(jnp.where(top == block, lookup(table, base, chunk, lane, bits), old))
        return tuple(fresh)

    zero = jnp.zeros(indices[0].shape, jnp.float32)
    return lax.fori_loop(0, rows // chunk, step, tuple(zero for _ in indices))


def depart_kernel(heat, picks, out, index):
    ways = picks.shape[1]
    slots = picks.shape[3]
    per = slots // LANES
    for a in range(ways):
        for b in range(ways):
            for row in range(0, per, SUB):
                piece = picks[0, a, b, pl.ds(row * LANES, SUB * LANES)]
                index[pl.ds((a * ways + b) * per + row, SUB), :] = piece.reshape(SUB, LANES)
    group = SUB * SUB

    def body(g, carry):
        base = pl.multiple_of(g * group, group)
        found = lookup_all(heat, [index[pl.ds(base + SUB * k, SUB), :] for k in range(SUB)], 64)
        for k in range(SUB):
            out[pl.ds(base + SUB * k, SUB), :] = found[k]
        return carry

    lax.fori_loop(0, ways * ways * per // group, body, 0)


def interp_kernel(low, near_low, near, near_high, high, shift, bucket, factor, out, table):
    corners, nx, _, nz = shift.shape
    per = near.shape[1]
    slots = per * LANES
    for b, ref in ((0, low), (2, high)):
        for a in range(3):
            table[pl.ds((3 * a + b) * per, per), :] = ref[a]
    for a, ref in enumerate((near_low, near, near_high)):
        table[pl.ds((3 * a + 1) * per, per), :] = ref[1]

    def body(x, carry):
        for z in range(0, nz, 2 * LANES):
            where = []
            for c in range(corners):
                for part in range(2):
                    at = pl.ds(z + part * LANES, LANES)
                    where.append(shift[c, x, :, at] * slots + bucket[c, x, :, at])
            found = lookup_all(table, where, 64)
            for part in range(2):
                at = pl.ds(z + part * LANES, LANES)
                total = factor[0, x, :, at] * found[part]
                for c in range(1, corners):
                    total = total + factor[c, x, :, at] * found[2 * c + part]
                out[x, :, at] = total
        return carry

    lax.fori_loop(0, nx, body, 0)


def pack_kernel(width, low, own, high, up, down):
    ny, nz = own.shape[1:]
    extent = low.shape[0] + own.shape[0] + high.shape[0]
    for t in range(nz // LANES):
        at = pl.ds(t * LANES, LANES)
        for x in range(extent):
            ref, k = low, x
            if k >= low.shape[0]:
                ref, k = own, k - low.shape[0]
                if k >= own.shape[0]:
                    ref, k = high, k - own.shape[0]
            to = pl.ds((t * extent + x) * width, width)
            up[to, :] = ref[k, pl.ds(ny - width, width), at]
            down[to, :] = ref[k, pl.ds(0, width), at]


def unpack(target, margin, width, own, dom_low, dom_high, slab_low, slab_high, change):
    nx, ny, nz = own.shape
    tiles = nz // LANES
    extent = nx + 2 * width
    start = REACH - width
    for t in range(tiles):
        at = pl.ds(t * LANES, LANES)
        for x in range(extent):
            if x < width:
                ref, k = dom_low, x
            elif x < width + nx:
                ref, k = own, x - width
            else:
                ref, k = dom_high, x - width - nx
            rows = pl.ds((t * extent + x) * width, width)
            target[t, start + x, pl.ds(SUB, ny), :] = change(ref[k, :, at], start + x, 1)
            target[t, start + x, pl.ds(SUB - width, width), :] = change(slab_low[rows, :], start + x, 0)
            target[t, start + x, pl.ds(SUB + ny, width), :] = change(slab_high[rows, :], start + x, 2)


def krylov_kernel(inside, own, p_low, p_high, p_left, p_right, rigid, d_low, d_high, d_left, d_right,
                  basis, sums, temp, diag, u0, u1, u2, u3):
    nx, ny, nz = own.shape
    tiles = nz // LANES
    parts = temp.shape[2] // SUB
    held = (u0, u1, u2, u3)
    flag = [inside[k].astype(jnp.float32) for k in range(4)]

    def mask(x, part):
        at_x = jnp.where(x < REACH, flag[0], jnp.where(x >= REACH + nx, flag[1], 1.0))
        return at_x * (flag[2] if part == 0 else flag[3] if part == 2 else 1.0)

    temp[...] = jnp.zeros_like(temp)
    unpack(temp, REACH, REACH, own, p_low, p_high, p_left, p_right, lambda v, x, part: v)
    diag[...] = jnp.zeros_like(diag)
    unpack(diag, REACH, REACH - 2, rigid, d_low, d_high, d_left, d_right,
           lambda v, x, part: (v * (2.0 / HALF) + 2.0 * (6.0 - CENTRE) / HALF) * mask(x, part))
    lane = lax.broadcasted_iota(jnp.int32, (SUB, LANES), 1)
    first, last = lane == 0, lane == LANES - 1
    zero = jnp.zeros((SUB, LANES), jnp.float32)

    def around_z(values):
        back = [pltpu.roll(v, 1, axis=1) for v in values]
        ahead = [pltpu.roll(v, LANES - 1, axis=1) for v in values]
        pairs = []
        for t in range(tiles):
            before = jnp.where(first, back[t - 1] if t else zero, back[t])
            after = jnp.where(last, ahead[t + 1] if t + 1 < tiles else zero, ahead[t])
            pairs.append((before, after))
        return pairs

    def around_y(ref, head, x, part):
        base = part * SUB
        mine = ref[(*head, x, pl.ds(base, SUB))]
        below = pltpu.roll(mine, 1, axis=0) if part == 0 else ref[(*head, x, pl.ds(base - 1, SUB))]
        above = pltpu.roll(mine, SUB - 1, axis=0) if part == parts - 1 else ref[(*head, x, pl.ds(base + 1, SUB))]
        return mine, below, above

    def load_row(x, carry):
        for part in range(parts):
            scale = COEF * mask(x, part)
            rows = [around_y(temp, (t,), x, part) for t in range(tiles)]
            along = around_z([r[0] for r in rows])
            for t in range(tiles):
                ahead = temp[t, x + 1, pl.ds(part * SUB, SUB), :]
                back = temp[t, x - 1, pl.ds(part * SUB, SUB), :]
                u0[0, t, x, pl.ds(part * SUB, SUB), :] = scale * (ahead - back)
                u0[1, t, x, pl.ds(part * SUB, SUB), :] = scale * (rows[t][2] - rows[t][1])
                u0[2, t, x, pl.ds(part * SUB, SUB), :] = scale * (along[t][1] - along[t][0])
        return carry

    lax.fori_loop(1, nx + 2 * REACH - 1, load_row, 0)

    def twice(ref, c, x, part):
        coefficient = (2.0 / HALF) * mask(x, part)
        rows = [around_y(ref, (c, t), x, part) for t in range(tiles)]
        along = around_z([r[0] for r in rows])
        results = []
        for t in range(tiles):
            near = rows[t][1] + rows[t][2] + along[t][0] + along[t][1]
            near = near + ref[c, t, x + 1, pl.ds(part * SUB, SUB), :] + ref[c, t, x - 1, pl.ds(part * SUB, SUB), :]
            results.append(diag[t, x, pl.ds(part * SUB, SUB), :] * rows[t][0] - coefficient * near)
        return results, [r[0] for r in rows]

    for order in range(1, ITERS):
        source, target = held[order - 1], held[order]

        def apply_row(x, carry):
            for c in range(3):
                for part in range(parts):
                    doubled, _ = twice(source, c, x, part)
                    for t in range(tiles):
                        at = (c, t, x, pl.ds(part * SUB, SUB))
                        if order == 1:
                            target[at] = 0.5 * doubled[t]
                        else:
                            target[at] = doubled[t] - held[order - 2][at]
            return carry

        margin = ITERS - order
        lax.fori_loop(REACH - margin, REACH + nx + margin, apply_row, 0)

    def dots_row(x, carry):
        carry = list(carry)
        for c in range(3):
            doubled, u = twice(u3, c, REACH + x, 1)
            for t in range(tiles):
                at = (c, t, REACH + x, pl.ds(SUB, SUB))
                v = [u0[at], u1[at], u2[at], u[t]]
                pairs = [(v[0], v[0]), (v[0], v[1]), (v[1], v[1]), (v[1], v[2]), (v[2], v[2]), (v[2], v[3]),
                         (v[3], v[3]), (v[3], doubled[t])]
                for k, (left, right) in enumerate(pairs):
                    carry[k] = carry[k] + left * right
                for j in range(4):
                    basis[3 * j + c, pl.ds(pl.multiple_of(t * nx * SUB + x * SUB, SUB), SUB), :] = v[j]
        return tuple(carry)

    totals = lax.fori_loop(0, nx, dots_row, tuple(zero for _ in range(8)))
    for k in range(8):
        sums[pl.ds(k, 1), :] = jnp.sum(totals[k], axis=0, keepdims=True)


def surface_kernel(nz, tally, basis, picks, out, index, live):
    fields, rows, _ = basis.shape
    ways = picks.shape[1]
    count = ways * ways
    block = rows // (nz // LANES)
    lane = lax.broadcasted_iota(jnp.int32, (1, LANES), 1)
    index[...] = jnp.zeros_like(index)
    live[...] = jnp.zeros_like(live)
    for a in range(ways):
        for b in range(ways):
            spot = picks[0, a, pl.ds(b, 1), :]
            along = spot % nz
            high = (along // LANES) * block + spot // nz
            index[pl.ds(a * ways + b, 1), :] = high * LANES + spot % LANES
            live[pl.ds(a * ways + b, 1), :] = (lane < tally[0, a * ways + b]).astype(jnp.float32)

    def body(f, carry):
        found = lookup_all(basis.at[f], [index[pl.ds(0, SUB), :], index[pl.ds(SUB, SUB), :]], 64)
        for k in range(count):
            value = found[k // SUB][k % SUB : k % SUB + 1, :]
            value = jnp.where(live[pl.ds(k, 1), :] > 0.5, value, 0.0)
            out[k // ways, k % ways, pl.ds(f, 1), :] = value
        return carry

    lax.fori_loop(0, fields, body, 0)


def coefficients(nu):
    half = 0.5

    def gram(i, j):
        return half * (nu[i + j] + nu[abs(i - j)])

    def inner(i, j):
        if j == 0:
            return gram(i, 1)
        return half * (gram(i, j + 1) + gram(i, j - 1))

    def form(vector, matrix):
        n = len(vector)
        total = None
        for i in range(n):
            for j in range(i, n):
                term = vector[i] * vector[j] * matrix(i, j)
                term = term if i == j else 2.0 * term
                total = term if total is None else total + term
        return total

    one = jnp.ones_like(nu[0])
    found, residual, direction = [], [one], [one]
    rr = nu[0]
    for iteration in range(ITERS):
        energy = form(direction, lambda i, j: CENTRE * gram(i, j) + HALF * inner(i, j))
        alpha = rr / energy
        found = [
            (found[i] if i < len(found) else 0.0) + alpha * direction[i] for i in range(len(direction))
        ]
        if iteration + 1 == ITERS:
            break
        image = [CENTRE * d for d in direction] + [jnp.zeros_like(one)]
        for j, d in enumerate(direction):
            if j == 0:
                image[1] = image[1] + HALF * d
            else:
                image[j + 1] = image[j + 1] + half * HALF * d
                image[j - 1] = image[j - 1] + half * HALF * d
        residual = residual + [jnp.zeros_like(one)]
        residual = [r - alpha * w for r, w in zip(residual, image)]
        fresh = form(residual, gram)
        ratio = fresh / rr
        direction = direction + [jnp.zeros_like(one)]
        direction = [r + ratio * d for r, d in zip(residual, direction)]
        rr = fresh
    return found


def finish_kernel(sums, basis, surface, picks, disp, thermal, shift):
    raw = [jnp.broadcast_to(jnp.sum(sums[pl.ds(k, 1), :], axis=1, keepdims=True), (1, LANES)) for k in range(8)]
    nu = [raw[0], raw[1]]
    for k in range(2, 7):
        nu.append(2.0 * raw[k] - raw[k % 2])
    nu.append(2.0 * raw[7] - nu[5] - 2.0 * raw[1])
    weights = coefficients(nu)
    wide = [jnp.broadcast_to(w, (SUB, LANES)) for w in weights]
    _, nx, ny, nz = disp.shape
    tiles = nz // LANES

    def row(x, carry):
        for c in range(3):
            for t in range(tiles):
                at = pl.ds(pl.multiple_of(t * nx * SUB + x * SUB, SUB), SUB)
                total = wide[0] * basis[c, at, :]
                for j in range(1, 4):
                    total = total + wide[j] * basis[3 * j + c, at, :]
                disp[c, x, :, pl.ds(t * LANES, LANES)] = total
        return carry

    lax.fori_loop(0, nx, row, 0)
    ways = picks.shape[1]
    depth = thermal.shape[1] // LANES
    place = lax.broadcasted_iota(jnp.int32, (LANES, LANES), 0)
    tall = lax.broadcasted_iota(jnp.int32, (depth, LANES), 0)
    total = jnp.zeros((9 * depth, LANES), jnp.float32)
    for a in range(ways):
        for b in range(ways):
            spot = picks[0, a, pl.ds(b, 1), :]
            lane_hot = (place == spot % LANES).astype(jnp.float32).astype(jnp.bfloat16)
            row_hot = tall == spot // LANES
            pieces = []
            for c in range(3):
                value = weights[0] * surface[a, b, pl.ds(c, 1), :]
                for j in range(1, 4):
                    value = value + weights[j] * surface[a, b, pl.ds(3 * j + c, 1), :]
                for _ in range(3):
                    part = value.astype(jnp.bfloat16).astype(jnp.float32)
                    value = value - part
                    pieces.append(jnp.where(row_hot, jnp.broadcast_to(part, row_hot.shape), 0.0))
            left = jnp.concatenate(pieces, axis=0).astype(jnp.bfloat16)
            total = total + lax.dot_general(left, lane_hot, (((1,), (1,)), ((), ())),
                                            preferred_element_type=jnp.float32)
    for c in range(3):
        whole = total[3 * c * depth : (3 * c + 1) * depth]
        whole = whole + total[(3 * c + 1) * depth : (3 * c + 2) * depth]
        shift[...] = whole + total[(3 * c + 2) * depth : (3 * c + 3) * depth]
        for r in range(depth):
            thermal[pl.ds(c, 1), pl.ds(r * LANES, LANES)] = shift[pl.ds(r, 1), :]


def swap(last, leading, axis):
    peers = lax.axis_size(axis)
    up = [(i, i + 1) for i in range(peers - 1)]
    down = [(j, i) for i, j in up]
    return lax.ppermute(last, axis, up), lax.ppermute(leading, axis, down)


def total_over(value, axis):
    peers = lax.axis_size(axis)
    hop = 1
    while hop < peers:
        value = value + lax.ppermute(value, axis, [(i, i ^ hop) for i in range(peers)])
        hop *= 2
    return value


def on_device(heat_level, emitting, holder, bucket, factors, rigidity, boundary, tally, accepting):
    f32 = jnp.float32
    ways = emitting.shape[1]
    slots = emitting.shape[3]
    per = slots // LANES
    nx, ny, nz = rigidity.shape
    tiles = nz // LANES
    call = pl.pallas_call
    heat = heat_level.reshape(-1, LANES)
    departing = call(
        depart_kernel,
        out_shape=jax.ShapeDtypeStruct((ways * ways * per, LANES), f32),
        in_specs=[VMEM] * 2,
        out_specs=VMEM,
        scratch_shapes=[pltpu.VMEM((ways * ways * per, LANES), jnp.int32)],
        name="depart",
    )(heat, emitting).reshape(ways, ways, per, LANES)
    from_low, from_high = swap(departing[2], departing[0], "dom")
    near = departing[1]
    up = jnp.stack([from_low[2], near[2], from_high[2]])
    down = jnp.stack([from_low[0], near[0], from_high[0]])
    left, right = swap(up, down, "slab")

    narrow = REACH - 2

    def packed(width, low, own, high):
        shape = jax.ShapeDtypeStruct((tiles * (nx + 2 * width) * width, LANES), f32)
        return call(functools.partial(pack_kernel, width), out_shape=(shape, shape), in_specs=[VMEM] * 3,
                    out_specs=(VMEM, VMEM), name=f"pack{width}")(low, own, high)

    d_low, d_high = swap(rigidity[nx - narrow :], rigidity[:narrow], "dom")
    d_up, d_down = packed(narrow, d_low, rigidity, d_high)
    d_left, d_right = swap(d_up, d_down, "slab")

    interp = call(
        interp_kernel,
        out_shape=jax.ShapeDtypeStruct((nx, ny, nz), f32),
        in_specs=[VMEM] * 8,
        out_specs=VMEM,
        scratch_shapes=[pltpu.VMEM((ways * ways * per, LANES), f32)],
        compiler_params=params(32),
        name="interp",
    )(left, from_low, near, from_high, right, holder, bucket, factors)

    p_low, p_high = swap(interp[nx - REACH :], interp[:REACH], "dom")
    p_up, p_down = packed(REACH, p_low, interp, p_high)
    p_left, p_right = swap(p_up, p_down, "slab")
    dom, slab = lax.axis_index("dom"), lax.axis_index("slab")
    inside = jnp.stack([dom > 0, dom < lax.axis_size("dom") - 1, slab > 0, slab < lax.axis_size("slab") - 1])
    extent = nx + 2 * REACH
    field = pltpu.VMEM((3, tiles, extent, 3 * SUB, LANES), f32)
    basis, sums = call(
        krylov_kernel,
        out_shape=(jax.ShapeDtypeStruct((3 * ITERS, tiles * nx * ny, LANES), f32), jax.ShapeDtypeStruct((SUB, LANES), f32)),
        in_specs=[SMEM] + [VMEM] * 10,
        out_specs=(VMEM, VMEM),
        scratch_shapes=[pltpu.VMEM((tiles, extent, 3 * SUB, LANES), f32)] * 2 + [field] * 4,
        compiler_params=params(48),
        name="krylov",
    )(inside.astype(jnp.int32), interp, p_low, p_high, p_left, p_right, rigidity, d_low, d_high, d_left, d_right)
    sums = total_over(total_over(sums, "dom"), "slab")
    surface = call(
        functools.partial(surface_kernel, nz),
        out_shape=jax.ShapeDtypeStruct((ways, ways, 3 * ITERS, LANES), f32),
        in_specs=[SMEM, VMEM, VMEM],
        out_specs=VMEM,
        scratch_shapes=[pltpu.VMEM((2 * SUB, LANES), jnp.int32), pltpu.VMEM((2 * SUB, LANES), f32)],
        compiler_params=params(16),
        name="surface",
    )(tally, basis, boundary)
    s_low, s_high = swap(surface[2], surface[0], "dom")
    stacked = jnp.stack([s_low, surface[1], s_high])
    s_left, s_right = swap(stacked[:, 2], stacked[:, 0], "slab")
    arrived = jnp.stack([s_left, stacked[:, 1], s_right], axis=1)
    return call(
        finish_kernel,
        out_shape=(jax.ShapeDtypeStruct((3, nx, ny, nz), f32), jax.ShapeDtypeStruct((3, heat_level.shape[0]), f32)),
        in_specs=[VMEM] * 4,
        out_specs=(VMEM, VMEM),
        scratch_shapes=[pltpu.VMEM((heat_level.shape[0] // LANES, LANES), f32)],
        compiler_params=params(32),
        name="finish",
    )(sums, basis, arrived, accepting)


def solution(mesh):
    both = ("dom", "slab")
    in_specs = (
        P(both),
        P(both, None, None, None),
        P(None, "dom", "slab", None),
        P(None, "dom", "slab", None),
        P(None, "dom", "slab", None),
        P("dom", "slab", None),
        P(both, None, None, None),
        P(both, None),
        P(both, None, None, None),
    )
    out_specs = (P(None, "dom", "slab", None), P(None, both))
    return jax.shard_map(on_device, mesh=mesh, in_specs=in_specs, out_specs=out_specs, check_vma=False)
```

time: 1080 us -> 222 us (0.21)
  local copies, waits for them, and re-layouts: 693 us -> 9.44 us
  blocking collectives: 181 us -> 0 us
  Pallas kernels: 0 us -> 131 us
  other arithmetic: 82.4 us -> 0.13 us
  starting transfers between devices: 70.8 us -> 54.8 us
  between operations: 15.3 us -> 1.05 us
    gather x8 -> x0, local copies, waits for them, and re-layouts: 687 us -> none  [fetch_entries(): picked = table_rows[positions // lane_count]]
    psum x4 -> x0, blocking collectives: 181 us -> none  [paired(): lax.psum((jnp.sum(residual * residual), jnp.sum(residual * applied)), ('d...]
    pallas_call x0 -> x7, Pallas kernels: none -> 131 us  [the longest x1 92.8 us: on_device(): call(interp_kernel, out_shape=jax.ShapeDtypeStruct((nx, ny, nz), f32), in...]
    reduce_sum x8 -> x0, other arithmetic: 74.3 us -> none  [the longest x4 70.3 us: fetch_entries(): return jnp.sum(jnp.where(chosen, picked, jnp.zeros_like(picked)), axis=-1)]
    ppermute x28 -> x21, starting transfers between devices: 70.8 us -> 54.8 us  [the longest x16 43.7 us: swap(): return (lax.ppermute(last, axis, up), lax.ppermute(leading, axis, down))]
    ppermute x28 -> x21, waiting for transfers between devices: 30.2 us -> 24.1 us  [the longest x16 17 us: swap(): return (lax.ppermute(last, axis, up), lax.ppermute(leading, axis, down))]
  transfers between devices with their start and end apart: 28 -> 21, of which waited for: 18 -> 12; matrix products, arithmetic and copies ran while one was open for 0% -> 0% of each run, Pallas kernels for 0% -> 1%
where the time goes in v1:
time: 222 us; the launch traced here: 221 us
  Pallas kernels  131 us (59%)
  starting transfers between devices  54.8 us (25%)
  waiting for transfers between devices  24.1 us (11%)
  local copies, waits for them, and re-layouts  9.44 us (4%)
    pallas_call x1, Pallas kernels, on_device(): call(interp_kernel, out_shape=jax.ShapeDtypeStruct((nx, ny, nz), f32), in...  92.8 us
    ppermute x16, starting transfers between devices, swap(): return (lax.ppermute(last, axis, up), lax.ppermute(leading, axis, down))  43.7 us
    ppermute x16, waiting for transfers between devices, swap(): return (lax.ppermute(last, axis, up), lax.ppermute(leading, axis, down))  17 us
    pallas_call x1, Pallas kernels, on_device(): call(depart_kernel, out_shape=jax.ShapeDtypeStruct((ways * ways * per, LA...  13.4 us
    ppermute x5, starting transfers between devices, total_over(): lax.ppermute(value, axis, [(i, i ^ hop) for i in range(peers)])  11.2 us
    pallas_call x1, Pallas kernels, on_device(): call(functools.partial(surface_kernel, nz), out_shape=jax.ShapeDtypeStruc...  10.8 us
    pallas_call x1, Pallas kernels, on_device(): call(krylov_kernel, out_shape=(jax.ShapeDtypeStruct((3 * ITERS, tiles * n...  9.07 us
    unnamed x39, local copies, waits for them, and re-layouts  7.6 us
  transfers between devices with their start and end apart: 21, of which 12 were waited for; matrix products, arithmetic and copies ran while one was open for 0% of the time, Pallas kernels for 1%

profile of v1, /device:TPU:0, one launch (start us, length us, event | category | flops | bytes accessed | tf_op | source)
XLA Modules:
  0.0 221.0 jit_solution(2654825866859614718)
XLA Ops:
  0.7 2.0 copy.11.picks
  2.7 13.4 %depart.1 = f32[576,128]{1,0:T(8,128)} custom-call(f32[128,128]{1,0:T(8,128)} %bitcast.33, s32[1,3,3,8192]{3,2,1,0:T(4,128)} %copy.11.picks), custom_call_target="tpu_custom_call" | custom-call | tf_op jit(solution)/shard_map/depart/pallas_call | solution.py:396
  16.1 1.0 fusion
  17.1 2.4 %collective-permute-start = (f32[3,64,128]{2,1,0:T(8,128)S(1)}, f32[3,64,128]{2,1,0:T(8,128)S(1)}, u32[]{:S(2)}, u32[]{:S(2)}) collective-permute-start(f32[3,64,128]{2,1,0:T(8,128)S(1)} %bitcast.32), channel_id=1, source_target_pairs={{0,8},{8,16},{16,24},{1,9},{9,17},{17,25},{2,10},{10,18},{18,26},{... | collective-permute-start | bytes 294920 | tf_op jit(solution)/shard_map/ppermute | solution.py:375
  19.5 1.3 collective-permute-start.1
  20.8 0.8 slice_bitcast_fusion
  21.6 3.2 %collective-permute-done.1.near_high = f32[3,64,128]{2,1,0:T(8,128)S(1)} collective-permute-done((f32[3,64,128]{2,1,0:T(8,128)S(1)}, f32[3,64,128]{2,1,0:T(8,128)S(1)}, u32[]{:S(2)}, u32[]{:S(2)}) %collective-permute-start.1) | collective-permute-done | bytes 98336 | tf_op jit(solution)/shard_map/ppermute | solution.py:375
  24.8 1.4 collective-permute-start.3
  26.3 4.6 %collective-permute-start.2 = (f32[3,64,128]{2,1,0:T(8,128)S(1)}, f32[3,64,128]{2,1,0:T(8,128)S(1)}, u32[]{:S(2)}, u32[]{:S(2)}) collective-permute-start(f32[3,64,128]{2,1,0:T(8,128)S(1)} %pad_maximum_fusion), channel_id=1, source_target_pairs={{0,1},{1,2},{2,3},{3,4},{4,5},{5,6},{6,7},{8,9},{9,10},{10,11},{11... | collective-permute-start | bytes 294920 | tf_op jit(solution)/shard_map/ppermute | solution.py:375
  30.9 0.6 collective-permute-done.3.high
  31.5 2.6 %collective-permute-done.2.low = f32[3,64,128]{2,1,0:T(8,128)S(1)} collective-permute-done((f32[3,64,128]{2,1,0:T(8,128)S(1)}, f32[3,64,128]{2,1,0:T(8,128)S(1)}, u32[]{:S(2)}, u32[]{:S(2)}) %collective-permute-start.2) | collective-permute-done | bytes 98336 | tf_op jit(solution)/shard_map/ppermute | solution.py:375
  34.1 92.8 %interp.1.own = f32[8,8,512]{2,1,0:T(8,128)S(1)} custom-call(f32[3,64,128]{2,1,0:T(8,128)S(1)} %collective-permute-done.2.low, f32[3,64,128]{2,1,0:T(8,128)S(1)} %collective-permute-done.near_low, f32[3,64,128]{2,1,0:T(8,128)S(1)} %bitcast.30, f32[3,64,128]{2,1,0:T(8,128)S(1)} %collective-permute-done.1.near_high, ...), custom_call_target="tpu_custom_call" | custom-call | tf_op jit(solution)/shard_map/interp/pallas_call | solution.py:421
  126.9 3.0 %collective-permute-start.4 = (f32[5,8,512]{2,1,0:T(8,128)S(1)}, f32[5,8,512]{2,1,0:T(8,128)S(1)}, u32[]{:S(2)}, u32[]{:S(2)}) collective-permute-start(f32[5,8,512]{2,1,0:T(8,128)S(1)} %get-tuple-element.22), channel_id=1, source_target_pairs={{0,8},{8,16},{16,24},{1,9},{9,17},{17,25},{2,10},{10,18},{18,26},{... | collective-permute-start | bytes 245768 | tf_op jit(solution)/shard_map/ppermute | solution.py:375
  130.0 1.3 collective-permute-start.5
  131.3 2.4 %collective-permute-done.5.high.p_high = f32[5,8,512]{2,1,0:T(8,128)S(1)} collective-permute-done((f32[5,8,512]{2,1,0:T(8,128)S(1)}, f32[5,8,512]{2,1,0:T(8,128)S(1)}, u32[]{:S(2)}, u32[]{:S(2)}) %collective-permute-start.5) | collective-permute-done | bytes 81952 | tf_op jit(solution)/shard_map/ppermute | solution.py:375
  133.6 0.6 copy-done.9
  134.3 1.8 pack5.1
  136.1 4.3 %collective-permute-start.6 = (f32[360,128]{1,0:T(8,128)}, f32[360,128]{1,0:T(8,128)S(1)}, u32[]{:S(2)}, u32[]{:S(2)}) collective-permute-start(f32[360,128]{1,0:T(8,128)} %get-tuple-element.8), channel_id=1, source_target_pairs={{0,1},{1,2},{2,3},{3,4},{4,5},{5,6},{6,7},{8,9},{9,10},{10,11},{11... | collective-permute-start | bytes 552968 | tf_op jit(solution)/shard_map/ppermute | solution.py:375
  140.4 1.3 collective-permute-start.7
  141.7 4.7 %collective-permute-start.8 = (f32[3,8,512]{2,1,0:T(8,128)S(1)}, f32[3,8,512]{2,1,0:T(8,128)S(1)}, u32[]{:S(2)}, u32[]{:S(2)}) collective-permute-start(f32[3,8,512]{2,1,0:T(8,128)S(1)} %get-tuple-element.20), channel_id=1, source_target_pairs={{0,8},{8,16},{16,24},{1,9},{9,17},{17,25},{2,10},{10,18},{18,26},{... | collective-permute-start | bytes 147464 | tf_op jit(solution)/shard_map/ppermute | solution.py:375
  146.4 1.3 collective-permute-start.9
  147.8 1.8 collective-permute-done.9.high.d_high
  150.2 1.6 pack3.1
  151.8 5.8 %collective-permute-start.10 = (f32[168,128]{1,0:T(8,128)}, f32[168,128]{1,0:T(8,128)S(1)}, u32[]{:S(2)}, u32[]{:S(2)}) collective-permute-start(f32[168,128]{1,0:T(8,128)} %get-tuple-element.10), channel_id=1, source_target_pairs={{0,1},{1,2},{2,3},{3,4},{4,5},{5,6},{6,7},{8,9},{9,10},{10,11},{11... | collective-permute-start | bytes 258056 | tf_op jit(solution)/shard_map/ppermute | solution.py:375
  157.6 1.3 collective-permute-start.11
  159.0 1.0 collective-permute-done.10.d_left
  160.0 4.8 %collective-permute-done.11.d_right = f32[168,128]{1,0:T(8,128)S(1)} collective-permute-done((f32[168,128]{1,0:T(8,128)}, f32[168,128]{1,0:T(8,128)S(1)}, u32[]{:S(2)}, u32[]{:S(2)}) %collective-permute-start.11) | collective-permute-done | bytes 86048 | tf_op jit(solution)/shard_map/ppermute | solution.py:375
  164.8 0.9 copy-done.1
  165.7 0.9 copy-done.8
  166.6 0.9 copy-done.10
  167.5 0.8 copy-done.12
  168.3 0.8 copy-done.14
  169.1 9.1 %krylov.1 = (f32[12,256,128]{2,1,0:T(8,128)S(1)}, f32[8,128]{1,0:T(8,128)S(1)}) custom-call(s32[4]{0:T(128)S(1)} %add_convert_fusion.inside, f32[8,8,512]{2,1,0:T(8,128)S(1)} %copy-done.1, f32[5,8,512]{2,1,0:T(8,128)S(1)} %copy-done.8, f32[5,8,512]{2,1,0:T(8,128)S(1)} %copy-done.10, f32[360,128]{1,0:T(8,128)S(1)} %collective-permute-done.6.p_left, ...), custom_call_target="tpu_custom_call" | custom-call | tf_op jit(solution)/shard_map/krylov/pallas_call | solution.py:438
  178.2 10.8 %surface.1 = f32[3,3,12,128]{3,2,1,0:T(8,128)S(1)} custom-call(s32[1,9]{1,0:T(1,128)S(1)} %copy-done.15, f32[12,256,128]{2,1,0:T(8,128)S(1)} %get-tuple-element.13.basis, s32[1,3,3,128]{3,2,1,0:T(4,128)S(1)} %copy.12.picks), custom_call_target="tpu_custom_call" | custom-call | tf_op jit(solution)/shard_map/surface/pallas_call | solution.py:448
  189.0 3.5 %collective-permute-start.17 = (f32[3,12,128]{2,1,0:T(8,128)S(1)}, f32[3,12,128]{2,1,0:T(8,128)S(1)}, u32[]{:S(2)}, u32[]{:S(2)}) collective-permute-start(f32[3,12,128]{2,1,0:T(8,128)S(1)} %get-tuple-element.30), channel_id=1, source_target_pairs={{0,8},{8,16},{16,24},{1,9},{9,17},{17,25},{2,10},{10,18},{18,26},{... | collective-permute-start | bytes 55304 | tf_op jit(solution)/shard_map/ppermute | solution.py:375
  192.6 1.3 collective-permute-start.18
  193.9 1.8 collective-permute-start.12
  196.3 4.8 %collective-permute-start.19 = (f32[3,12,128]{2,1,0:T(8,128)S(1)}, f32[3,12,128]{2,1,0:T(8,128)S(1)}, u32[]{:S(2)}, u32[]{:S(2)}) collective-permute-start(f32[3,12,128]{2,1,0:T(8,128)S(1)} %get-tuple-element.27), channel_id=1, source_target_pairs={{0,1},{1,2},{2,3},{3,4},{4,5},{5,6},{6,7},{8,9},{9,10},{10,11},{11... | collective-permute-start | bytes 55304 | tf_op jit(solution)/shard_map/ppermute | solution.py:375
  201.2 1.3 collective-permute-start.20
  202.5 2.5 %collective-permute-start.13 = (f32[8,128]{1,0:T(8,128)S(1)}, f32[8,128]{1,0:T(8,128)S(1)}, u32[]{:S(2)}, u32[]{:S(2)}) collective-permute-start(f32[8,128]{1,0:T(8,128)S(1)} %add.15), channel_id=1, source_target_pairs={{0,16},{8,24},{16,0},{24,8},{1,17},{9,25},{17,1},{25,9},{2,18},{10... | collective-permute-start | bytes 12296 | tf_op jit(solution)/shard_map/ppermute | solution.py:382
  205.0 1.6 collective-permute-done.13
  206.6 2.6 %collective-permute-start.14 = (f32[8,128]{1,0:T(8,128)S(1)}, f32[8,128]{1,0:T(8,128)S(1)}, u32[]{:S(2)}, u32[]{:S(2)}) collective-permute-start(f32[8,128]{1,0:T(8,128)S(1)} %add.16), channel_id=1, source_target_pairs={{0,1},{1,0},{2,3},{3,2},{4,5},{5,4},{6,7},{7,6},{8,9},{9,8},{10,11... | collective-permute-start | bytes 12296 | tf_op jit(solution)/shard_map/ppermute | solution.py:382
  209.2 1.6 collective-permute-done.14
  210.8 1.6 collective-permute-start.15
  212.4 2.0 collective-permute-done.15
  214.4 2.6 %collective-permute-start.16 = (f32[8,128]{1,0:T(8,128)S(1)}, f32[8,128]{1,0:T(8,128)S(1)}, u32[]{:S(2)}, u32[]{:S(2)}) collective-permute-start(f32[8,128]{1,0:T(8,128)S(1)} %add.18), channel_id=1, source_target_pairs={{0,4},{1,5},{2,6},{3,7},{4,0},{5,1},{6,2},{7,3},{8,12},{9,13},{10,... | collective-permute-start | bytes 12296 | tf_op jit(solution)/shard_map/ppermute | solution.py:382
  217.0 1.9 collective-permute-done.16
  219.0 2.0 finish.1
  (58 shorter events, 1.5 us)
Async XLA Ops:
  0.6 33.4 %copy-start.4 = (s32[4,8,8,512]{3,2,1,0:T(8,128)S(1)}, s32[4,8,8,512]{3,2,1,0:T(8,128)}, u32[]{:S(2)}) copy-start(s32[4,8,8,512]{3,2,1,0:T(8,128)} %shift.1) | copy-start | bytes 1572868
  0.6 33.4 %copy-start.5 = (s32[4,8,8,512]{3,2,1,0:T(8,128)S(1)}, s32[4,8,8,512]{3,2,1,0:T(8,128)}, u32[]{:S(2)}) copy-start(s32[4,8,8,512]{3,2,1,0:T(8,128)} %bucket.1) | copy-start | bytes 1572868
  0.7 33.4 %copy-start.6 = (f32[4,8,8,512]{3,2,1,0:T(8,128)S(1)}, f32[4,8,8,512]{3,2,1,0:T(8,128)}, u32[]{:S(2)}) copy-start(f32[4,8,8,512]{3,2,1,0:T(8,128)} %factor.1) | copy-start | bytes 1572868
  17.1 4.5 %collective-permute-start = (f32[3,64,128]{2,1,0:T(8,128)S(1)}, f32[3,64,128]{2,1,0:T(8,128)S(1)}, u32[]{:S(2)}, u32[]{:S(2)}) collective-permute-start(f32[3,64,128]{2,1,0:T(8,128)S(1)} %bitcast.32), channel_id=1, source_target_pairs={{0,8},{8,16},{16,24},{1,9},{9,17},{17,25},{2,10},{10,18},{18,26},{... | collective-permute-start | bytes 294920 | tf_op jit(solution)/shard_map/ppermute | solution.py:375
  19.5 5.3 %collective-permute-start.1 = (f32[3,64,128]{2,1,0:T(8,128)S(1)}, f32[3,64,128]{2,1,0:T(8,128)S(1)}, u32[]{:S(2)}, u32[]{:S(2)}) collective-permute-start(f32[3,64,128]{2,1,0:T(8,128)S(1)} %bitcast.31), channel_id=1, source_target_pairs={{8,0},{16,8},{24,16},{9,1},{17,9},{25,17},{10,2},{18,10},{26,18},{... | collective-permute-start | bytes 294920 | tf_op jit(solution)/shard_map/ppermute | solution.py:375
  24.8 116.9 %copy-start.2 = (f32[8,8,512]{2,1,0:T(8,128)S(1)}, f32[8,8,512]{2,1,0:T(8,128)}, u32[]{:S(2)}) copy-start(f32[8,8,512]{2,1,0:T(8,128)} %rigid.1) | copy-start | bytes 393220
  24.8 6.6 %collective-permute-start.3 = (f32[3,64,128]{2,1,0:T(8,128)S(1)}, f32[3,64,128]{2,1,0:T(8,128)S(1)}, u32[]{:S(2)}, u32[]{:S(2)}) collective-permute-start(f32[3,64,128]{2,1,0:T(8,128)S(1)} %pad_maximum_fusion.1), channel_id=1, source_target_pairs={{1,0},{2,1},{3,2},{4,3},{5,4},{6,5},{7,6},{9,8},{10,9},{11,10},{12... | collective-permute-start | bytes 294920 | tf_op jit(solution)/shard_map/ppermute | solution.py:375
  26.3 121.5 %copy-start.16 = (s32[1,3,3,128]{3,0,2,1:T(1,128)S(1)}, s32[1,3,3,128]{3,0,2,1:T(1,128)}, u32[]{:S(2)}) copy-start(s32[1,3,3,128]{3,0,2,1:T(1,128)} %param.15) | copy-start | bytes 13828
  26.3 7.8 %collective-permute-start.2 = (f32[3,64,128]{2,1,0:T(8,128)S(1)}, f32[3,64,128]{2,1,0:T(8,128)S(1)}, u32[]{:S(2)}, u32[]{:S(2)}) collective-permute-start(f32[3,64,128]{2,1,0:T(8,128)S(1)} %pad_maximum_fusion), channel_id=1, source_target_pairs={{0,1},{1,2},{2,3},{3,4},{4,5},{5,6},{6,7},{8,9},{9,10},{10,11},{11... | collective-permute-start | bytes 294920 | tf_op jit(solution)/shard_map/ppermute | solution.py:375
  34.1 130.8 %copy-start.3 = (f32[8,8,512]{2,1,0:T(8,128)S(1)}, f32[8,8,512]{2,1,0:T(8,128)}, u32[]{:S(2)}) copy-start(f32[8,8,512]{2,1,0:T(8,128)} %rigid.1) | copy-start | bytes 393220
  126.9 6.8 %copy-start = (f32[8,8,512]{2,1,0:T(8,128)}, f32[8,8,512]{2,1,0:T(8,128)S(1)}, u32[]{:S(2)}) copy-start(f32[8,8,512]{2,1,0:T(8,128)S(1)} %interp.1.own) | copy-start | bytes 393220
  126.9 51.3 %copy-start.15 = (s32[1,9]{1,0:T(1,128)S(1)}, s32[1,9]{1,0:T(1,128)}, u32[]{:S(2)}) copy-start(s32[1,9]{1,0:T(1,128)} %tally.1) | copy-start | bytes 112
  126.9 4.4 %collective-permute-start.4 = (f32[5,8,512]{2,1,0:T(8,128)S(1)}, f32[5,8,512]{2,1,0:T(8,128)S(1)}, u32[]{:S(2)}, u32[]{:S(2)}) collective-permute-start(f32[5,8,512]{2,1,0:T(8,128)S(1)} %get-tuple-element.22), channel_id=1, source_target_pairs={{0,8},{8,16},{16,24},{1,9},{9,17},{17,25},{2,10},{10,18},{18,26},{... | collective-permute-start | bytes 245768 | tf_op jit(solution)/shard_map/ppermute | solution.py:375
  130.0 3.7 %collective-permute-start.5 = (f32[5,8,512]{2,1,0:T(8,128)S(1)}, f32[5,8,512]{2,1,0:T(8,128)S(1)}, u32[]{:S(2)}, u32[]{:S(2)}) collective-permute-start(f32[5,8,512]{2,1,0:T(8,128)S(1)} %get-tuple-element.21), channel_id=1, source_target_pairs={{8,0},{16,8},{24,16},{9,1},{17,9},{25,17},{10,2},{18,10},{26,18},{... | collective-permute-start | bytes 245768 | tf_op jit(solution)/shard_map/ppermute | solution.py:375
  131.3 2.4 %copy-start.7 = (f32[5,8,512]{2,1,0:T(8,128)}, f32[5,8,512]{2,1,0:T(8,128)S(1)}, u32[]{:S(2)}) copy-start(f32[5,8,512]{2,1,0:T(8,128)S(1)} %collective-permute-done.4.low.p_low) | copy-start | bytes 245764
  133.6 0.6 copy-start.9
  136.1 28.8 %collective-permute-start.6 = (f32[360,128]{1,0:T(8,128)}, f32[360,128]{1,0:T(8,128)S(1)}, u32[]{:S(2)}, u32[]{:S(2)}) collective-permute-start(f32[360,128]{1,0:T(8,128)} %get-tuple-element.8), channel_id=1, source_target_pairs={{0,1},{1,2},{2,3},{3,4},{4,5},{5,6},{6,7},{8,9},{9,10},{10,11},{11... | collective-permute-start | bytes 552968 | tf_op jit(solution)/shard_map/ppermute | solution.py:375
  140.4 24.4 %collective-permute-start.7 = (f32[360,128]{1,0:T(8,128)}, f32[360,128]{1,0:T(8,128)S(1)}, u32[]{:S(2)}, u32[]{:S(2)}) collective-permute-start(f32[360,128]{1,0:T(8,128)} %get-tuple-element.9), channel_id=1, source_target_pairs={{1,0},{2,1},{3,2},{4,3},{5,4},{6,5},{7,6},{9,8},{10,9},{11,10},{12... | collective-permute-start | bytes 552968 | tf_op jit(solution)/shard_map/ppermute | solution.py:375
  141.7 6.1 %collective-permute-start.8 = (f32[3,8,512]{2,1,0:T(8,128)S(1)}, f32[3,8,512]{2,1,0:T(8,128)S(1)}, u32[]{:S(2)}, u32[]{:S(2)}) collective-permute-start(f32[3,8,512]{2,1,0:T(8,128)S(1)} %get-tuple-element.20), channel_id=1, source_target_pairs={{0,8},{8,16},{16,24},{1,9},{9,17},{17,25},{2,10},{10,18},{18,26},{... | collective-permute-start | bytes 147464 | tf_op jit(solution)/shard_map/ppermute | solution.py:375
  146.4 3.1 %collective-permute-start.9 = (f32[3,8,512]{2,1,0:T(8,128)S(1)}, f32[3,8,512]{2,1,0:T(8,128)S(1)}, u32[]{:S(2)}, u32[]{:S(2)}) collective-permute-start(f32[3,8,512]{2,1,0:T(8,128)S(1)} %get-tuple-element.19), channel_id=1, source_target_pairs={{8,0},{16,8},{24,16},{9,1},{17,9},{25,17},{10,2},{18,10},{26,18},{... | collective-permute-start | bytes 147464 | tf_op jit(solution)/shard_map/ppermute | solution.py:375
  147.8 1.8 copy-start.11
  149.6 0.6 copy-start.13
  151.8 8.2 %collective-permute-start.10 = (f32[168,128]{1,0:T(8,128)}, f32[168,128]{1,0:T(8,128)S(1)}, u32[]{:S(2)}, u32[]{:S(2)}) collective-permute-start(f32[168,128]{1,0:T(8,128)} %get-tuple-element.10), channel_id=1, source_target_pairs={{0,1},{1,2},{2,3},{3,4},{4,5},{5,6},{6,7},{8,9},{9,10},{10,11},{11... | collective-permute-start | bytes 258056 | tf_op jit(solution)/shard_map/ppermute | solution.py:375
  157.6 7.2 %collective-permute-start.11 = (f32[168,128]{1,0:T(8,128)}, f32[168,128]{1,0:T(8,128)S(1)}, u32[]{:S(2)}, u32[]{:S(2)}) collective-permute-start(f32[168,128]{1,0:T(8,128)} %get-tuple-element.11), channel_id=1, source_target_pairs={{1,0},{2,1},{3,2},{4,3},{5,4},{6,5},{7,6},{9,8},{10,9},{11,10},{12... | collective-permute-start | bytes 258056 | tf_op jit(solution)/shard_map/ppermute | solution.py:375
  158.9 58.1 %copy-start.17 = (s32[1,3,3,128]{3,0,2,1:T(1,128)S(1)}, s32[1,3,3,128]{3,0,2,1:T(1,128)}, u32[]{:S(2)}) copy-start(s32[1,3,3,128]{3,0,2,1:T(1,128)} %param.17) | copy-start | bytes 13828
  164.8 0.9 copy-start.1
  165.7 0.9 copy-start.8
  166.6 0.9 copy-start.10
  167.5 0.8 copy-start.12
  168.3 0.8 copy-start.14
  189.0 6.7 %collective-permute-start.17 = (f32[3,12,128]{2,1,0:T(8,128)S(1)}, f32[3,12,128]{2,1,0:T(8,128)S(1)}, u32[]{:S(2)}, u32[]{:S(2)}) collective-permute-start(f32[3,12,128]{2,1,0:T(8,128)S(1)} %get-tuple-element.30), channel_id=1, source_target_pairs={{0,8},{8,16},{16,24},{1,9},{9,17},{17,25},{2,10},{10,18},{18,26},{... | collective-permute-start | bytes 55304 | tf_op jit(solution)/shard_map/ppermute | solution.py:375
  192.6 3.7 %collective-permute-start.18 = (f32[3,12,128]{2,1,0:T(8,128)S(1)}, f32[3,12,128]{2,1,0:T(8,128)S(1)}, u32[]{:S(2)}, u32[]{:S(2)}) collective-permute-start(f32[3,12,128]{2,1,0:T(8,128)S(1)} %get-tuple-element.31), channel_id=1, source_target_pairs={{8,0},{16,8},{24,16},{9,1},{17,9},{25,17},{10,2},{18,10},{26,18},{... | collective-permute-start | bytes 55304 | tf_op jit(solution)/shard_map/ppermute | solution.py:375
  193.9 8.6 %collective-permute-start.12 = (f32[8,128]{1,0:T(8,128)S(1)}, f32[8,128]{1,0:T(8,128)S(1)}, u32[]{:S(2)}, u32[]{:S(2)}) collective-permute-start(f32[8,128]{1,0:T(8,128)S(1)} %get-tuple-element.12), channel_id=1, source_target_pairs={{0,8},{8,0},{16,24},{24,16},{1,9},{9,1},{17,25},{25,17},{2,10},{10... | collective-permute-start | bytes 12296 | tf_op jit(solution)/shard_map/ppermute | solution.py:382
  196.3 22.6 %collective-permute-start.19 = (f32[3,12,128]{2,1,0:T(8,128)S(1)}, f32[3,12,128]{2,1,0:T(8,128)S(1)}, u32[]{:S(2)}, u32[]{:S(2)}) collective-permute-start(f32[3,12,128]{2,1,0:T(8,128)S(1)} %get-tuple-element.27), channel_id=1, source_target_pairs={{0,1},{1,2},{2,3},{3,4},{4,5},{5,6},{6,7},{8,9},{9,10},{10,11},{11... | collective-permute-start | bytes 55304 | tf_op jit(solution)/shard_map/ppermute | solution.py:375
  201.2 17.8 %collective-permute-start.20 = (f32[3,12,128]{2,1,0:T(8,128)S(1)}, f32[3,12,128]{2,1,0:T(8,128)S(1)}, u32[]{:S(2)}, u32[]{:S(2)}) collective-permute-start(f32[3,12,128]{2,1,0:T(8,128)S(1)} %get-tuple-element.28), channel_id=1, source_target_pairs={{1,0},{2,1},{3,2},{4,3},{5,4},{6,5},{7,6},{9,8},{10,9},{11,10},{12... | collective-permute-start | bytes 55304 | tf_op jit(solution)/shard_map/ppermute | solution.py:375
  202.5 4.1 %collective-permute-start.13 = (f32[8,128]{1,0:T(8,128)S(1)}, f32[8,128]{1,0:T(8,128)S(1)}, u32[]{:S(2)}, u32[]{:S(2)}) collective-permute-start(f32[8,128]{1,0:T(8,128)S(1)} %add.15), channel_id=1, source_target_pairs={{0,16},{8,24},{16,0},{24,8},{1,17},{9,25},{17,1},{25,9},{2,18},{10... | collective-permute-start | bytes 12296 | tf_op jit(solution)/shard_map/ppermute | solution.py:382
  206.6 4.2 %collective-permute-start.14 = (f32[8,128]{1,0:T(8,128)S(1)}, f32[8,128]{1,0:T(8,128)S(1)}, u32[]{:S(2)}, u32[]{:S(2)}) collective-permute-start(f32[8,128]{1,0:T(8,128)S(1)} %add.16), channel_id=1, source_target_pairs={{0,1},{1,0},{2,3},{3,2},{4,5},{5,4},{6,7},{7,6},{8,9},{9,8},{10,11... | collective-permute-start | bytes 12296 | tf_op jit(solution)/shard_map/ppermute | solution.py:382
  210.8 3.6 %collective-permute-start.15 = (f32[8,128]{1,0:T(8,128)S(1)}, f32[8,128]{1,0:T(8,128)S(1)}, u32[]{:S(2)}, u32[]{:S(2)}) collective-permute-start(f32[8,128]{1,0:T(8,128)S(1)} %add.17), channel_id=1, source_target_pairs={{0,2},{1,3},{2,0},{3,1},{4,6},{5,7},{6,4},{7,5},{8,10},{9,11},{10,... | collective-permute-start | bytes 12296 | tf_op jit(solution)/shard_map/ppermute | solution.py:382
  214.4 4.5 %collective-permute-start.16 = (f32[8,128]{1,0:T(8,128)S(1)}, f32[8,128]{1,0:T(8,128)S(1)}, u32[]{:S(2)}, u32[]{:S(2)}) collective-permute-start(f32[8,128]{1,0:T(8,128)S(1)} %add.18), channel_id=1, source_target_pairs={{0,4},{1,5},{2,6},{3,7},{4,0},{5,1},{6,2},{7,3},{8,12},{9,13},{10,... | collective-permute-start | bytes 12296 | tf_op jit(solution)/shard_map/ppermute | solution.py:382

commit v2 on v1

--- a/solution.py
+++ b/solution.py
@@ -11,6 +11,8 @@
 ITERS = 4
 COEF = 0.5
 LANES = 128
+CHUNK = 16
+WEIGHT = 4e8
 SUB = 8
 CENTRE = 7.125
 HALF = 6.875
@@ -21,6 +23,10 @@
 
 def params(mib):
     return pltpu.CompilerParams(vmem_limit_bytes=mib * 1024 * 1024)
+
+
+def cost(micro, moved=0):
+    return pl.CostEstimate(flops=int(micro * WEIGHT), bytes_accessed=moved, transcendentals=0)
 
 
 def lookup(table, first, rows, lanes, bits):
@@ -52,54 +58,239 @@
     return lax.fori_loop(0, rows // chunk, step, tuple(zero for _ in indices))
 
 
-def depart_kernel(heat, picks, out, index):
-    ways = picks.shape[1]
-    slots = picks.shape[3]
-    per = slots // LANES
-    for a in range(ways):
-        for b in range(ways):
-            for row in range(0, per, SUB):
-                piece = picks[0, a, b, pl.ds(row * LANES, SUB * LANES)]
-                index[pl.ds((a * ways + b) * per + row, SUB), :] = piece.reshape(SUB, LANES)
+def order2(a, b):
+    if len(a) == 1:
+        return (jnp.minimum(a[0], b[0]),), (jnp.maximum(a[0], b[0]),)
+    swap = a[0] > b[0]
+    low = [jnp.minimum(a[0], b[0])] + [jnp.where(swap, y, x) for x, y in zip(a[1:], b[1:])]
+    high = [jnp.maximum(a[0], b[0])] + [jnp.where(swap, x, y) for x, y in zip(a[1:], b[1:])]
+    return tuple(low), tuple(high)
+
+def sublane_xor(value, mask):
+    sub = lax.broadcasted_iota(jnp.int32, value.shape, 0)
+    return jnp.take_along_axis(value, sub ^ mask, axis=0, mode="promise_in_bounds")
+
+def keep_one(a, other, lower):
+    if len(a) == 1:
+        return (jnp.where(lower, jnp.minimum(a[0], other[0]), jnp.maximum(a[0], other[0])),)
+    take = (a[0] > other[0]) == lower
+    return tuple(jnp.where(take, y, x) for x, y in zip(a, other))
+
+def sort_rows(refs, block):
+    count = refs[0].shape[0] // SUB
+    def load(v):
+        at = pl.ds(pl.multiple_of(v * SUB, SUB), SUB)
+        return tuple(r[at, :] for r in refs)
+    def store(v, value):
+        at = pl.ds(pl.multiple_of(v * SUB, SUB), SUB)
+        for r, x in zip(refs, value): r[at, :] = x
+    def strides(held, stride):
+        while stride:
+            for i in range(len(held)):
+                if not i & stride:
+                    held[i], held[i | stride] = order2(held[i], held[i | stride])
+            stride //= 2
+    def whole(t, carry):
+        held = [load(t * block + i) for i in range(block)]
+        size = 2
+        while size <= block:
+            for i in range(block):
+                j = i ^ (size - 1)
+                if i < j: held[i], held[j] = order2(held[i], held[j])
+            strides(held, size // 4)
+            size *= 2
+        for i in range(block): store(t * block + i, held[i])
+        return carry
+    def finish(t, carry):
+        held = [load(t * block + i) for i in range(block)]
+        strides(held, block // 2)
+        for i in range(block): store(t * block + i, held[i])
+        return carry
+    lax.fori_loop(0, count // block, whole, 0)
+    size = 2 * block
+    while size <= count * SUB:
+        span = min(size, count)
+        flip = size // count - 1 if size > count else 0
+        groups = span // block
+        def top(t, carry):
+            base = (t // (block // 2)) * span
+            i = t % (block // 2)
+            spots = []
+            for j in range(groups):
+                spots += [base + i + block * j, base + block - 1 - i + block * j]
+            held = [load(v) for v in spots]
+            n = len(held)
+            if flip:
+                sub = lax.broadcasted_iota(jnp.int32, (SUB, LANES), 0)
+                lower = (sub & ((flip + 1) // 2)) == 0
+                turned = [tuple(sublane_xor(x, flip) for x in h) for h in held]
+                held = [keep_one(held[k], turned[n - 1 - k], lower) for k in range(n)]
+                bit = (flip + 1) // 4
+                while bit:
+                    lower = (sub & bit) == 0
+                    held = [keep_one(h, tuple(sublane_xor(x, bit) for x in h), lower) for h in held]
+                    bit //= 2
+                far = groups // 2
+            else:
+                for k in range(n // 2):
+                    held[k], held[n - 1 - k] = order2(held[k], held[n - 1 - k])
+                far = groups // 4
+            while far:
+                for j in range(groups):
+                    if not j & far:
+                        for side in range(2):
+                            x, y = 2 * j + side, 2 * (j | far) + side
+                            held[x], held[y] = order2(held[x], held[y])
+                far //= 2
+            for v, h in zip(spots, held): store(v, h)
+            return carry
+        lax.fori_loop(0, (count // span) * (block // 2), top, 0)
+        lax.fori_loop(0, count // block, finish, 0)
+        size *= 2
+
+
+def plan_kernel(per, rows, shift, bucket, keys, bounds):
+    corners, nx, _, nz = shift.shape
+    tiles = nz // LANES
+    count = corners * nx * tiles
+    sub = lax.broadcasted_iota(jnp.int32, (SUB, LANES), 0)
+    def build(x, carry):
+        for c in range(corners):
+            for t in range(tiles):
+                at = pl.ds(t * LANES, LANES)
+                flat = shift[c, x, :, at] * (per * LANES) + bucket[c, x, :, at]
+                if c: flat = pltpu.roll(flat, c * (LANES // corners), axis=1)
+                v = (c * nx + x) * tiles + t
+                keys[pl.ds(pl.multiple_of(v * SUB, SUB), SUB), :] = flat * (count * SUB) + (sub * count + v)
+        return carry
+    lax.fori_loop(0, nx, build, 0)
+    sort_rows([keys], 32)
+    low_bits = int(math.log2(count * SUB * LANES))
+    lane = lax.broadcasted_iota(jnp.int32, (SUB, LANES), 1)
+    base = jnp.zeros((SUB, LANES), jnp.float32)
+    width = jnp.zeros((SUB, 1), jnp.float32)
+    for g in range(count // SUB):
+        least = (keys[pl.ds(g * SUB * SUB, SUB), :] >> low_bits).astype(jnp.float32)
+        most = (keys[pl.ds(g * SUB * SUB + SUB * (SUB - 1), SUB), :] >> low_bits).astype(jnp.float32)
+        least = jnp.min(least, axis=1, keepdims=True)
+        most = jnp.max(most, axis=1, keepdims=True)
+        base = jnp.where(lane == g, least, base)
+        width = jnp.maximum(width, most - least + 1.0)
+    trips = (width.astype(jnp.int32) + (CHUNK - 1)) // CHUNK
+    start = jnp.minimum(base.astype(jnp.int32), rows - trips * CHUNK)
+    bounds[...] = jnp.where(lane == LANES - 1, trips, start)
+
+
+def depart_kernel(heat, picks, rigid, up, down):
+    ways = 3
+    nx, _, nz = rigid.shape
+    tiles = nz // LANES
+    narrow = REACH - 2
+    per = picks.shape[0] // (ways * ways)
+    group = SUB * SUB
+    for a, out, first in ((ways - 1, up, nx - narrow), (0, down, 0)):
+        start = a * ways * per
+
+        def body(g, carry):
+            base = pl.multiple_of(g * group, group)
+            found = lookup_all(heat, [picks[pl.ds(start + base + SUB * k, SUB), :] for k in range(SUB)], heat.shape[0])
+            for k in range(SUB):
+                out[pl.ds(base + SUB * k, SUB), :] = found[k]
+            return carry
+
+        lax.fori_loop(0, ways * per // group, body, 0)
+        for x in range(narrow):
+            for t in range(tiles):
+                row = ways * per + (x * tiles + t) * SUB
+                out[pl.ds(row, SUB), :] = rigid[first + x, :, pl.ds(t * LANES, LANES)]
+
+
+def near_kernel(heat, picks, near):
+    rows = near.shape[0]
     group = SUB * SUB
 
     def body(g, carry):
         base = pl.multiple_of(g * group, group)
-        found = lookup_all(heat, [index[pl.ds(base + SUB * k, SUB), :] for k in range(SUB)], 64)
+        found = lookup_all(heat, [picks[pl.ds(rows + base + SUB * k, SUB), :] for k in range(SUB)], heat.shape[0])
         for k in range(SUB):
-            out[pl.ds(base + SUB * k, SUB), :] = found[k]
-        return carry
-
-    lax.fori_loop(0, ways * ways * per // group, body, 0)
-
-
-def interp_kernel(low, near_low, near, near_high, high, shift, bucket, factor, out, table):
-    corners, nx, _, nz = shift.shape
-    per = near.shape[1]
-    slots = per * LANES
-    for b, ref in ((0, low), (2, high)):
-        for a in range(3):
-            table[pl.ds((3 * a + b) * per, per), :] = ref[a]
-    for a, ref in enumerate((near_low, near, near_high)):
-        table[pl.ds((3 * a + 1) * per, per), :] = ref[1]
-
-    def body(x, carry):
-        for z in range(0, nz, 2 * LANES):
-            where = []
+            near[pl.ds(base + SUB * k, SUB), :] = found[k]
+        return carry
+
+    lax.fori_loop(0, rows // group, body, 0)
+
+
+def forward_kernel(low, near, high, rigid, up, down):
+    nx, ny, nz = rigid.shape
+    per = near.shape[0] // 3
+    narrow = REACH - 2
+    tiles = nz // LANES
+    extent = nx + 2 * narrow
+    for out, b, y in ((up, 2, ny - narrow), (down, 0, 0)):
+        for a, ref in enumerate((low, near, high)):
+            out[pl.ds(a * per, per), :] = ref[pl.ds(b * per, per), :]
+        for t in range(tiles):
+            for x in range(extent):
+                to = pl.ds(3 * per + (t * extent + x) * narrow, narrow)
+                if narrow <= x < narrow + nx:
+                    out[to, :] = rigid[x - narrow, pl.ds(y, narrow), pl.ds(t * LANES, LANES)]
+                else:
+                    ref, k = (low, x) if x < narrow else (high, x - narrow - nx)
+                    out[to, :] = ref[pl.ds(3 * per + (k * tiles + t) * SUB + y, narrow), :]
+
+
+def pick_kernel(left, low, near, high, right, keys, bounds, factor, out, table, position, value):
+    corners, nx, _, nz = factor.shape
+    tiles = nz // LANES
+    slots = near.shape[0] // 3
+    for a, ref in enumerate((low, near, high)):
+        table[pl.ds((3 * a) * slots, slots), :] = left[pl.ds(a * slots, slots), :]
+        table[pl.ds((3 * a + 1) * slots, slots), :] = ref[pl.ds(slots, slots), :]
+        table[pl.ds((3 * a + 2) * slots, slots), :] = right[pl.ds(a * slots, slots), :]
+    count = keys.shape[0] // SUB
+    pos_bits = int(math.log2(count * SUB))
+    depth = int(math.log2(CHUNK))
+    per = count // SUB
+
+    def body(s, carry):
+        own = [keys[pl.ds(SUB * SUB * g + s, SUB, stride=SUB), :] for g in range(per)]
+        start = [bounds[s, g] for g in range(per)]
+
+        def step(n, found):
+            fresh = []
+            for g in range(per):
+                lanes = (own[g] >> pos_bits) & (LANES - 1)
+                first = start[g] + n * CHUNK
+                rel = (own[g] >> (pos_bits + 7)) - first
+                bits = [((rel >> b) & 1) == 1 for b in range(depth)]
+                fresh.append(jnp.where((rel >> depth) == 0, lookup(table, first, CHUNK, lanes, bits), found[g]))
+            return tuple(fresh)
+
+        zero = jnp.zeros((SUB, LANES), jnp.float32)
+        found = lax.fori_loop(0, bounds[s, LANES - 1], step, tuple(zero for _ in range(per)))
+        for g in range(per):
+            at = pl.ds(SUB * SUB * g + s, SUB, stride=SUB)
+            value[at, :] = found[g]
+            position[at, :] = own[g] & (count * SUB - 1)
+        return carry
+
+    lax.fori_loop(0, SUB, body, 0)
+    sort_rows([position, value], 16)
+
+    def blend(x, carry):
+        for t in range(tiles):
+            at = pl.ds(t * LANES, LANES)
+            total = None
             for c in range(corners):
-                for part in range(2):
-                    at = pl.ds(z + part * LANES, LANES)
-                    where.append(shift[c, x, :, at] * slots + bucket[c, x, :, at])
-            found = lookup_all(table, where, 64)
-            for part in range(2):
-                at = pl.ds(z + part * LANES, LANES)
-                total = factor[0, x, :, at] * found[part]
-                for c in range(1, corners):
-                    total = total + factor[c, x, :, at] * found[2 * c + part]
-                out[x, :, at] = total
-        return carry
-
-    lax.fori_loop(0, nx, body, 0)
+                v = (c * nx + x) * tiles + t
+                got = value[pl.ds(pl.multiple_of(v * SUB, SUB), SUB), :]
+                if c:
+                    got = pltpu.roll(got, LANES - c * (LANES // corners), axis=1)
+                got = factor[c, x, :, at] * got
+                total = got if total is None else total + got
+            out[x, :, at] = total
+        return carry
+
+    lax.fori_loop(0, nx, blend, 0)
 
 
 def pack_kernel(width, low, own, high, up, down):
@@ -118,24 +309,23 @@
             down[to, :] = ref[k, pl.ds(0, width), at]
 
 
-def unpack(target, margin, width, own, dom_low, dom_high, slab_low, slab_high, change):
+def unpack(target, width, own, dom_low, dom_high, slab_low, slab_high, change):
     nx, ny, nz = own.shape
     tiles = nz // LANES
     extent = nx + 2 * width
     start = REACH - width
     for t in range(tiles):
-        at = pl.ds(t * LANES, LANES)
         for x in range(extent):
             if x < width:
-                ref, k = dom_low, x
+                mine = dom_low(x, t)
             elif x < width + nx:
-                ref, k = own, x - width
+                mine = own[x - width, :, pl.ds(t * LANES, LANES)]
             else:
-                ref, k = dom_high, x - width - nx
-            rows = pl.ds((t * extent + x) * width, width)
-            target[t, start + x, pl.ds(SUB, ny), :] = change(ref[k, :, at], start + x, 1)
-            target[t, start + x, pl.ds(SUB - width, width), :] = change(slab_low[rows, :], start + x, 0)
-            target[t, start + x, pl.ds(SUB + ny, width), :] = change(slab_high[rows, :], start + x, 2)
+                mine = dom_high(x - width - nx, t)
+            row = (t * extent + x) * width
+            target[t, start + x, pl.ds(SUB, ny), :] = change(mine, start + x, 1)
+            target[t, start + x, pl.ds(SUB - width, width), :] = change(slab_low(row), start + x, 0)
+            target[t, start + x, pl.ds(SUB + ny, width), :] = change(slab_high(row), start + x, 2)
 
 
 def krylov_kernel(inside, own, p_low, p_high, p_left, p_right, rigid, d_low, d_high, d_left, d_right,
@@ -151,9 +341,23 @@
         return at_x * (flag[2] if part == 0 else flag[3] if part == 2 else 1.0)
 
     temp[...] = jnp.zeros_like(temp)
-    unpack(temp, REACH, REACH, own, p_low, p_high, p_left, p_right, lambda v, x, part: v)
+    wide, narrow = REACH, REACH - 2
+    base = d_left.shape[0] - tiles * (nx + 2 * narrow) * narrow
+
+    def plane(ref):
+        return lambda x, t: ref[x, :, pl.ds(t * LANES, LANES)]
+
+    def message(ref):
+        return lambda x, t: ref[pl.ds(base + (x * tiles + t) * SUB, SUB), :]
+
+    def packed(ref, offset, width):
+        return lambda row: ref[pl.ds(offset + row, width), :]
+
+    unpack(temp, wide, own, plane(p_low), plane(p_high), packed(p_left, 0, wide), packed(p_right, 0, wide),
+           lambda v, x, part: v)
     diag[...] = jnp.zeros_like(diag)
-    unpack(diag, REACH, REACH - 2, rigid, d_low, d_high, d_left, d_right,
+    unpack(diag, narrow, rigid, message(d_low), message(d_high), packed(d_left, base, narrow),
+           packed(d_right, base, narrow),
            lambda v, x, part: (v * (2.0 / HALF) + 2.0 * (6.0 - CENTRE) / HALF) * mask(x, part))
     lane = lax.broadcasted_iota(jnp.int32, (SUB, LANES), 1)
     first, last = lane == 0, lane == LANES - 1
@@ -242,29 +446,63 @@
 
 def surface_kernel(nz, tally, basis, picks, out, index, live):
     fields, rows, _ = basis.shape
-    ways = picks.shape[1]
-    count = ways * ways
+    count = picks.shape[0]
     block = rows // (nz // LANES)
     lane = lax.broadcasted_iota(jnp.int32, (1, LANES), 1)
-    index[...] = jnp.zeros_like(index)
-    live[...] = jnp.zeros_like(live)
-    for a in range(ways):
-        for b in range(ways):
-            spot = picks[0, a, pl.ds(b, 1), :]
-            along = spot % nz
-            high = (along // LANES) * block + spot // nz
-            index[pl.ds(a * ways + b, 1), :] = high * LANES + spot % LANES
-            live[pl.ds(a * ways + b, 1), :] = (lane < tally[0, a * ways + b]).astype(jnp.float32)
+    sub = lax.broadcasted_iota(jnp.int32, (SUB, LANES), 0)
+    out[...] = jnp.zeros_like(out)
+    for k in range(count):
+        spot = picks[k]
+        along = spot % nz
+        index[pl.ds(k, 1), :] = ((along // LANES) * block + spot // nz) * LANES + spot % LANES
+        live[pl.ds(k, 1), :] = (lane < tally[0, k]).astype(jnp.float32)
+    depth = int(math.log2(rows))
 
     def body(f, carry):
-        found = lookup_all(basis.at[f], [index[pl.ds(0, SUB), :], index[pl.ds(SUB, SUB), :]], 64)
-        for k in range(count):
-            value = found[k // SUB][k % SUB : k % SUB + 1, :]
-            value = jnp.where(live[pl.ds(k, 1), :] > 0.5, value, 0.0)
-            out[k // ways, k % ways, pl.ds(f, 1), :] = value
+        table = basis.at[f]
+        spots = index[pl.ds(0, SUB), :]
+        high = spots >> 7
+        bits = [((high >> bit) & 1) == 1 for bit in range(depth)]
+        found = lookup(table, 0, rows, spots & (LANES - 1), bits)
+        found = jnp.where(live[pl.ds(0, SUB), :] > 0.5, found, 0.0)
+        for k in range(SUB):
+            out[pl.ds(SUB + k * fields + f, 1), :] = found[k : k + 1, :]
+        for k in range(SUB, count):
+            spots = jnp.broadcast_to(index[pl.ds(k, 1), :], (SUB, LANES))
+            lanes, high = spots & (LANES - 1), spots >> 7
+            total = jnp.zeros((SUB, LANES), jnp.float32)
+            for g in range(0, rows, SUB):
+                got = jnp.take_along_axis(table[pl.ds(g, SUB), :], lanes, axis=1, mode="promise_in_bounds")
+                total = jnp.where(high == sub + g, got, total)
+            total = jnp.sum(total, axis=0, keepdims=True)
+            total = jnp.where(live[pl.ds(k, 1), :] > 0.5, total, 0.0)
+            out[pl.ds(SUB + k * fields + f, 1), :] = total
         return carry
 
     lax.fori_loop(0, fields, body, 0)
+
+
+def route_kernel(place, gathered, keep, pair, other):
+    peers = gathered.shape[0]
+    fields = 3 * ITERS
+    total = gathered[0, pl.ds(0, SUB), :]
+    for k in range(1, peers):
+        total = total + gathered[k, pl.ds(0, SUB), :]
+    pair[...] = jnp.zeros_like(pair)
+    other[...] = jnp.zeros_like(other)
+    pair[pl.ds(0, SUB), :] = total
+    odd = place[4]
+    for a in range(3):
+        source = place[5] + a - 1
+        here = jnp.logical_and(source >= 0, source < peers).astype(jnp.float32)
+        source = jnp.clip(source, 0, peers - 1)
+        rows = [SUB + (3 * (2 - a) + b) * fields for b in range(3)]
+        to = pl.ds(SUB + a * fields, fields)
+        low = gathered[source, pl.ds(rows[0], fields), :] * here
+        high = gathered[source, pl.ds(rows[2], fields), :] * here
+        keep[pl.ds(a * fields, fields), :] = gathered[source, pl.ds(rows[1], fields), :] * here
+        pair[to, :] = jnp.where(odd == 1, low, high)
+        other[to, :] = jnp.where(odd == 1, high, low)
 
 
 def coefficients(nu):
@@ -316,8 +554,9 @@
     return found
 
 
-def finish_kernel(sums, basis, surface, picks, disp, thermal, shift):
-    raw = [jnp.broadcast_to(jnp.sum(sums[pl.ds(k, 1), :], axis=1, keepdims=True), (1, LANES)) for k in range(8)]
+def finish_kernel(place, keep, pair, sent, other, basis, picks, disp, thermal, shift):
+    sums = sent[pl.ds(0, SUB), :] + other[pl.ds(0, SUB), :]
+    raw = [jnp.broadcast_to(jnp.sum(sums[k : k + 1, :], axis=1, keepdims=True), (1, LANES)) for k in range(8)]
     nu = [raw[0], raw[1]]
     for k in range(2, 7):
         nu.append(2.0 * raw[k] - raw[k % 2])
@@ -338,27 +577,35 @@
         return carry
 
     lax.fori_loop(0, nx, row, 0)
-    ways = picks.shape[1]
     depth = thermal.shape[1] // LANES
-    place = lax.broadcasted_iota(jnp.int32, (LANES, LANES), 0)
+    fields = 3 * ITERS
+    spot_of = lax.broadcasted_iota(jnp.int32, (LANES, LANES), 0)
     tall = lax.broadcasted_iota(jnp.int32, (depth, LANES), 0)
     total = jnp.zeros((9 * depth, LANES), jnp.float32)
-    for a in range(ways):
-        for b in range(ways):
-            spot = picks[0, a, pl.ds(b, 1), :]
-            lane_hot = (place == spot % LANES).astype(jnp.float32).astype(jnp.bfloat16)
+    odd = place[4]
+    for ref, offset, b, here in (
+        (keep, 0, 1, 1),
+        (pair, SUB, 2 - 2 * odd, jnp.where(odd == 1, place[2], place[3])),
+        (other, SUB, 2 * odd, jnp.where(odd == 1, place[3], place[2])),
+    ):
+        valid = jnp.full((1, LANES), here, jnp.int32) == 1
+        for a in range(3):
+            spot = picks[3 * a + b]
+            lane_hot = (spot_of == spot % LANES).astype(jnp.float32).astype(jnp.bfloat16)
             row_hot = tall == spot // LANES
             pieces = []
             for c in range(3):
-                value = weights[0] * surface[a, b, pl.ds(c, 1), :]
-                for j in range(1, 4):
-                    value = value + weights[j] * surface[a, b, pl.ds(3 * j + c, 1), :]
+                value = None
+                for j in range(ITERS):
+                    term = weights[j] * ref[pl.ds(offset + a * fields + 3 * j + c, 1), :]
+                    value = term if value is None else value + term
+                value = jnp.where(valid, value, 0.0)
                 for _ in range(3):
                     part = value.astype(jnp.bfloat16).astype(jnp.float32)
                     value = value - part
                     pieces.append(jnp.where(row_hot, jnp.broadcast_to(part, row_hot.shape), 0.0))
-            left = jnp.concatenate(pieces, axis=0).astype(jnp.bfloat16)
-            total = total + lax.dot_general(left, lane_hot, (((1,), (1,)), ((), ())),
+            wanted = jnp.concatenate(pieces, axis=0).astype(jnp.bfloat16)
+            total = total + lax.dot_general(wanted, lane_hot, (((1,), (1,)), ((), ())),
                                             preferred_element_type=jnp.float32)
     for c in range(3):
         whole = total[3 * c * depth : (3 * c + 1) * depth]
@@ -375,98 +622,88 @@
     return lax.ppermute(last, axis, up), lax.ppermute(leading, axis, down)
 
 
-def total_over(value, axis):
-    peers = lax.axis_size(axis)
-    hop = 1
-    while hop < peers:
-        value = value + lax.ppermute(value, axis, [(i, i ^ hop) for i in range(peers)])
-        hop *= 2
-    return value
-
-
 def on_device(heat_level, emitting, holder, bucket, factors, rigidity, boundary, tally, accepting):
-    f32 = jnp.float32
+    f32, i32 = jnp.float32, jnp.int32
     ways = emitting.shape[1]
-    slots = emitting.shape[3]
-    per = slots // LANES
+    per = emitting.shape[3] // LANES
     nx, ny, nz = rigidity.shape
     tiles = nz // LANES
+    narrow = REACH - 2
     call = pl.pallas_call
+    shape = jax.ShapeDtypeStruct
+    dom, slab = lax.axis_index("dom"), lax.axis_index("slab")
+    place = jnp.stack([dom > 0, dom < lax.axis_size("dom") - 1, slab > 0, slab < lax.axis_size("slab") - 1,
+                       slab % 2, dom]).astype(i32)
     heat = heat_level.reshape(-1, LANES)
-    departing = call(
-        depart_kernel,
-        out_shape=jax.ShapeDtypeStruct((ways * ways * per, LANES), f32),
-        in_specs=[VMEM] * 2,
-        out_specs=VMEM,
-        scratch_shapes=[pltpu.VMEM((ways * ways * per, LANES), jnp.int32)],
-        name="depart",
-    )(heat, emitting).reshape(ways, ways, per, LANES)
-    from_low, from_high = swap(departing[2], departing[0], "dom")
-    near = departing[1]
-    up = jnp.stack([from_low[2], near[2], from_high[2]])
-    down = jnp.stack([from_low[0], near[0], from_high[0]])
+    emit_rows = emitting.reshape(-1, LANES)
+    dom_message = shape((ways * per + narrow * tiles * ny, LANES), f32)
+    up, down = call(depart_kernel, out_shape=(dom_message,) * 2, in_specs=[VMEM] * 3, out_specs=(VMEM,) * 2,
+                    compiler_params=params(6), cost_estimate=cost(8), name="depart")(heat, emit_rows, rigidity)
+    from_low, from_high = swap(up, down, "dom")
+    near = call(near_kernel, out_shape=shape((ways * per, LANES), f32), in_specs=[VMEM] * 2, out_specs=VMEM,
+                compiler_params=params(4), cost_estimate=cost(4), name="near")(heat, emit_rows)
+    count = holder.size // LANES
+    rows = ways * ways * per
+    keys, bounds = call(
+        functools.partial(plan_kernel, per, rows),
+        out_shape=(shape((count, LANES), i32), shape((SUB, LANES), i32)),
+        in_specs=[VMEM] * 2, out_specs=(VMEM, VMEM), compiler_params=params(6), cost_estimate=cost(5), name="plan",
+    )(holder, bucket)
+    slab_message = shape((ways * per + tiles * (nx + 2 * narrow) * narrow, LANES), f32)
+    up, down = call(forward_kernel, out_shape=(slab_message,) * 2, in_specs=[VMEM] * 4, out_specs=(VMEM,) * 2,
+                    compiler_params=params(6), cost_estimate=cost(1), name="forward")(from_low, near, from_high, rigidity)
     left, right = swap(up, down, "slab")
-
-    narrow = REACH - 2
-
-    def packed(width, low, own, high):
-        shape = jax.ShapeDtypeStruct((tiles * (nx + 2 * width) * width, LANES), f32)
-        return call(functools.partial(pack_kernel, width), out_shape=(shape, shape), in_specs=[VMEM] * 3,
-                    out_specs=(VMEM, VMEM), name=f"pack{width}")(low, own, high)
-
-    d_low, d_high = swap(rigidity[nx - narrow :], rigidity[:narrow], "dom")
-    d_up, d_down = packed(narrow, d_low, rigidity, d_high)
-    d_left, d_right = swap(d_up, d_down, "slab")
-
     interp = call(
-        interp_kernel,
-        out_shape=jax.ShapeDtypeStruct((nx, ny, nz), f32),
-        in_specs=[VMEM] * 8,
-        out_specs=VMEM,
-        scratch_shapes=[pltpu.VMEM((ways * ways * per, LANES), f32)],
-        compiler_params=params(32),
-        name="interp",
-    )(left, from_low, near, from_high, right, holder, bucket, factors)
-
+        pick_kernel, out_shape=shape((nx, ny, nz), f32), in_specs=[VMEM] * 6 + [SMEM, VMEM], out_specs=VMEM,
+        scratch_shapes=[pltpu.VMEM((rows, LANES), f32), pltpu.VMEM((count, LANES), i32), pltpu.VMEM((count, LANES), f32)],
+        compiler_params=params(8), cost_estimate=cost(14), name="pick",
+    )(left, from_low, near, from_high, right, keys, bounds, factors)
     p_low, p_high = swap(interp[nx - REACH :], interp[:REACH], "dom")
-    p_up, p_down = packed(REACH, p_low, interp, p_high)
-    p_left, p_right = swap(p_up, p_down, "slab")
-    dom, slab = lax.axis_index("dom"), lax.axis_index("slab")
-    inside = jnp.stack([dom > 0, dom < lax.axis_size("dom") - 1, slab > 0, slab < lax.axis_size("slab") - 1])
+    halo = shape((tiles * (nx + 2 * REACH) * REACH, LANES), f32)
+    up, down = call(functools.partial(pack_kernel, REACH), out_shape=(halo, halo), in_specs=[VMEM] * 3,
+                    out_specs=(VMEM, VMEM), compiler_params=params(6), cost_estimate=cost(1), name="pack")(p_low, interp, p_high)
+    p_left, p_right = swap(up, down, "slab")
     extent = nx + 2 * REACH
     field = pltpu.VMEM((3, tiles, extent, 3 * SUB, LANES), f32)
     basis, sums = call(
         krylov_kernel,
-        out_shape=(jax.ShapeDtypeStruct((3 * ITERS, tiles * nx * ny, LANES), f32), jax.ShapeDtypeStruct((SUB, LANES), f32)),
+        out_shape=(shape((3 * ITERS, tiles * nx * ny, LANES), f32), shape((SUB, LANES), f32)),
         in_specs=[SMEM] + [VMEM] * 10,
         out_specs=(VMEM, VMEM),
         scratch_shapes=[pltpu.VMEM((tiles, extent, 3 * SUB, LANES), f32)] * 2 + [field] * 4,
-        compiler_params=params(48),
-        name="krylov",
-    )(inside.astype(jnp.int32), interp, p_low, p_high, p_left, p_right, rigidity, d_low, d_high, d_left, d_right)
-    sums = total_over(total_over(sums, "dom"), "slab")
+        compiler_params=params(20), cost_estimate=cost(7), name="krylov",
+    )(place, interp, p_low, p_high, p_left, p_right, rigidity, from_low, from_high, left, right)
+    peers = lax.axis_size("slab")
+    hop = peers // 2
+    while hop >= 4:
+        sums = sums + lax.ppermute(sums, "slab", [(i, (i + hop) % peers) for i in range(peers)])
+        hop //= 2
+    fields = 3 * ITERS
+    length = SUB + -(-ways * ways * fields // SUB) * SUB
     surface = call(
-        functools.partial(surface_kernel, nz),
-        out_shape=jax.ShapeDtypeStruct((ways, ways, 3 * ITERS, LANES), f32),
-        in_specs=[SMEM, VMEM, VMEM],
-        out_specs=VMEM,
-        scratch_shapes=[pltpu.VMEM((2 * SUB, LANES), jnp.int32), pltpu.VMEM((2 * SUB, LANES), f32)],
-        compiler_params=params(16),
-        name="surface",
-    )(tally, basis, boundary)
-    s_low, s_high = swap(surface[2], surface[0], "dom")
-    stacked = jnp.stack([s_low, surface[1], s_high])
-    s_left, s_right = swap(stacked[:, 2], stacked[:, 0], "slab")
-    arrived = jnp.stack([s_left, stacked[:, 1], s_right], axis=1)
+        functools.partial(surface_kernel, nz), out_shape=shape((length, LANES), f32), in_specs=[SMEM, VMEM, VMEM],
+        out_specs=VMEM, scratch_shapes=[pltpu.VMEM((2 * SUB, LANES), i32), pltpu.VMEM((2 * SUB, LANES), f32)],
+        compiler_params=params(6), cost_estimate=cost(4), name="surface",
+    )(tally, basis, boundary.reshape(-1, 1, LANES))
+    gathered = lax.all_gather(lax.dynamic_update_slice(surface, sums, (0, 0)), "dom")
+    short = -(-ways * fields // SUB) * SUB
+    message = shape((SUB + short, LANES), f32)
+    keep, pair, other = call(
+        route_kernel, out_shape=(shape((short, LANES), f32), message, message), in_specs=[SMEM, VMEM],
+        out_specs=(VMEM,) * 3, compiler_params=params(4), cost_estimate=cost(1), name="route",
+    )(place, gathered)
+    pair_in = lax.ppermute(pair, "slab", [(i, i ^ 1) for i in range(peers)])
+    sent = lax.dynamic_update_slice(other, pair[:SUB] + pair_in[:SUB], (0, 0))
+    rounds = [(i, (i + 1) % peers if i % 2 else (i - 1) % peers) for i in range(peers)]
+    other_in = lax.ppermute(sent, "slab", rounds)
     return call(
         finish_kernel,
-        out_shape=(jax.ShapeDtypeStruct((3, nx, ny, nz), f32), jax.ShapeDtypeStruct((3, heat_level.shape[0]), f32)),
-        in_specs=[VMEM] * 4,
+        out_shape=(shape((3, nx, ny, nz), f32), shape((3, heat_level.shape[0]), f32)),
+        in_specs=[SMEM] + [VMEM] * 6,
         out_specs=(VMEM, VMEM),
         scratch_shapes=[pltpu.VMEM((heat_level.shape[0] // LANES, LANES), f32)],
-        compiler_params=params(32),
-        name="finish",
-    )(sums, basis, arrived, accepting)
+        compiler_params=params(8), cost_estimate=cost(2), name="finish",
+    )(place, keep, pair_in, sent, other_in, basis, accepting.reshape(-1, 1, LANES))
 
 
 def solution(mesh):

time: 222 us -> 107 us (0.48)
  Pallas kernels: 131 us -> 45.9 us
  starting transfers between devices: 54.8 us -> 31.1 us
  blocking collectives: 0 us -> 7.7 us
  local copies, waits for them, and re-layouts: 9.44 us -> 2.83 us
  waiting for transfers between devices: 24.1 us -> 17.9 us
    pallas_call x7 -> x10, Pallas kernels: 131 us -> 45.9 us  [the longest x1 13.2 us: on_device(): call(pick_kernel, out_shape=shape((nx, ny, nz), f32), in_specs=[VMEM] * 6...]
    ppermute x16 -> x8, starting transfers between devices: 43.7 us -> 22.9 us  [swap(): return (lax.ppermute(last, axis, up), lax.ppermute(leading, axis, down))]
    all_gather x0 -> x1, blocking collectives: none -> 7.7 us  [on_device(): lax.all_gather(lax.dynamic_update_slice(surface, sums, (0, 0)), 'dom')]
    ppermute x16 -> x8, waiting for transfers between devices: 17 us -> 11.4 us  [swap(): return (lax.ppermute(last, axis, up), lax.ppermute(leading, axis, down))]
    unnamed x39 -> x20, local copies, waits for them, and re-layouts: 7.6 us -> 2.74 us
    ppermute x5 -> x3, starting transfers between devices: 11.2 us -> 8.19 us  [the longest x1 4.33 us: on_device(): lax.ppermute(sums, 'slab', [(i, (i + hop) % peers) for i in range(peers)])]
    ppermute x5 -> x3, waiting for transfers between devices: 7.09 us -> 6.56 us  [the longest x1 4.34 us: on_device(): other_in = lax.ppermute(sent, 'slab', rounds)]
  transfers between devices with their start and end apart: 21 -> 11, of which waited for: 12 -> 7; matrix products, arithmetic and copies ran while one was open for 0% -> 0% of each run, Pallas kernels for 1% -> 13%
where the time goes in v2:
time: 107 us; the launch traced here: 106 us
  Pallas kernels  45.9 us (43%)
  starting transfers between devices  31.1 us (29%)
  waiting for transfers between devices  17.9 us (17%)
  blocking collectives  7.7 us (7%)
  local copies, waits for them, and re-layouts  2.83 us (3%)
    ppermute x8, starting transfers between devices, swap(): return (lax.ppermute(last, axis, up), lax.ppermute(leading, axis, down))  22.9 us
    pallas_call x1, Pallas kernels, on_device(): call(pick_kernel, out_shape=shape((nx, ny, nz), f32), in_specs=[VMEM] * 6...  13.2 us
    ppermute x8, waiting for transfers between devices, swap(): return (lax.ppermute(last, axis, up), lax.ppermute(leading, axis, down))  11.4 us
    pallas_call x1, Pallas kernels, on_device(): call(krylov_kernel, out_shape=(shape((3 * ITERS, tiles * nx * ny, LANES),...  9.06 us
    all_gather x1, blocking collectives, on_device(): lax.all_gather(lax.dynamic_update_slice(surface, sums, (0, 0)), 'dom')  7.7 us
    pallas_call x1, Pallas kernels, on_device(): call(depart_kernel, out_shape=(dom_message,) * 2, in_specs=[VMEM] * 3, ou...  7.08 us
    pallas_call x1, Pallas kernels, on_device(): call(functools.partial(surface_kernel, nz), out_shape=shape((length, LANE...  5.26 us
    pallas_call x1, Pallas kernels, on_device(): call(functools.partial(plan_kernel, per, rows), out_shape=(shape((count,...  4.53 us
  transfers between devices with their start and end apart: 11, of which 7 were waited for; matrix products, arithmetic and copies ran while one was open for 0% of the time, Pallas kernels for 13%

profile of v2, /device:TPU:0, one launch (start us, length us, event | category | flops | bytes accessed | tf_op | source)
XLA Modules:
  0.0 106.3 jit_solution(8317406620814957681)
XLA Ops:
  0.6 0.0 copy-start.3
  0.6 1.0 copy-done.3
  1.6 0.9 copy-done.4
  2.5 0.8 copy-done.6
  3.3 7.1 %depart.1 = (f32[288,128]{1,0:T(8,128)S(1)}, f32[288,128]{1,0:T(8,128)S(1)}) custom-call(f32[128,128]{1,0:T(8,128)S(1)} %bitcast.16, s32[576,128]{1,0:T(8,128)S(1)} %bitcast.14, f32[8,8,512]{2,1,0:T(8,128)S(1)} %copy-done.4), custom_call_target="tpu_custom_call" | custom-call | flops 3200000000 | tf_op jit(solution)/shard_map/depart/pallas_call | solution.py:640
  10.4 2.4 %collective-permute-start = (f32[288,128]{1,0:T(8,128)S(1)}, f32[288,128]{1,0:T(8,128)S(1)}, u32[]{:S(2)}, u32[]{:S(2)}) collective-permute-start(f32[288,128]{1,0:T(8,128)S(1)} %get-tuple-element.15), channel_id=1, source_target_pairs={{0,8},{8,16},{16,24},{1,9},{9,17},{17,25},{2,10},{10,18},{18,26},{... | collective-permute-start | bytes 442376 | tf_op jit(solution)/shard_map/ppermute | solution.py:622
  12.8 0.0 copy-start
  12.8 0.0 copy-start.1
  12.9 1.4 %collective-permute-start.1 = (f32[288,128]{1,0:T(8,128)S(1)}, f32[288,128]{1,0:T(8,128)S(1)}, u32[]{:S(2)}, u32[]{:S(2)}) collective-permute-start(f32[288,128]{1,0:T(8,128)S(1)} %get-tuple-element.16), channel_id=1, source_target_pairs={{8,0},{16,8},{24,16},{9,1},{17,9},{25,17},{10,2},{18,10},{26,18},{... | collective-permute-start | bytes 442376 | tf_op jit(solution)/shard_map/ppermute | solution.py:622
  14.3 3.5 %near.1 = f32[192,128]{1,0:T(8,128)S(1)} custom-call(f32[128,128]{1,0:T(8,128)S(1)} %bitcast.17, s32[576,128]{1,0:T(8,128)S(1)} %bitcast.15), custom_call_target="tpu_custom_call" | custom-call | flops 1600000000 | tf_op jit(solution)/shard_map/near/pallas_call | solution.py:643
  17.8 0.0 collective-permute-done.low.d_low
  17.8 0.5 collective-permute-done.1.high.d_high
  18.4 0.1 forward.1
  18.4 3.7 %collective-permute-start.2 = (f32[360,128]{1,0:T(8,128)S(1)}, f32[360,128]{1,0:T(8,128)S(1)}, u32[]{:S(2)}, u32[]{:S(2)}) collective-permute-start(f32[360,128]{1,0:T(8,128)S(1)} %get-tuple-element.17), channel_id=1, source_target_pairs={{0,1},{1,2},{2,3},{3,4},{4,5},{5,6},{6,7},{8,9},{9,10},{10,11},{11... | collective-permute-start | bytes 552968 | tf_op jit(solution)/shard_map/ppermute | solution.py:622
  22.1 0.0 copy-start.2
  22.2 1.4 %collective-permute-start.3 = (f32[360,128]{1,0:T(8,128)S(1)}, f32[360,128]{1,0:T(8,128)S(1)}, u32[]{:S(2)}, u32[]{:S(2)}) collective-permute-start(f32[360,128]{1,0:T(8,128)S(1)} %get-tuple-element.18), channel_id=1, source_target_pairs={{1,0},{2,1},{3,2},{4,3},{5,4},{6,5},{7,6},{9,8},{10,9},{11,10},{12... | collective-permute-start | bytes 552968 | tf_op jit(solution)/shard_map/ppermute | solution.py:622
  23.6 0.0 copy-done
  23.6 0.0 copy-done.1
  23.6 4.5 %plan.1 = (s32[1024,128]{1,0:T(8,128)S(1)}, s32[8,128]{1,0:T(8,128)S(1)}) custom-call(s32[4,8,8,512]{3,2,1,0:T(8,128)S(1)} %copy-done, s32[4,8,8,512]{3,2,1,0:T(8,128)S(1)} %copy-done.1), custom_call_target="tpu_custom_call" | custom-call | flops 2000000000 | tf_op jit(solution)/shard_map/plan/pallas_call | solution.py:647
  28.2 0.0 collective-permute-done.2.left.d_left
  28.2 1.6 %collective-permute-done.3.right.d_right = f32[360,128]{1,0:T(8,128)S(1)} collective-permute-done((f32[360,128]{1,0:T(8,128)S(1)}, f32[360,128]{1,0:T(8,128)S(1)}, u32[]{:S(2)}, u32[]{:S(2)}) %collective-permute-start.3) | collective-permute-done | bytes 184352 | tf_op jit(solution)/shard_map/ppermute | solution.py:622
  29.7 0.0 copy-done.2
  29.7 13.2 %pick.1.own = f32[8,8,512]{2,1,0:T(8,128)S(1)} custom-call(f32[360,128]{1,0:T(8,128)S(1)} %collective-permute-done.2.left.d_left, f32[288,128]{1,0:T(8,128)S(1)} %collective-permute-done.low.d_low, f32[192,128]{1,0:T(8,128)S(1)} %near.1, f32[288,128]{1,0:T(8,128)S(1)} %collective-permute-done.1.high.d_high, ...), custom_call_target="tpu_custom_call" | custom-call | flops 5600000000 | tf_op jit(solution)/shard_map/pick/pallas_call | solution.py:656
  42.9 0.0 copy-start.5
  42.9 1.4 %collective-permute-start.5 = (f32[5,8,512]{2,1,0:T(8,128)S(1)}, f32[5,8,512]{2,1,0:T(8,128)S(1)}, u32[]{:S(2)}, u32[]{:S(2)}) collective-permute-start(f32[5,8,512]{2,1,0:T(8,128)S(1)} %get-tuple-element.28), channel_id=1, source_target_pairs={{8,0},{16,8},{24,16},{9,1},{17,9},{25,17},{10,2},{18,10},{26,18},{... | collective-permute-start | bytes 245768 | tf_op jit(solution)/shard_map/ppermute | solution.py:622
  44.4 8.8 %collective-permute-start.4 = (f32[5,8,512]{2,1,0:T(8,128)S(1)}, f32[5,8,512]{2,1,0:T(8,128)S(1)}, u32[]{:S(2)}, u32[]{:S(2)}) collective-permute-start(f32[5,8,512]{2,1,0:T(8,128)S(1)} %get-tuple-element.29), channel_id=1, source_target_pairs={{0,8},{8,16},{16,24},{1,9},{9,17},{17,25},{2,10},{10,18},{18,26},{... | collective-permute-start | bytes 245768 | tf_op jit(solution)/shard_map/ppermute | solution.py:622
  53.2 0.0 collective-permute-done.5.high.p_high
  53.2 0.9 collective-permute-done.4.low.p_low
  54.1 0.1 pack.1
  54.1 2.4 %collective-permute-start.6 = (f32[360,128]{1,0:T(8,128)S(1)}, f32[360,128]{1,0:T(8,128)S(1)}, u32[]{:S(2)}, u32[]{:S(2)}) collective-permute-start(f32[360,128]{1,0:T(8,128)S(1)} %get-tuple-element.21), channel_id=1, source_target_pairs={{0,1},{1,2},{2,3},{3,4},{4,5},{5,6},{6,7},{8,9},{9,10},{10,11},{11... | collective-permute-start | bytes 552968 | tf_op jit(solution)/shard_map/ppermute | solution.py:622
  56.5 1.3 %collective-permute-start.7 = (f32[360,128]{1,0:T(8,128)S(1)}, f32[360,128]{1,0:T(8,128)S(1)}, u32[]{:S(2)}, u32[]{:S(2)}) collective-permute-start(f32[360,128]{1,0:T(8,128)S(1)} %get-tuple-element.22), channel_id=1, source_target_pairs={{1,0},{2,1},{3,2},{4,3},{5,4},{6,5},{7,6},{9,8},{10,9},{11,10},{12... | collective-permute-start | bytes 552968 | tf_op jit(solution)/shard_map/ppermute | solution.py:622
  57.9 0.1 stack.43.inside.place
  58.0 1.6 %collective-permute-done.6.p_left = f32[360,128]{1,0:T(8,128)S(1)} collective-permute-done((f32[360,128]{1,0:T(8,128)S(1)}, f32[360,128]{1,0:T(8,128)S(1)}, u32[]{:S(2)}, u32[]{:S(2)}) %collective-permute-start.6) | collective-permute-done | bytes 184352 | tf_op jit(solution)/shard_map/ppermute | solution.py:622
  59.6 6.8 %collective-permute-done.7.p_right = f32[360,128]{1,0:T(8,128)S(1)} collective-permute-done((f32[360,128]{1,0:T(8,128)S(1)}, f32[360,128]{1,0:T(8,128)S(1)}, u32[]{:S(2)}, u32[]{:S(2)}) %collective-permute-start.7) | collective-permute-done | bytes 184352 | tf_op jit(solution)/shard_map/ppermute | solution.py:622
  66.4 0.0 copy-done.5
  66.4 9.1 %krylov.1 = (f32[12,256,128]{2,1,0:T(8,128)S(1)}, f32[8,128]{1,0:T(8,128)S(1)}) custom-call(s32[6]{0:T(128)S(1)} %stack.43.inside.place, f32[8,8,512]{2,1,0:T(8,128)S(1)} %pick.1.own, f32[5,8,512]{2,1,0:T(8,128)S(1)} %collective-permute-done.4.low.p_low, f32[5,8,512]{2,1,0:T(8,128)S(1)} %collective-permute-done.5.high.p_high, ...), custom_call_target="tpu_custom_call" | custom-call | flops 2800000000 | tf_op jit(solution)/shard_map/krylov/pallas_call | solution.py:668
  75.4 4.3 %collective-permute-start.8 = (f32[8,128]{1,0:T(8,128)S(1)}, f32[8,128]{1,0:T(8,128)S(1)}, u32[]{:S(2)}, u32[]{:S(2)}) collective-permute-start(f32[8,128]{1,0:T(8,128)S(1)} %get-tuple-element.24), channel_id=1, source_target_pairs={{0,4},{1,5},{2,6},{3,7},{4,0},{5,1},{6,2},{7,3},{8,12},{9,13},{10,... | collective-permute-start | bytes 12296 | tf_op jit(solution)/shard_map/ppermute | solution.py:679
  79.8 5.3 %surface.1 = f32[120,128]{1,0:T(8,128)S(1)} custom-call(s32[1,9]{1,0:T(1,128)S(1)} %copy-done.9, f32[12,256,128]{2,1,0:T(8,128)S(1)} %get-tuple-element.23.basis, s32[9,1,128]{2,1,0:T(1,128)S(1)} %bitcast.18), custom_call_target="tpu_custom_call" | custom-call | flops 1600000000 | tf_op jit(solution)/shard_map/surface/pallas_call | solution.py:683
  85.0 0.0 copy-start.8
  85.0 0.0 collective-permute-done.8
  85.1 7.7 %all_gather.10.gathered = f32[4,120,128]{2,1,0:T(8,128)S(1)} all-gather(f32[1,120,128]{2,1,0:T(8,128)S(1)} %bitcast_dynamic-update-slice_fusion), channel_id=1, replica_groups=mesh['dom'=4,'slab'=8] {'dom'}, dimensions={0}, use_global_device_ids=true | all-gather | bytes 307200 | tf_op jit(solution)/shard_map/all_gather | solution.py:688
  92.8 0.6 route.1
  93.3 1.7 %collective-permute-start.9 = (f32[48,128]{1,0:T(8,128)S(1)}, f32[48,128]{1,0:T(8,128)S(1)}, u32[]{:S(2)}, u32[]{:S(2)}) collective-permute-start(f32[48,128]{1,0:T(8,128)S(1)} %get-tuple-element.26), channel_id=1, source_target_pairs={{0,1},{1,0},{2,3},{3,2},{4,5},{5,4},{6,7},{7,6},{8,9},{9,8},{10,11... | collective-permute-start | bytes 73736 | tf_op jit(solution)/shard_map/ppermute | solution.py:695
  95.0 2.2 %collective-permute-done.9.pair = f32[48,128]{1,0:T(8,128)S(1)} collective-permute-done((f32[48,128]{1,0:T(8,128)S(1)}, f32[48,128]{1,0:T(8,128)S(1)}, u32[]{:S(2)}, u32[]{:S(2)}) %collective-permute-start.9) | collective-permute-done | bytes 24608 | tf_op jit(solution)/shard_map/ppermute | solution.py:695
  97.2 2.2 %collective-permute-start.10 = (f32[48,128]{1,0:T(8,128)S(1)}, f32[48,128]{1,0:T(8,128)S(1)}, u32[]{:S(2)}, u32[]{:S(2)}) collective-permute-start(f32[48,128]{1,0:T(8,128)S(1)} %fusion.sent), channel_id=1, source_target_pairs={{0,7},{1,2},{2,1},{3,4},{4,3},{5,6},{6,5},{7,0},{8,15},{9,10},{10,... | collective-permute-start | bytes 73736 | tf_op jit(solution)/shard_map/ppermute | solution.py:698
  99.4 4.3 %collective-permute-done.10.other = f32[48,128]{1,0:T(8,128)S(1)} collective-permute-done((f32[48,128]{1,0:T(8,128)S(1)}, f32[48,128]{1,0:T(8,128)S(1)}, u32[]{:S(2)}, u32[]{:S(2)}) %collective-permute-start.10) | collective-permute-done | bytes 24608 | tf_op jit(solution)/shard_map/ppermute | solution.py:698
  103.7 0.0 copy-done.8
  103.7 2.6 %finish.1 = (f32[3,8,8,512]{3,2,1,0:T(8,128)}, f32[3,16384]{1,0:T(4,128)}) custom-call(s32[6]{0:T(128)S(1)} %stack.43.inside.place, f32[40,128]{1,0:T(8,128)S(1)} %get-tuple-element.25.keep, f32[48,128]{1,0:T(8,128)S(1)} %collective-permute-done.9.pair, f32[48,128]{1,0:T(8,128)S(1)} %fusion.sent, f32[48,128]{1,0:T(8,128)S(1)} %collective-permute-done.10.other, ...), custom_call_target="tpu_custom_call" | custom-call | flops 800000000 | tf_op jit(solution)/shard_map/finish/pallas_call | solution.py:699
  (9 shorter events, 0.0 us)
Async XLA Ops:
  0.6 1.0 copy-start.3
  1.6 0.9 copy-start.4
  2.5 0.8 copy-start.6
  10.4 7.4 %collective-permute-start = (f32[288,128]{1,0:T(8,128)S(1)}, f32[288,128]{1,0:T(8,128)S(1)}, u32[]{:S(2)}, u32[]{:S(2)}) collective-permute-start(f32[288,128]{1,0:T(8,128)S(1)} %get-tuple-element.15), channel_id=1, source_target_pairs={{0,8},{8,16},{16,24},{1,9},{9,17},{17,25},{2,10},{10,18},{18,26},{... | collective-permute-start | bytes 442376 | tf_op jit(solution)/shard_map/ppermute | solution.py:622
  12.8 10.8 %copy-start = (s32[4,8,8,512]{3,2,1,0:T(8,128)S(1)}, s32[4,8,8,512]{3,2,1,0:T(8,128)}, u32[]{:S(2)}) copy-start(s32[4,8,8,512]{3,2,1,0:T(8,128)} %shift.1) | copy-start | bytes 1572868
  12.8 10.8 %copy-start.1 = (s32[4,8,8,512]{3,2,1,0:T(8,128)S(1)}, s32[4,8,8,512]{3,2,1,0:T(8,128)}, u32[]{:S(2)}) copy-start(s32[4,8,8,512]{3,2,1,0:T(8,128)} %bucket.1) | copy-start | bytes 1572868
  12.9 5.5 %collective-permute-start.1 = (f32[288,128]{1,0:T(8,128)S(1)}, f32[288,128]{1,0:T(8,128)S(1)}, u32[]{:S(2)}, u32[]{:S(2)}) collective-permute-start(f32[288,128]{1,0:T(8,128)S(1)} %get-tuple-element.16), channel_id=1, source_target_pairs={{8,0},{16,8},{24,16},{9,1},{17,9},{25,17},{10,2},{18,10},{26,18},{... | collective-permute-start | bytes 442376 | tf_op jit(solution)/shard_map/ppermute | solution.py:622
  18.4 9.7 %collective-permute-start.2 = (f32[360,128]{1,0:T(8,128)S(1)}, f32[360,128]{1,0:T(8,128)S(1)}, u32[]{:S(2)}, u32[]{:S(2)}) collective-permute-start(f32[360,128]{1,0:T(8,128)S(1)} %get-tuple-element.17), channel_id=1, source_target_pairs={{0,1},{1,2},{2,3},{3,4},{4,5},{5,6},{6,7},{8,9},{9,10},{10,11},{11... | collective-permute-start | bytes 552968 | tf_op jit(solution)/shard_map/ppermute | solution.py:622
  22.1 7.6 %copy-start.2 = (f32[4,8,8,512]{3,2,1,0:T(8,128)S(1)}, f32[4,8,8,512]{3,2,1,0:T(8,128)}, u32[]{:S(2)}) copy-start(f32[4,8,8,512]{3,2,1,0:T(8,128)} %factor.1) | copy-start | bytes 1572868
  22.2 7.6 %collective-permute-start.3 = (f32[360,128]{1,0:T(8,128)S(1)}, f32[360,128]{1,0:T(8,128)S(1)}, u32[]{:S(2)}, u32[]{:S(2)}) collective-permute-start(f32[360,128]{1,0:T(8,128)S(1)} %get-tuple-element.18), channel_id=1, source_target_pairs={{1,0},{2,1},{3,2},{4,3},{5,4},{6,5},{7,6},{9,8},{10,9},{11,10},{12... | collective-permute-start | bytes 552968 | tf_op jit(solution)/shard_map/ppermute | solution.py:622
  42.9 23.5 %copy-start.5 = (f32[8,8,512]{2,1,0:T(8,128)S(1)}, f32[8,8,512]{2,1,0:T(8,128)}, u32[]{:S(2)}) copy-start(f32[8,8,512]{2,1,0:T(8,128)} %rigid.5) | copy-start | bytes 393220
  42.9 10.2 %collective-permute-start.5 = (f32[5,8,512]{2,1,0:T(8,128)S(1)}, f32[5,8,512]{2,1,0:T(8,128)S(1)}, u32[]{:S(2)}, u32[]{:S(2)}) collective-permute-start(f32[5,8,512]{2,1,0:T(8,128)S(1)} %get-tuple-element.28), channel_id=1, source_target_pairs={{8,0},{16,8},{24,16},{9,1},{17,9},{25,17},{10,2},{18,10},{26,18},{... | collective-permute-start | bytes 245768 | tf_op jit(solution)/shard_map/ppermute | solution.py:622
  44.4 9.7 %collective-permute-start.4 = (f32[5,8,512]{2,1,0:T(8,128)S(1)}, f32[5,8,512]{2,1,0:T(8,128)S(1)}, u32[]{:S(2)}, u32[]{:S(2)}) collective-permute-start(f32[5,8,512]{2,1,0:T(8,128)S(1)} %get-tuple-element.29), channel_id=1, source_target_pairs={{0,8},{8,16},{16,24},{1,9},{9,17},{17,25},{2,10},{10,18},{18,26},{... | collective-permute-start | bytes 245768 | tf_op jit(solution)/shard_map/ppermute | solution.py:622
  54.1 5.4 %collective-permute-start.6 = (f32[360,128]{1,0:T(8,128)S(1)}, f32[360,128]{1,0:T(8,128)S(1)}, u32[]{:S(2)}, u32[]{:S(2)}) collective-permute-start(f32[360,128]{1,0:T(8,128)S(1)} %get-tuple-element.21), channel_id=1, source_target_pairs={{0,1},{1,2},{2,3},{3,4},{4,5},{5,6},{6,7},{8,9},{9,10},{10,11},{11... | collective-permute-start | bytes 552968 | tf_op jit(solution)/shard_map/ppermute | solution.py:622
  56.5 9.8 %collective-permute-start.7 = (f32[360,128]{1,0:T(8,128)S(1)}, f32[360,128]{1,0:T(8,128)S(1)}, u32[]{:S(2)}, u32[]{:S(2)}) collective-permute-start(f32[360,128]{1,0:T(8,128)S(1)} %get-tuple-element.22), channel_id=1, source_target_pairs={{1,0},{2,1},{3,2},{4,3},{5,4},{6,5},{7,6},{9,8},{10,9},{11,10},{12... | collective-permute-start | bytes 552968 | tf_op jit(solution)/shard_map/ppermute | solution.py:622
  58.0 21.8 %copy-start.7 = (s32[1,3,3,128]{3,0,2,1:T(1,128)S(1)}, s32[1,3,3,128]{3,0,2,1:T(1,128)}, u32[]{:S(2)}) copy-start(s32[1,3,3,128]{3,0,2,1:T(1,128)} %param.15) | copy-start | bytes 13828
  58.0 21.8 %copy-start.9 = (s32[1,9]{1,0:T(1,128)S(1)}, s32[1,9]{1,0:T(1,128)}, u32[]{:S(2)}) copy-start(s32[1,9]{1,0:T(1,128)} %tally.1) | copy-start | bytes 112
  75.4 9.6 %collective-permute-start.8 = (f32[8,128]{1,0:T(8,128)S(1)}, f32[8,128]{1,0:T(8,128)S(1)}, u32[]{:S(2)}, u32[]{:S(2)}) collective-permute-start(f32[8,128]{1,0:T(8,128)S(1)} %get-tuple-element.24), channel_id=1, source_target_pairs={{0,4},{1,5},{2,6},{3,7},{4,0},{5,1},{6,2},{7,3},{8,12},{9,13},{10,... | collective-permute-start | bytes 12296 | tf_op jit(solution)/shard_map/ppermute | solution.py:679
  85.0 18.7 %copy-start.8 = (s32[1,3,3,128]{3,0,2,1:T(1,128)S(1)}, s32[1,3,3,128]{3,0,2,1:T(1,128)}, u32[]{:S(2)}) copy-start(s32[1,3,3,128]{3,0,2,1:T(1,128)} %param.17) | copy-start | bytes 13828
  93.3 3.9 %collective-permute-start.9 = (f32[48,128]{1,0:T(8,128)S(1)}, f32[48,128]{1,0:T(8,128)S(1)}, u32[]{:S(2)}, u32[]{:S(2)}) collective-permute-start(f32[48,128]{1,0:T(8,128)S(1)} %get-tuple-element.26), channel_id=1, source_target_pairs={{0,1},{1,0},{2,3},{3,2},{4,5},{5,4},{6,7},{7,6},{8,9},{9,8},{10,11... | collective-permute-start | bytes 73736 | tf_op jit(solution)/shard_map/ppermute | solution.py:695
  97.2 6.5 %collective-permute-start.10 = (f32[48,128]{1,0:T(8,128)S(1)}, f32[48,128]{1,0:T(8,128)S(1)}, u32[]{:S(2)}, u32[]{:S(2)}) collective-permute-start(f32[48,128]{1,0:T(8,128)S(1)} %fusion.sent), channel_id=1, source_target_pairs={{0,7},{1,2},{2,1},{3,4},{4,3},{5,6},{6,5},{7,0},{8,15},{9,10},{10,... | collective-permute-start | bytes 73736 | tf_op jit(solution)/shard_map/ppermute | solution.py:698

commit v3 on v2

v3 whole, which is shorter than its diff:
```python
import functools
import math

import jax
import jax.numpy as jnp
from jax import lax
from jax.experimental import pallas as pl
from jax.experimental.pallas import tpu as pltpu
from jax.sharding import PartitionSpec as P

ITERS = 4
COEF = 0.5
LANES = 128
CHUNK = 16
WEIGHT = 4e8
DEPART_MIB = 56
SUB = 8
CENTRE = 7.125
HALF = 6.875
REACH = ITERS + 1
VMEM = pl.BlockSpec(memory_space=pltpu.VMEM)
SMEM = pl.BlockSpec(memory_space=pltpu.SMEM)
HBM = pl.BlockSpec(memory_space=pltpu.HBM)


def params(mib):
    return pltpu.CompilerParams(vmem_limit_bytes=mib * 1024 * 1024)


def cost(micro, moved=0):
    return pl.CostEstimate(flops=int(micro * WEIGHT), bytes_accessed=moved, transcendentals=0)


def permute(value, lanes):
    return jnp.take_along_axis(value, lanes, axis=1, mode="promise_in_bounds")


def mix(values):
    tiles = len(values)
    lane = lax.broadcasted_iota(jnp.int32, values[0].shape, 1)
    share = LANES // tiles
    mixed = []
    for t in range(tiles):
        source = (lane * tiles + t) % LANES
        total = permute(values[0], source)
        for k in range(1, tiles):
            total = jnp.where(lane >= k * share, permute(values[k], source), total)
        mixed.append(total)
    return mixed


def unmix(values):
    tiles = len(values)
    lane = lax.broadcasted_iota(jnp.int32, values[0].shape, 1)
    share = LANES // tiles
    plain = []
    for k in range(tiles):
        source = k * share + lane // tiles
        total = permute(values[0], source)
        for t in range(1, tiles):
            total = jnp.where(lane % tiles == t, permute(values[t], source), total)
        plain.append(total)
    return plain


def wedge(nx, reach):
    rows, offset = [], 0
    for x in range(1 - reach, nx + reach - 1):
        width = reach - max(0, -x, x - nx + 1)
        rows.append((x, width, offset))
        offset += width
    return rows, offset


def lookup(table, first, rows, lanes, bits):
    if rows == 1:
        row = jnp.broadcast_to(table[pl.ds(first, 1), :], lanes.shape)
        return jnp.take_along_axis(row, lanes, axis=1, mode="promise_in_bounds")
    half = rows // 2
    lower = lookup(table, first, half, lanes, bits[:-1])
    upper = lookup(table, first + half, half, lanes, bits[:-1])
    return jnp.where(bits[-1], upper, lower)


def lookup_all(table, indices, chunk):
    rows = table.shape[0]
    depth = int(math.log2(chunk))
    lanes = [index & (LANES - 1) for index in indices]
    high = [index >> 7 for index in indices]
    outer = [value >> depth for value in high]

    def step(block, found):
        base = pl.multiple_of(block * chunk, chunk)
        fresh = []
        for lane, value, top, old in zip(lanes, high, outer, found):
            bits = [((value >> bit) & 1) == 1 for bit in range(depth)]
            fresh.append(jnp.where(top == block, lookup(table, base, chunk, lane, bits), old))
        return tuple(fresh)

    zero = jnp.zeros(indices[0].shape, jnp.float32)
    return lax.fori_loop(0, rows // chunk, step, tuple(zero for _ in indices))


def order2(a, b):
    if len(a) == 1:
        return (jnp.minimum(a[0], b[0]),), (jnp.maximum(a[0], b[0]),)
    swap = a[0] > b[0]
    low = [jnp.minimum(a[0], b[0])] + [jnp.where(swap, y, x) for x, y in zip(a[1:], b[1:])]
    high = [jnp.maximum(a[0], b[0])] + [jnp.where(swap, x, y) for x, y in zip(a[1:], b[1:])]
    return tuple(low), tuple(high)


def sublane_xor(value, mask):
    sub = lax.broadcasted_iota(jnp.int32, value.shape, 0)
    return jnp.take_along_axis(value, sub ^ mask, axis=0, mode="promise_in_bounds")


def keep_one(a, other, lower):
    if len(a) == 1:
        return (jnp.where(lower, jnp.minimum(a[0], other[0]), jnp.maximum(a[0], other[0])),)
    take = (a[0] > other[0]) == lower
    return tuple(jnp.where(take, y, x) for x, y in zip(a, other))


def sort_rows(refs, block, done=0, until=None):
    count = refs[0].shape[0] // SUB

    def load(v):
        at = pl.ds(pl.multiple_of(v * SUB, SUB), SUB)
        return tuple(r[at, :] for r in refs)

    def store(v, value):
        at = pl.ds(pl.multiple_of(v * SUB, SUB), SUB)
        for r, x in zip(refs, value): r[at, :] = x

    def strides(held, stride):
        while stride:
            for i in range(len(held)):
                if not i & stride:
                    held[i], held[i | stride] = order2(held[i], held[i | stride])
            stride //= 2

    def whole(t, carry):
        held = [load(t * block + i) for i in range(block)]
        size = 2
        while size <= block:
            for i in range(block):
                j = i ^ (size - 1)
                if i < j: held[i], held[j] = order2(held[i], held[j])
            strides(held, size // 4)
            size *= 2
        for i in range(block): store(t * block + i, held[i])
        return carry

    def finish(t, carry):
        held = [load(t * block + i) for i in range(block)]
        strides(held, block // 2)
        for i in range(block): store(t * block + i, held[i])
        return carry

    if not done:
        lax.fori_loop(0, count // block, whole, 0)
    size = 2 * max(done, block)
    while size <= (until or count * SUB):
        span = min(size, count)
        flip = size // count - 1 if size > count else 0
        groups = span // block

        def top(t, carry):
            base = (t // (block // 2)) * span
            i = t % (block // 2)
            spots = []
            for j in range(groups):
                spots += [base + i + block * j, base + block - 1 - i + block * j]
            held = [load(v) for v in spots]
            n = len(held)
            if flip:
                sub = lax.broadcasted_iota(jnp.int32, (SUB, LANES), 0)
                lower = (sub & ((flip + 1) // 2)) == 0
                turned = [tuple(sublane_xor(x, flip) for x in h) for h in held]
                held = [keep_one(held[k], turned[n - 1 - k], lower) for k in range(n)]
                bit = (flip + 1) // 4
                while bit:
                    lower = (sub & bit) == 0
                    held = [keep_one(h, tuple(sublane_xor(x, bit) for x in h), lower) for h in held]
                    bit //= 2
                far = groups // 2
            else:
                for k in range(n // 2):
                    held[k], held[n - 1 - k] = order2(held[k], held[n - 1 - k])
                far = groups // 4
            while far:
                for j in range(groups):
                    if not j & far:
                        for side in range(2):
                            x, y = 2 * j + side, 2 * (j | far) + side
                            held[x], held[y] = order2(held[x], held[y])
                far //= 2
            for v, h in zip(spots, held): store(v, h)
            return carry

        lax.fori_loop(0, (count // span) * (block // 2), top, 0, unroll=max(1, 8 // groups))
        lax.fori_loop(0, count // block, finish, 0)
        size *= 2


def blocks_of(place):
    kinds = 1 + place[0] + place[1]
    return kinds, 1 - place[0], 2 - place[4], 1 + place[4]


def plan_kernel(per, place, shift, bucket, keys):
    kinds, first, left, right = blocks_of(place)
    corners, nx, _, nz = shift.shape
    tiles = nz // LANES
    count = corners * nx * tiles
    sub = lax.broadcasted_iota(jnp.int32, (SUB, LANES), 0)

    def build(x, carry):
        for c in range(corners):
            for t in range(tiles):
                at = pl.ds(t * LANES, LANES)
                way = shift[c, x, :, at]
                a = (way * 11) >> 5
                b = way - 3 * a
                block = jnp.where(b == 1, 0, jnp.where(b == 0, left * kinds, right * kinds)) + (a - first)
                flat = block * (per * LANES) + bucket[c, x, :, at]
                if c:
                    flat = pltpu.roll(flat, c * (LANES // corners), axis=1)
                v = (c * nx + x) * tiles + t
                keys[pl.ds(pl.multiple_of(v * SUB, SUB), SUB), :] = flat * (count * SUB) + (sub * count + v)
        return carry

    lax.fori_loop(0, nx, build, 0)
    sort_rows([keys], 32, until=count)


def order_kernel(per, place, begun, keys, bounds):
    keys[...] = begun[...]
    count = keys.shape[0] // SUB
    sort_rows([keys], 32, done=count)
    low_bits = int(math.log2(count * SUB * LANES))
    lane = lax.broadcasted_iota(jnp.int32, (SUB, LANES), 1)
    base = jnp.zeros((SUB, LANES), jnp.float32)
    width = jnp.zeros((SUB, 1), jnp.float32)
    top = jnp.zeros((SUB, 1), jnp.float32)
    for g in range(count // SUB):
        least = (keys[pl.ds(g * SUB * SUB, SUB), :] >> low_bits).astype(jnp.float32)
        most = (keys[pl.ds(g * SUB * SUB + SUB * (SUB - 1), SUB), :] >> low_bits).astype(jnp.float32)
        least = jnp.min(least, axis=1, keepdims=True)
        most = jnp.max(most, axis=1, keepdims=True)
        base = jnp.where(lane == g, least, base)
        width = jnp.maximum(width, most - least + 1.0)
        top = jnp.maximum(top, most)
    trips = (width.astype(jnp.int32) + (CHUNK - 1)) // CHUNK
    ready = 2 * blocks_of(place)[0] * per
    rows = jnp.where(top.astype(jnp.int32) < ready, ready, 9 * per)
    start = jnp.minimum(base.astype(jnp.int32), rows - trips * CHUNK)
    latest = jnp.max(jnp.where(lane < count // SUB, start, 0).astype(jnp.float32), axis=1, keepdims=True)
    soon = jnp.clip((ready - latest.astype(jnp.int32)) // CHUNK, 0, trips)
    bounds[...] = jnp.where(lane == LANES - 1, trips, jnp.where(lane == LANES - 2, soon, start))


def visit(table, keys, bounds, soon, before, store):
    count = keys.shape[0] // SUB
    pos_bits = int(math.log2(count * SUB))
    depth = int(math.log2(CHUNK))
    per = count // SUB

    def body(s, carry):
        own = [keys[pl.ds(SUB * SUB * g + s, SUB, stride=SUB), :] for g in range(per)]
        start = [bounds[s, g] for g in range(per)]

        def step(n, found):
            fresh = []
            for g in range(per):
                lanes = (own[g] >> pos_bits) & (LANES - 1)
                first = start[g] + n * CHUNK
                rel = (own[g] >> (pos_bits + 7)) - first
                bits = [((rel >> b) & 1) == 1 for b in range(depth)]
                fresh.append(jnp.where((rel >> depth) == 0, lookup(table, first, CHUNK, lanes, bits), found[g]))
            return tuple(fresh)

        spots = [pl.ds(SUB * SUB * g + s, SUB, stride=SUB) for g in range(per)]
        least = 0 if soon else bounds[s, LANES - 2]
        most = bounds[s, LANES - 2 if soon else LANES - 1]
        found = lax.fori_loop(least, most, step, tuple(before(at) for at in spots))
        for g, at in enumerate(spots):
            store(at, found[g], own[g] & (count * SUB - 1))
        return carry

    lax.fori_loop(0, SUB, body, 0)


def slots_of(heat, picks, first, out, rows):
    group = SUB * SUB

    def body(g, carry):
        base = pl.multiple_of(g * group, group)
        found = lookup_all(heat, [picks[pl.ds(first + base + SUB * k, SUB), :] for k in range(SUB)], heat.shape[0])
        for k in range(SUB):
            out[pl.ds(base + SUB * k, SUB), :] = found[k]
        return carry

    lax.fori_loop(0, rows // group, body, 0)


def depart_kernel(heat_hbm, picks_hbm, rigid_hbm, up, mixed, heat, picks, rigid, arrived):
    rows = picks.shape[0]
    sources = (rigid_hbm, heat_hbm, picks_hbm.at[pl.ds(picks_hbm.shape[0] - rows, rows), :])
    copies = [
        pltpu.make_async_copy(source, target, arrived.at[k])
        for k, (source, target) in enumerate(zip(sources, (rigid, heat, picks)))
    ]
    for copy in copies:
        copy.start()
    nx, _, nz = rigid.shape
    tiles = nz // LANES
    narrow = REACH - 2
    copies[0].wait()
    for x in range(nx):
        values = mix([rigid[x, :, pl.ds(t * LANES, LANES)] for t in range(tiles)])
        for t in range(tiles):
            mixed[x, pl.ds(t * SUB, SUB), :] = values[t]
            if x >= nx - narrow:
                up[pl.ds(rows + ((x - nx + narrow) * tiles + t) * SUB, SUB), :] = values[t]
    copies[1].wait()
    copies[2].wait()
    slots_of(heat, picks, 0, up, rows)


def depart_down_kernel(heat, picks, mixed, down):
    narrow = REACH - 2
    tall = mixed.shape[1]
    rows = down.shape[0] - narrow * tall
    for x in range(narrow):
        down[pl.ds(rows + x * tall, tall), :] = mixed[x]
    slots_of(heat, picks, 0, down, rows)


def near_kernel(heat, picks, near):
    slots_of(heat, picks, near.shape[0], near, near.shape[0])


def forward_kernel(place, low, near, high, rigid, pair, other):
    nx, ny = rigid.shape[0], SUB
    per = near.shape[0] // 3
    tiles = rigid.shape[1] // SUB
    odd = place[4] == 1
    rows, size = wedge(nx, REACH - 2)

    def give(to, up, down):
        pair[to, :] = jnp.where(odd, down, up)
        other[to, :] = jnp.where(odd, up, down)

    for a, ref in enumerate((low, near, high)):
        give(pl.ds(a * per, per), ref[pl.ds(2 * per, per), :], ref[pl.ds(0, per), :])
    for t in range(tiles):
        for x, width, offset in rows:
            to = pl.ds(3 * per + t * size + offset, width)
            if 0 <= x < nx:
                base = t * SUB
                give(to, rigid[x, pl.ds(base + ny - width, width), :], rigid[x, pl.ds(base, width), :])
            else:
                ref, k = (low, x + REACH - 2) if x < 0 else (high, x - nx)
                base = 3 * per + (k * tiles + t) * SUB
                give(to, ref[pl.ds(base + ny - width, width), :], ref[pl.ds(base, width), :])


def lay(table, per, place, columns):
    kinds, first = blocks_of(place)[:2]
    for valid, column, readers in columns:
        for a, read in enumerate(readers):
            here = valid if a == 1 else jnp.logical_and(valid, place[0 if a == 0 else 1] == 1)

            @pl.when(here)
            def _():
                row = pl.multiple_of((column * kinds + a - first) * per, per)
                table[pl.ds(row, per), :] = read()


def early_kernel(place, pair, low, near, high, keys, bounds, value, table):
    per = near.shape[0] // 3
    own = [lambda ref=ref: ref[pl.ds(per, per), :] for ref in (low, near, high)]
    side = [lambda at=pl.ds(a * per, per): pair[at, :] for a in range(3)]
    lay(table, per, place, [(place[0] >= 0, 0, own), (place[0] >= 0, 1, side)])

    def store(at, found, spot):
        value[at, :] = found

    visit(table, keys, bounds, True, lambda at: jnp.zeros((SUB, LANES), jnp.float32), store)


def pick_kernel(place, pair, other, low, near, high, keys, early, bounds, factor, out, table, position, value):
    odd = place[4] == 1
    corners, nx, _, nz = factor.shape
    tiles = nz // LANES
    slots = near.shape[0] // 3
    own = [lambda ref=ref: ref[pl.ds(slots, slots), :] for ref in (low, near, high)]

    def side(even_ref, odd_ref):
        return [lambda at=pl.ds(a * slots, slots): jnp.where(odd, odd_ref[at, :], even_ref[at, :]) for a in range(3)]

    _, _, left, right = blocks_of(place)
    lay(table, slots, place, [(place[0] >= 0, 0, own), (place[2] == 1, left, side(other, pair)),
                              (place[3] == 1, right, side(pair, other))])

    def store(at, found, spot):
        value[at, :] = found
        position[at, :] = spot

    visit(table, keys, bounds, False, lambda at: early[at, :], store)
    sort_rows([position, value], 16)

    def blend(x, carry):
        blended = []
        for t in range(tiles):
            at = pl.ds(t * LANES, LANES)
            total = None
            for c in range(corners):
                v = (c * nx + x) * tiles + t
                got = value[pl.ds(pl.multiple_of(v * SUB, SUB), SUB), :]
                if c:
                    got = pltpu.roll(got, LANES - c * (LANES // corners), axis=1)
                got = factor[c, x, :, at] * got
                total = got if total is None else total + got
            blended.append(total)
        for t, total in enumerate(mix(blended)):
            out[x, pl.ds(t * SUB, SUB), :] = total
        return carry

    lax.fori_loop(0, nx, blend, 0)


def pack_kernel(place, low, own, high, pair, other):
    nx, ny = own.shape[0], SUB
    tiles = own.shape[1] // SUB
    odd = place[4] == 1
    rows, size = wedge(nx, REACH)
    for t in range(tiles):
        for x, width, offset in rows:
            ref, k = (own, x) if 0 <= x < nx else (low, x + REACH) if x < 0 else (high, x - nx)
            up = ref[k, pl.ds(t * SUB + ny - width, width), :]
            down = ref[k, pl.ds(t * SUB, width), :]
            to = pl.ds(t * size + offset, width)
            pair[to, :] = jnp.where(odd, down, up)
            other[to, :] = jnp.where(odd, up, down)


def unpack(target, reach, own, dom_low, dom_high, pair, other, offset, odd, change):
    nx = own.shape[0]
    tiles = own.shape[1] // SUB
    rows, size = wedge(nx, reach)
    for t in range(tiles):
        for x in range(-reach, nx + reach):
            if 0 <= x < nx:
                mine = own[x, pl.ds(t * SUB, SUB), :]
            else:
                mine = dom_low(x + reach, t) if x < 0 else dom_high(x - nx, t)
            target[t, REACH + x, pl.ds(SUB, SUB), :] = change(mine, REACH + x, 1)
        for x, width, row in rows:
            at = pl.ds(offset + t * size + row, width)
            even_low, odd_low = other[at, :], pair[at, :]
            target[t, REACH + x, pl.ds(SUB - width, width), :] = change(jnp.where(odd, odd_low, even_low), REACH + x, 0)
            target[t, REACH + x, pl.ds(2 * SUB, width), :] = change(jnp.where(odd, even_low, odd_low), REACH + x, 2)


def krylov_kernel(inside, own, p_low, p_high, p_pair, p_other, rigid, d_low, d_high, d_pair, d_other,
                  basis, sums, temp, diag, u0, u1, u2, u3):
    nx = own.shape[0]
    tiles = own.shape[1] // SUB
    parts = temp.shape[2] // SUB
    held = (u0, u1, u2, u3)
    flag = [inside[k].astype(jnp.float32) for k in range(4)]

    def mask(x, part):
        at_x = jnp.where(x < REACH, flag[0], jnp.where(x >= REACH + nx, flag[1], 1.0))
        return at_x * (flag[2] if part == 0 else flag[3] if part == 2 else 1.0)

    temp[...] = jnp.zeros_like(temp)
    odd = inside[4] == 1
    base = d_pair.shape[0] - tiles * wedge(nx, REACH - 2)[1]
    first_d = d_low.shape[0] - tiles * SUB * (REACH - 2)

    def plane(ref):
        return lambda x, t: ref[x, pl.ds(t * SUB, SUB), :]

    def message(ref):
        return lambda x, t: ref[pl.ds(first_d + (x * tiles + t) * SUB, SUB), :]

    unpack(temp, REACH, own, plane(p_low), plane(p_high), p_pair, p_other, 0, odd, lambda v, x, part: v)
    diag[...] = jnp.zeros_like(diag)
    unpack(diag, REACH - 2, rigid, message(d_low), message(d_high), d_pair, d_other, base, odd,
           lambda v, x, part: (v * (2.0 / HALF) + 2.0 * (6.0 - CENTRE) / HALF) * mask(x, part))
    lane = lax.broadcasted_iota(jnp.int32, (SUB, LANES), 1)
    first, last = lane == 0, lane == LANES - 1
    zero = jnp.zeros((SUB, LANES), jnp.float32)

    def around_z(values):
        back = jnp.where(first, zero, pltpu.roll(values[-1], 1, axis=1))
        ahead = jnp.where(last, zero, pltpu.roll(values[0], LANES - 1, axis=1))
        return [(values[t - 1] if t else back, values[t + 1] if t + 1 < tiles else ahead) for t in range(tiles)]

    def around_y(ref, head, x, part):
        base = part * SUB
        mine = ref[(*head, x, pl.ds(base, SUB))]
        below = pltpu.roll(mine, 1, axis=0) if part == 0 else ref[(*head, x, pl.ds(base - 1, SUB))]
        above = pltpu.roll(mine, SUB - 1, axis=0) if part == parts - 1 else ref[(*head, x, pl.ds(base + 1, SUB))]
        return mine, below, above

    def load_row(x, carry):
        for part in range(parts):
            scale = COEF * mask(x, part)
            rows = [around_y(temp, (t,), x, part) for t in range(tiles)]
            along = around_z([r[0] for r in rows])
            for t in range(tiles):
                ahead = temp[t, x + 1, pl.ds(part * SUB, SUB), :]
                back = temp[t, x - 1, pl.ds(part * SUB, SUB), :]
                u0[0, t, x, pl.ds(part * SUB, SUB), :] = scale * (ahead - back)
                u0[1, t, x, pl.ds(part * SUB, SUB), :] = scale * (rows[t][2] - rows[t][1])
                u0[2, t, x, pl.ds(part * SUB, SUB), :] = scale * (along[t][1] - along[t][0])
        return carry

    lax.fori_loop(1, nx + 2 * REACH - 1, load_row, 0)

    def twice(ref, c, x, part):
        coefficient = (2.0 / HALF) * mask(x, part)
        rows = [around_y(ref, (c, t), x, part) for t in range(tiles)]
        along = around_z([r[0] for r in rows])
        results = []
        for t in range(tiles):
            near = rows[t][1] + rows[t][2] + along[t][0] + along[t][1]
            near = near + ref[c, t, x + 1, pl.ds(part * SUB, SUB), :] + ref[c, t, x - 1, pl.ds(part * SUB, SUB), :]
            results.append(diag[t, x, pl.ds(part * SUB, SUB), :] * rows[t][0] - coefficient * near)
        return results, [r[0] for r in rows]

    for order in range(1, ITERS):
        source, target = held[order - 1], held[order]

        def apply_row(x, carry):
            for c in range(3):
                for part in range(parts):
                    doubled, _ = twice(source, c, x, part)
                    for t in range(tiles):
                        at = (c, t, x, pl.ds(part * SUB, SUB))
                        if order == 1:
                            target[at] = 0.5 * doubled[t]
                        else:
                            target[at] = doubled[t] - held[order - 2][at]
            return carry

        margin = ITERS - order
        lax.fori_loop(REACH - margin, REACH + nx + margin, apply_row, 0)

    def dots_row(x, carry):
        carry = list(carry)
        for c in range(3):
            doubled, u = twice(u3, c, REACH + x, 1)
            for t in range(tiles):
                at = (c, t, REACH + x, pl.ds(SUB, SUB))
                v = [u0[at], u1[at], u2[at], u[t]]
                pairs = [(v[0], v[0]), (v[0], v[1]), (v[1], v[1]), (v[1], v[2]), (v[2], v[2]), (v[2], v[3]),
                         (v[3], v[3]), (v[3], doubled[t])]
                for k, (left, right) in enumerate(pairs):
                    carry[k] = carry[k] + left * right
                for j in range(4):
                    basis[3 * j + c, pl.ds(pl.multiple_of(t * nx * SUB + x * SUB, SUB), SUB), :] = v[j]
        return tuple(carry)

    totals = lax.fori_loop(0, nx, dots_row, tuple(zero for _ in range(8)))
    for k in range(8):
        sums[pl.ds(k, 1), :] = jnp.sum(totals[k], axis=0, keepdims=True)


def surface_kernel(nz, tally, place, basis, picks, keep, pair, other, index, live):
    fields, rows, _ = basis.shape
    count = picks.shape[0]
    tiles = nz // LANES
    block = rows // tiles
    odd = place[6] == 1
    lane = lax.broadcasted_iota(jnp.int32, (1, LANES), 1)
    sub = lax.broadcasted_iota(jnp.int32, (SUB, LANES), 0)
    for k in range(count):
        spot = picks[k]
        along = spot % nz
        index[pl.ds(k, 1), :] = ((along % tiles) * block + spot // nz) * LANES + along // tiles
        live[pl.ds(k, 1), :] = (lane < tally[0, k]).astype(jnp.float32)

    def give(f, values):
        for b in range(3):
            keep[pl.ds(b * fields + f, 1), :] = values[3 + b]
            to = pl.ds(SUB + b * fields + f, 1)
            pair[to, :] = jnp.where(odd, values[b], values[6 + b])
            other[to, :] = jnp.where(odd, values[6 + b], values[b])

    depth = int(math.log2(rows))

    def body(f, carry):
        table = basis.at[f]
        spots = index[pl.ds(0, SUB), :]
        high = spots >> 7
        bits = [((high >> bit) & 1) == 1 for bit in range(depth)]
        found = lookup(table, 0, rows, spots & (LANES - 1), bits)
        found = jnp.where(live[pl.ds(0, SUB), :] > 0.5, found, 0.0)
        values = [found[k : k + 1, :] for k in range(SUB)]
        for k in range(SUB, count):
            spots = jnp.broadcast_to(index[pl.ds(k, 1), :], (SUB, LANES))
            lanes, high = spots & (LANES - 1), spots >> 7
            total = jnp.zeros((SUB, LANES), jnp.float32)
            for g in range(0, rows, SUB):
                got = jnp.take_along_axis(table[pl.ds(g, SUB), :], lanes, axis=1, mode="promise_in_bounds")
                total = jnp.where(high == sub + g, got, total)
            total = jnp.sum(total, axis=0, keepdims=True)
            total = jnp.where(live[pl.ds(k, 1), :] > 0.5, total, 0.0)
            values.append(total)
        give(f, values)
        return carry

    lax.fori_loop(0, fields, body, 0)


def route_kernel(place, kept, pair_in, sent, other_in, keep, pair, other):
    fields = 3 * ITERS
    pair[pl.ds(0, SUB), :] = sent[pl.ds(0, SUB), :] + other_in[pl.ds(0, SUB), :]
    odd, odd_dom = place[4] == 1, place[6] == 1
    for b in range(3):
        at = pl.ds(SUB + b * fields, fields)
        one, two = pair_in[at, :], other_in[at, :]
        low = jnp.where(odd_dom, one, two) * place[0].astype(jnp.float32)
        high = jnp.where(odd_dom, two, one) * place[1].astype(jnp.float32)
        for a, rows in ((0, low), (1, kept[pl.ds(b * fields, fields), :]), (2, high)):
            if b == 1:
                keep[pl.ds(a * fields, fields), :] = rows
            else:
                to = pl.ds(SUB + a * fields, fields)
                chosen = odd if b == 0 else jnp.logical_not(odd)

                @pl.when(chosen)
                def _():
                    pair[to, :] = rows

                @pl.when(jnp.logical_not(chosen))
                def _():
                    other[to, :] = rows


def coefficients(nu):
    half = 0.5

    def gram(i, j):
        return half * (nu[i + j] + nu[abs(i - j)])

    def inner(i, j):
        if j == 0:
            return gram(i, 1)
        return half * (gram(i, j + 1) + gram(i, j - 1))

    def form(vector, matrix):
        n = len(vector)
        total = None
        for i in range(n):
            for j in range(i, n):
                term = vector[i] * vector[j] * matrix(i, j)
                term = term if i == j else 2.0 * term
                total = term if total is None else total + term
        return total

    one = jnp.ones_like(nu[0])
    found, residual, direction = [], [one], [one]
    rr = nu[0]
    for iteration in range(ITERS):
        energy = form(direction, lambda i, j: CENTRE * gram(i, j) + HALF * inner(i, j))
        alpha = rr / energy
        found = [
            (found[i] if i < len(found) else 0.0) + alpha * direction[i] for i in range(len(direction))
        ]
        if iteration + 1 == ITERS:
            break
        image = [CENTRE * d for d in direction] + [jnp.zeros_like(one)]
        for j, d in enumerate(direction):
            if j == 0:
                image[1] = image[1] + HALF * d
            else:
                image[j + 1] = image[j + 1] + half * HALF * d
                image[j - 1] = image[j - 1] + half * HALF * d
        residual = residual + [jnp.zeros_like(one)]
        residual = [r - alpha * w for r, w in zip(residual, image)]
        fresh = form(residual, gram)
        ratio = fresh / rr
        direction = direction + [jnp.zeros_like(one)]
        direction = [r + ratio * d for r, d in zip(residual, direction)]
        rr = fresh
    return found


def hot_kernel(picks, row_hot, lane_hot):
    count = picks.shape[0]
    place = lax.broadcasted_iota(jnp.int32, lane_hot.shape[1:], 0)
    tall = lax.broadcasted_iota(jnp.int32, row_hot.shape[1:], 0)
    for k in range(count):
        spot = picks[k]
        lane_hot[k] = (place == spot % LANES).astype(jnp.float32).astype(jnp.bfloat16)
        row_hot[k] = (tall == spot // LANES).astype(jnp.float32).astype(jnp.bfloat16)


def finish_kernel(place, keep, pair, sent, other, basis, row_hot, lane_hot, disp_hbm, thermal_hbm, disp, thermal, shift,
                  left):
    sums = sent[pl.ds(0, SUB), :] + other[pl.ds(0, SUB), :]
    raw = [jnp.broadcast_to(jnp.sum(sums[k : k + 1, :], axis=1, keepdims=True), (1, LANES)) for k in range(8)]
    nu = [raw[0], raw[1]]
    for k in range(2, 7):
        nu.append(2.0 * raw[k] - raw[k % 2])
    nu.append(2.0 * raw[7] - nu[5] - 2.0 * raw[1])
    weights = coefficients(nu)
    wide = [jnp.broadcast_to(w, (SUB, LANES)) for w in weights]
    _, nx, _, nz = disp.shape
    tiles = nz // LANES
    depth = thermal.shape[1] // LANES
    fields = 3 * ITERS
    total = jnp.zeros((9 * depth, LANES), jnp.float32)
    odd = place[4]
    blocks = []
    for ref, offset, b, here in (
        (keep, 0, 1, 1),
        (pair, SUB, 2 - 2 * odd, jnp.where(odd == 1, place[2], place[3])),
        (other, SUB, 2 * odd, jnp.where(odd == 1, place[3], place[2])),
    ):
        valid = jnp.full((1, LANES), here, jnp.int32) == 1
        for a in range(3):
            pieces = []
            for c in range(3):
                value = None
                for j in range(ITERS):
                    term = weights[j] * ref[pl.ds(offset + a * fields + 3 * j + c, 1), :]
                    value = term if value is None else value + term
                value = jnp.where(valid, value, 0.0)
                for _ in range(3):
                    part = value.astype(jnp.bfloat16)
                    value = value - part.astype(jnp.float32)
                    pieces.append(row_hot[3 * a + b] * jnp.broadcast_to(part, (depth, LANES)))
            blocks.append((jnp.concatenate(pieces, axis=0), lane_hot[3 * a + b]))
            if len(blocks) == 2 or (ref is other and a == 2):
                wanted = jnp.concatenate([p for p, _ in blocks], axis=1)
                hot = jnp.concatenate([h for _, h in blocks], axis=1)
                total = total + lax.dot_general(wanted, hot, (((1,), (1,)), ((), ())),
                                                preferred_element_type=jnp.float32)
                blocks = []
    for c in range(3):
        whole = total[3 * c * depth : (3 * c + 1) * depth]
        whole = whole + total[(3 * c + 1) * depth : (3 * c + 2) * depth]
        shift[...] = whole + total[(3 * c + 2) * depth : (3 * c + 3) * depth]
        for r in range(depth):
            thermal[pl.ds(c, 1), pl.ds(r * LANES, LANES)] = shift[pl.ds(r, 1), :]
    copies = [pltpu.make_async_copy(thermal, thermal_hbm, left.at[0])]
    copies[0].start()

    def row(x, carry):
        for c in range(3):
            totals = []
            for t in range(tiles):
                at = pl.ds(pl.multiple_of(t * nx * SUB + x * SUB, SUB), SUB)
                total = wide[0] * basis[c, at, :]
                for j in range(1, 4):
                    total = total + wide[j] * basis[3 * j + c, at, :]
                totals.append(total)
            for t, total in enumerate(unmix(totals)):
                disp[c, x, :, pl.ds(t * LANES, LANES)] = total
        return carry

    half = nx // 2
    for k in range(2):
        at = pl.ds(k * half, half)
        lax.fori_loop(k * half, (k + 1) * half, row, 0)
        copies.append(pltpu.make_async_copy(disp.at[:, at], disp_hbm.at[:, at], left.at[1 + k]))
        copies[-1].start()
    for copy in copies:
        copy.wait()


def swap(last, leading, axis):
    peers = lax.axis_size(axis)
    up = [(i, i + 1) for i in range(peers - 1)]
    down = [(j, i) for i, j in up]
    return lax.ppermute(last, axis, up), lax.ppermute(leading, axis, down)


def after(value, *others):
    return lax.optimization_barrier((value, *others))[0]


def even_odd(axis):
    return [(i, i ^ 1) for i in range(lax.axis_size(axis))]


def odd_even(axis, around):
    peers = lax.axis_size(axis)
    pairs = [(i, i + 1 if i % 2 else i - 1) for i in range(peers)]
    return [(i, j % peers) for i, j in pairs if around or 0 <= j < peers]


def exchange(pair, other, axis):
    return lax.ppermute(pair, axis, even_odd(axis)), lax.ppermute(other, axis, odd_even(axis, False))


def far_hops(sums, axis):
    peers = lax.axis_size(axis)
    hop = peers // 2
    while hop >= 4:
        sums = sums + lax.ppermute(sums, axis, [(i, (i + hop) % peers) for i in range(peers)])
        hop //= 2
    return sums


def pair_hops(sums, pair, other, axis):
    pair = pair if sums is None else lax.dynamic_update_slice(pair, sums, (0, 0))
    pair_in = lax.ppermute(pair, axis, even_odd(axis))
    sent = lax.dynamic_update_slice(other, pair[:SUB] + pair_in[:SUB], (0, 0))
    return pair_in, sent, lax.ppermute(sent, axis, odd_even(axis, True))


def on_device(heat_level, emitting, holder, bucket, factors, rigidity, boundary, tally, accepting):
    f32, i32 = jnp.float32, jnp.int32
    ways = emitting.shape[1]
    per = emitting.shape[3] // LANES
    nx, ny, nz = rigidity.shape
    tiles = nz // LANES
    narrow = REACH - 2
    call = pl.pallas_call
    shape = jax.ShapeDtypeStruct
    dom, slab = lax.axis_index("dom"), lax.axis_index("slab")
    place = jnp.stack([dom > 0, dom < lax.axis_size("dom") - 1, slab > 0, slab < lax.axis_size("slab") - 1,
                       slab % 2, dom, dom % 2]).astype(i32)
    heat = heat_level.reshape(-1, LANES)
    emit_rows = emitting.reshape(-1, LANES)
    dom_message = shape((ways * per + narrow * tiles * ny, LANES), f32)
    third = shape((ways * per, LANES), i32)
    up, mixed = call(
        depart_kernel, out_shape=(dom_message, shape((nx, tiles * ny, LANES), f32)), in_specs=[HBM] * 3,
        out_specs=(VMEM,) * 2,
        scratch_shapes=[pltpu.VMEM(heat.shape, f32), pltpu.VMEM(third.shape, i32), pltpu.VMEM(rigidity.shape, f32),
                        pltpu.SemaphoreType.DMA((3,))],
        compiler_params=params(DEPART_MIB), cost_estimate=cost(5), name="depart",
    )(heat, emit_rows, rigidity)
    pairs_up = [(i, i + 1) for i in range(lax.axis_size("dom") - 1)]
    from_low = lax.ppermute(up, "dom", pairs_up)
    down = call(depart_down_kernel, out_shape=dom_message, in_specs=[VMEM] * 3, out_specs=VMEM,
                compiler_params=params(4), cost_estimate=cost(4), name="down")(heat, emit_rows, mixed)
    from_high = lax.ppermute(down, "dom", [(j, i) for i, j in pairs_up])
    near = call(near_kernel, out_shape=shape((ways * per, LANES), f32), in_specs=[VMEM] * 2, out_specs=VMEM,
                compiler_params=params(4), cost_estimate=cost(4), name="near")(after(heat, down), emit_rows)
    count = holder.size // LANES
    rows = ways * ways * per
    begun = call(
        functools.partial(plan_kernel, per), out_shape=shape((count, LANES), i32), in_specs=[SMEM, VMEM, VMEM],
        out_specs=VMEM,
        compiler_params=params(6), cost_estimate=cost(3), name="plan",
    )(place, after(holder, near), bucket)
    slab_message = shape((ways * per + tiles * wedge(nx, narrow)[1], LANES), f32)
    pair, other = call(
        forward_kernel, out_shape=(slab_message,) * 2, in_specs=[SMEM] + [VMEM] * 4, out_specs=(VMEM,) * 2,
        compiler_params=params(6), cost_estimate=cost(1), name="forward",
    )(place, from_low, after(near, begun), from_high, mixed)
    pair_in = lax.ppermute(pair, "slab", even_odd("slab"))
    keys, bounds = call(
        functools.partial(order_kernel, per), out_shape=(shape((count, LANES), i32), shape((SUB, LANES), i32)),
        in_specs=[SMEM, VMEM], out_specs=(VMEM, VMEM), compiler_params=params(6), cost_estimate=cost(3), name="order",
    )(place, after(begun, pair))
    other = after(other, keys, pair_in)
    other_in = lax.ppermute(other, "slab", odd_even("slab", False))
    early = call(
        early_kernel, out_shape=shape((count, LANES), f32), in_specs=[SMEM] + [VMEM] * 5 + [SMEM], out_specs=VMEM,
        scratch_shapes=[pltpu.VMEM((2 * ways * per, LANES), f32)], compiler_params=params(6), cost_estimate=cost(3),
        name="early",
    )(place, pair_in, from_low, near, from_high, keys, bounds)
    interp = call(
        pick_kernel, out_shape=shape((nx, tiles * ny, LANES), f32), in_specs=[SMEM] + [VMEM] * 7 + [SMEM, VMEM],
        out_specs=VMEM,
        scratch_shapes=[pltpu.VMEM((rows, LANES), f32), pltpu.VMEM((count, LANES), i32), pltpu.VMEM((count, LANES), f32)],
        compiler_params=params(8), cost_estimate=cost(12), name="pick",
    )(place, pair_in, other_in, from_low, near, from_high, keys, early, bounds, factors)
    p_low, p_high = swap(interp[nx - REACH :], interp[:REACH], "dom")
    halo = shape((tiles * wedge(nx, REACH)[1], LANES), f32)
    pair, other = call(pack_kernel, out_shape=(halo, halo), in_specs=[SMEM] + [VMEM] * 3,
                       out_specs=(VMEM, VMEM), compiler_params=params(6), cost_estimate=cost(1), name="pack",
                       )(place, p_low, interp, p_high)
    p_pair, p_other = exchange(pair, other, "slab")
    extent = nx + 2 * REACH
    field = pltpu.VMEM((3, tiles, extent, 3 * SUB, LANES), f32)
    basis, sums = call(
        krylov_kernel,
        out_shape=(shape((3 * ITERS, tiles * nx * ny, LANES), f32), shape((SUB, LANES), f32)),
        in_specs=[SMEM] + [VMEM] * 10,
        out_specs=(VMEM, VMEM),
        scratch_shapes=[pltpu.VMEM((tiles, extent, 3 * SUB, LANES), f32)] * 2 + [field] * 4,
        compiler_params=params(20), cost_estimate=cost(7), name="krylov",
    )(place, interp, p_low, p_high, p_pair, p_other, mixed, from_low, from_high, pair_in, other_in)
    sums = far_hops(sums, "dom")
    sums = far_hops(sums, "slab")
    fields = 3 * ITERS
    short = -(-ways * fields // SUB) * SUB
    kept, message = shape((short, LANES), f32), shape((SUB + short, LANES), f32)
    keep, pair, other = call(
        functools.partial(surface_kernel, nz), out_shape=(kept, message, message), in_specs=[SMEM, SMEM, VMEM, VMEM],
        out_specs=(VMEM,) * 3, scratch_shapes=[pltpu.VMEM((2 * SUB, LANES), i32), pltpu.VMEM((2 * SUB, LANES), f32)],
        compiler_params=params(6), cost_estimate=cost(4), name="surface",
    )(tally, place, basis, boundary.reshape(-1, 1, LANES))
    pair_in, sent, other_in = pair_hops(sums, pair, other, "dom")
    keep, pair, other = call(
        route_kernel, out_shape=(kept, message, message), in_specs=[SMEM] + [VMEM] * 4,
        out_specs=(VMEM,) * 3, compiler_params=params(4), cost_estimate=cost(1), name="route",
    )(place, keep, pair_in, sent, other_in)
    row_hot, lane_hot = call(
        hot_kernel, out_shape=(shape((ways * ways, heat.shape[0], LANES), jnp.bfloat16),
                               shape((ways * ways, LANES, LANES), jnp.bfloat16)),
        in_specs=[VMEM], out_specs=(VMEM, VMEM), compiler_params=params(4), cost_estimate=cost(1), name="hot",
    )(after(accepting, pair).reshape(-1, 1, LANES))
    pair_in = lax.ppermute(pair, "slab", even_odd("slab"))
    sent = lax.dynamic_update_slice(other, pair[:SUB] + pair_in[:SUB], (0, 0))
    other_in = lax.ppermute(sent, "slab", odd_even("slab", True))
    return call(
        finish_kernel,
        out_shape=(shape((3, nx, ny, nz), f32), shape((3, heat_level.shape[0]), f32)),
        in_specs=[SMEM] + [VMEM] * 7,
        out_specs=(HBM, HBM),
        scratch_shapes=[pltpu.VMEM((3, nx, ny, nz), f32), pltpu.VMEM((3, heat_level.shape[0]), f32),
                        pltpu.VMEM(heat.shape, f32), pltpu.SemaphoreType.DMA((3,))],
        compiler_params=params(8), cost_estimate=cost(2), name="finish",
    )(place, keep, pair_in, sent, other_in, basis, row_hot, lane_hot)


def solution(mesh):
    both = ("dom", "slab")
    in_specs = (
        P(both),
        P(both, None, None, None),
        P(None, "dom", "slab", None),
        P(None, "dom", "slab", None),
        P(None, "dom", "slab", None),
        P("dom", "slab", None),
        P(both, None, None, None),
        P(both, None),
        P(both, None, None, None),
    )
    out_specs = (P(None, "dom", "slab", None), P(None, both))

    return jax.shard_map(on_device, mesh=mesh, in_specs=in_specs, out_specs=out_specs, check_vma=False)
```

time: 107 us -> 105 us (0.981)
  blocking collectives: 7.7 us -> 0 us
  starting transfers between devices: 31.1 us -> 36.7 us
  Pallas kernels: 45.9 us -> 49.1 us
  local copies, waits for them, and re-layouts: 2.83 us -> 1.05 us
  waiting for transfers between devices: 17.9 us -> 16.3 us
    ppermute x3 -> x11, starting transfers between devices: 8.19 us -> 31.3 us  [the longest x1 9.03 us: exchange(): lax.ppermute(pair, axis, even_odd(axis))]
    ppermute x8 -> x2, starting transfers between devices: 22.9 us -> 5.45 us  [swap(): return (lax.ppermute(last, axis, up), lax.ppermute(leading, axis, down))]
    ppermute x8 -> x2, waiting for transfers between devices: 11.4 us -> 0.89 us  [swap(): return (lax.ppermute(last, axis, up), lax.ppermute(leading, axis, down))]
    ppermute x3 -> x11, waiting for transfers between devices: 6.56 us -> 15.4 us  [the longest x2 5.5 us: on_device(): pair_in = lax.ppermute(pair, 'slab', even_odd('slab'))]
    all_gather x1 -> x0, blocking collectives: 7.7 us -> none  [on_device(): lax.all_gather(lax.dynamic_update_slice(surface, sums, (0, 0)), 'dom')]
    pallas_call x7 -> x11, Pallas kernels: 30.7 us -> 35.4 us  [the longest x1 7.36 us: on_device(): call(pick_kernel, out_shape=shape((nx, tiles * ny, LANES), f32), in_specs...]
    pallas_call x1, Pallas kernels: 9.06 us -> 6.47 us  [on_device(): call(krylov_kernel, out_shape=(shape((3 * ITERS, tiles * nx * ny, LANES),...]
    unnamed x20 -> x22, local copies, waits for them, and re-layouts: 2.74 us -> 0.95 us
  transfers between devices with their start and end apart: 11 -> 13, of which waited for: 7 -> 7; matrix products, arithmetic and copies ran while one was open for 0% -> 0% of each run, Pallas kernels for 13% -> 20%
where the time goes in v3:
time: 105 us; the launch traced here: 104 us
  Pallas kernels  49.1 us (47%)
  starting transfers between devices  36.7 us (35%)
  waiting for transfers between devices  16.3 us (16%)
  local copies, waits for them, and re-layouts  1.05 us (1%)
    ppermute x1, starting transfers between devices, exchange(): lax.ppermute(pair, axis, even_odd(axis))  9.03 us
    ppermute x1, starting transfers between devices, far_hops(): lax.ppermute(sums, axis, [(i, (i + hop) % peers) for i in range(peers)])  7.86 us
    pallas_call x1, Pallas kernels, on_device(): call(pick_kernel, out_shape=shape((nx, tiles * ny, LANES), f32), in_specs...  7.36 us
    pallas_call x1, Pallas kernels, on_device(): call(krylov_kernel, out_shape=(shape((3 * ITERS, tiles * nx * ny, LANES),...  6.47 us
    pallas_call x1, Pallas kernels, on_device(): call(early_kernel, out_shape=shape((count, LANES), f32), in_specs=[SMEM]...  6.38 us
    ppermute x2, waiting for transfers between devices, on_device(): pair_in = lax.ppermute(pair, 'slab', even_odd('slab'))  5.5 us
    pallas_call x1, Pallas kernels, on_device(): call(depart_kernel, out_shape=(dom_message, shape((nx, tiles * ny, LANES)...  5.49 us
    ppermute x1, waiting for transfers between devices, on_device(): other_in = lax.ppermute(sent, 'slab', odd_even('slab', True))  5.47 us
  transfers between devices with their start and end apart: 13, of which 7 were waited for; matrix products, arithmetic and copies ran while one was open for 0% of the time, Pallas kernels for 20%

profile of v3, /device:TPU:0, one launch (start us, length us, event | category | flops | bytes accessed | tf_op | source)
XLA Modules:
  0.0 104.2 jit_solution(349870951902546963)
XLA Ops:
  0.6 5.5 %depart.1 = (f32[288,128]{1,0:T(8,128)}, f32[8,32,128]{2,1,0:T(8,128)}) custom-call(f32[128,128]{1,0:T(8,128)} %bitcast.14, s32[576,128]{1,0:T(8,128)} %bitcast.11, f32[8,8,512]{2,1,0:T(8,128)} %rigid_hbm.1), custom_call_target="tpu_custom_call" | custom-call | flops 2000000000 | tf_op jit(solution)/shard_map/depart/pallas_call | solution.py:837
  6.2 0.0 copy-start.8
  6.2 0.9 copy-done.8
  7.1 3.5 %down.1 = f32[288,128]{1,0:T(8,128)S(1)} custom-call(f32[128,128]{1,0:T(8,128)S(1)} %bitcast.15, s32[576,128]{1,0:T(8,128)S(1)} %bitcast.12, f32[8,32,128]{2,1,0:T(8,128)S(1)} %copy-done.8), custom_call_target="tpu_custom_call" | custom-call | flops 1600000000 | tf_op jit(solution)/shard_map/down/pallas_call | solution.py:846
  10.6 1.3 %collective-permute-start.1 = (f32[288,128]{1,0:T(8,128)S(1)}, f32[288,128]{1,0:T(8,128)S(1)}, u32[]{:S(2)}, u32[]{:S(2)}) collective-permute-start(f32[288,128]{1,0:T(8,128)S(1)} %down.1), channel_id=1, source_target_pairs={{8,0},{16,8},{24,16},{9,1},{17,9},{25,17},{10,2},{18,10},{26,18},{... | collective-permute-start | bytes 442376 | tf_op jit(solution)/shard_map/ppermute | solution.py:848
  11.9 0.0 copy-start
  11.9 0.0 copy-start.1
  12.0 3.2 %collective-permute-start = (f32[288,128]{1,0:T(8,128)S(1)}, f32[288,128]{1,0:T(8,128)S(1)}, u32[]{:S(2)}, u32[]{:S(2)}) collective-permute-start(f32[288,128]{1,0:T(8,128)S(1)} %copy-done.10), channel_id=1, source_target_pairs={{0,8},{8,16},{16,24},{1,9},{9,17},{17,25},{2,10},{10,18},{18,26},{... | collective-permute-start | bytes 442376 | tf_op jit(solution)/shard_map/ppermute | solution.py:845
  15.1 3.5 %near.1 = f32[192,128]{1,0:T(8,128)S(1)} custom-call(f32[128,128]{1,0:T(8,128)S(1)} %bitcast.16, s32[576,128]{1,0:T(8,128)S(1)} %bitcast.13), custom_call_target="tpu_custom_call" | custom-call | flops 1600000000 | tf_op jit(solution)/shard_map/near/pallas_call | solution.py:849
  18.7 0.1 stack.47.place.inside
  18.8 0.0 copy-done.1
  18.8 0.0 copy-start.9
  18.8 2.8 %plan.1.begun = s32[1024,128]{1,0:T(8,128)S(1)} custom-call(s32[7]{0:T(128)S(1)} %stack.47.place.inside, s32[4,8,8,512]{3,2,1,0:T(8,128)S(1)} %copy-done, s32[4,8,8,512]{3,2,1,0:T(8,128)S(1)} %copy-done.1), custom_call_target="tpu_custom_call" | custom-call | flops 1200000000 | tf_op jit(solution)/shard_map/plan/pallas_call | solution.py:853
  21.6 0.0 collective-permute-done.1.high.d_high
  21.6 0.0 collective-permute-done.low.d_low
  21.6 0.6 forward.1
  22.2 3.0 %collective-permute-start.2 = (f32[312,128]{1,0:T(8,128)S(1)}, f32[312,128]{1,0:T(8,128)S(1)}, u32[]{:S(2)}, u32[]{:S(2)}) collective-permute-start(f32[312,128]{1,0:T(8,128)S(1)} %get-tuple-element.31), channel_id=1, source_target_pairs={{0,1},{1,0},{2,3},{3,2},{4,5},{5,4},{6,7},{7,6},{8,9},{9,8},{10,11... | collective-permute-start | bytes 479240 | tf_op jit(solution)/shard_map/ppermute | solution.py:863
  25.2 2.7 %order.1 = (s32[1024,128]{1,0:T(8,128)S(1)}, s32[8,128]{1,0:T(8,128)S(1)}) custom-call(s32[7]{0:T(128)S(1)} %stack.47.place.inside, s32[1024,128]{1,0:T(8,128)S(1)} %plan.1.begun), custom_call_target="tpu_custom_call" | custom-call | flops 1200000000 | tf_op jit(solution)/shard_map/order/pallas_call | solution.py:864
  27.9 1.7 %collective-permute-done.2.pair.d_pair = f32[312,128]{1,0:T(8,128)S(1)} collective-permute-done((f32[312,128]{1,0:T(8,128)S(1)}, f32[312,128]{1,0:T(8,128)S(1)}, u32[]{:S(2)}, u32[]{:S(2)}) %collective-permute-start.2) | collective-permute-done | bytes 159776 | tf_op jit(solution)/shard_map/ppermute | solution.py:863
  29.6 0.7 collective-permute-start.3
  30.2 0.0 copy-start.2
  30.3 6.4 %early.1 = f32[1024,128]{1,0:T(8,128)S(1)} custom-call(s32[7]{0:T(128)S(1)} %stack.47.place.inside, f32[312,128]{1,0:T(8,128)S(1)} %collective-permute-done.2.pair.d_pair, f32[288,128]{1,0:T(8,128)S(1)} %collective-permute-done.low.d_low, f32[192,128]{1,0:T(8,128)S(1)} %near.1, f32[288,128]{1,0:T(8,128)S(1)} %collective-permute-done.1.high.d_high, ...), custom_call_target="tpu_custom_call" | custom-call | flops 1200000000 | tf_op jit(solution)/shard_map/early/pallas_call | solution.py:870
  36.6 0.0 collective-permute-done.3.other.d_other
  36.7 7.4 %pick.1.own = f32[8,32,128]{2,1,0:T(8,128)S(1)} custom-call(s32[7]{0:T(128)S(1)} %stack.47.place.inside, f32[312,128]{1,0:T(8,128)S(1)} %collective-permute-done.2.pair.d_pair, f32[312,128]{1,0:T(8,128)S(1)} %collective-permute-done.3.other.d_other, f32[288,128]{1,0:T(8,128)S(1)} %collective-permute-done.low.d_low, f32[192,128]{1,0:T(8,128)S(1)} %near.1, ...), custom_call_target="tpu_custom_call" | custom-call | flops 4800000000 | tf_op jit(solution)/shard_map/pick/pallas_call | solution.py:875
  44.1 1.3 %collective-permute-start.5 = (f32[5,32,128]{2,1,0:T(8,128)S(1)}, f32[5,32,128]{2,1,0:T(8,128)S(1)}, u32[]{:S(2)}, u32[]{:S(2)}) collective-permute-start(f32[5,32,128]{2,1,0:T(8,128)S(1)} %get-tuple-element.52), channel_id=1, source_target_pairs={{8,0},{16,8},{24,16},{9,1},{17,9},{25,17},{10,2},{18,10},{26,18},{... | collective-permute-start | bytes 245768 | tf_op jit(solution)/shard_map/ppermute | solution.py:784
  45.4 4.2 %collective-permute-start.4 = (f32[5,32,128]{2,1,0:T(8,128)S(1)}, f32[5,32,128]{2,1,0:T(8,128)S(1)}, u32[]{:S(2)}, u32[]{:S(2)}) collective-permute-start(f32[5,32,128]{2,1,0:T(8,128)S(1)} %get-tuple-element.53), channel_id=1, source_target_pairs={{0,8},{8,16},{16,24},{1,9},{9,17},{17,25},{2,10},{10,18},{18,26},{... | collective-permute-start | bytes 245768 | tf_op jit(solution)/shard_map/ppermute | solution.py:784
  49.5 0.0 collective-permute-done.5.high.p_high
  49.5 0.9 collective-permute-done.4.low.p_low
  50.4 0.6 pack.1
  51.0 9.0 %collective-permute-start.6 = (f32[240,128]{1,0:T(8,128)S(1)}, f32[240,128]{1,0:T(8,128)S(1)}, u32[]{:S(2)}, u32[]{:S(2)}) collective-permute-start(f32[240,128]{1,0:T(8,128)S(1)} %get-tuple-element.37), channel_id=1, source_target_pairs={{0,1},{1,0},{2,3},{3,2},{4,5},{5,4},{6,7},{7,6},{8,9},{9,8},{10,11... | collective-permute-start | bytes 368648 | tf_op jit(solution)/shard_map/ppermute | solution.py:802
  60.1 0.8 collective-permute-start.7
  60.9 2.1 %collective-permute-done.6.p_pair = f32[240,128]{1,0:T(8,128)S(1)} collective-permute-done((f32[240,128]{1,0:T(8,128)S(1)}, f32[240,128]{1,0:T(8,128)S(1)}, u32[]{:S(2)}, u32[]{:S(2)}) %collective-permute-start.6) | collective-permute-done | bytes 122912 | tf_op jit(solution)/shard_map/ppermute | solution.py:802
  62.9 0.0 collective-permute-done.7.p_other
  62.9 6.5 %krylov.1 = (f32[12,256,128]{2,1,0:T(8,128)S(1)}, f32[8,128]{1,0:T(8,128)S(1)}) custom-call(s32[7]{0:T(128)S(1)} %stack.47.place.inside, f32[8,32,128]{2,1,0:T(8,128)S(1)} %pick.1.own, f32[5,32,128]{2,1,0:T(8,128)S(1)} %collective-permute-done.4.low.p_low, f32[5,32,128]{2,1,0:T(8,128)S(1)} %collective-permute-done.5.high.p_high, ...), custom_call_target="tpu_custom_call" | custom-call | flops 2800000000 | tf_op jit(solution)/shard_map/krylov/pallas_call | solution.py:889
  69.4 7.9 %collective-permute-start.8 = (f32[8,128]{1,0:T(8,128)S(1)}, f32[8,128]{1,0:T(8,128)S(1)}, u32[]{:S(2)}, u32[]{:S(2)}) collective-permute-start(f32[8,128]{1,0:T(8,128)S(1)} %get-tuple-element.42), channel_id=1, source_target_pairs={{0,4},{1,5},{2,6},{3,7},{4,0},{5,1},{6,2},{7,3},{8,12},{9,13},{10,... | collective-permute-start | bytes 12296 | tf_op jit(solution)/shard_map/ppermute | solution.py:809
  77.3 5.3 %surface.1 = (f32[40,128]{1,0:T(8,128)S(1)}, f32[48,128]{1,0:T(8,128)S(1)}, f32[48,128]{1,0:T(8,128)S(1)}) custom-call(s32[1,9]{1,0:T(1,128)S(1)} %copy-done.7, s32[7]{0:T(128)S(1)} %stack.47.place.inside, f32[12,256,128]{2,1,0:T(8,128)S(1)} %get-tuple-element.39.basis, s32[9,1,128]{2,1,0:T(1,128)S(1)} %bitcast.17), custom_call_target="tpu_custom_call" | custom-call | flops 1600000000 | tf_op jit(solution)/shard_map/surface/pallas_call | solution.py:902
  82.6 0.0 collective-permute-done.8
  82.6 0.7 collective-permute-start.9
  83.3 0.8 collective-permute-done.9.pair_in
  84.1 3.8 %collective-permute-start.10 = (f32[48,128]{1,0:T(8,128)S(1)}, f32[48,128]{1,0:T(8,128)S(1)}, u32[]{:S(2)}, u32[]{:S(2)}) collective-permute-start(f32[48,128]{1,0:T(8,128)S(1)} %fusion.1.sent), channel_id=1, source_target_pairs={{0,24},{8,16},{16,8},{24,0},{1,25},{9,17},{17,9},{25,1},{2,26},{10... | collective-permute-start | bytes 73736 | tf_op jit(solution)/shard_map/ppermute | solution.py:818
  87.9 1.5 %collective-permute-done.10.other_in = f32[48,128]{1,0:T(8,128)S(1)} collective-permute-done((f32[48,128]{1,0:T(8,128)S(1)}, f32[48,128]{1,0:T(8,128)S(1)}, u32[]{:S(2)}, u32[]{:S(2)}) %collective-permute-start.10) | collective-permute-done | bytes 24608 | tf_op jit(solution)/shard_map/ppermute | solution.py:818
  89.4 0.6 route.1
  90.0 0.1 collective-permute-start.11
  90.1 3.8 %collective-permute-done.11.pair = f32[48,128]{1,0:T(8,128)S(1)} collective-permute-done((f32[48,128]{1,0:T(8,128)S(1)}, f32[48,128]{1,0:T(8,128)S(1)}, u32[]{:S(2)}, u32[]{:S(2)}) %collective-permute-start.11) | collective-permute-done | bytes 24608 | tf_op jit(solution)/shard_map/ppermute | solution.py:917
  93.9 0.9 collective-permute-start.12
  94.8 0.1 hot.1
  95.0 5.5 %collective-permute-done.12.other = f32[48,128]{1,0:T(8,128)S(1)} collective-permute-done((f32[48,128]{1,0:T(8,128)S(1)}, f32[48,128]{1,0:T(8,128)S(1)}, u32[]{:S(2)}, u32[]{:S(2)}) %collective-permute-start.12) | collective-permute-done | bytes 24608 | tf_op jit(solution)/shard_map/ppermute | solution.py:919
  100.5 3.8 %finish.1 = (f32[3,8,8,512]{3,2,1,0:T(8,128)}, f32[3,16384]{1,0:T(4,128)}) custom-call(s32[7]{0:T(128)S(1)} %stack.47.place.inside, f32[40,128]{1,0:T(8,128)S(1)} %get-tuple-element.44.keep, f32[48,128]{1,0:T(8,128)S(1)} %collective-permute-done.11.pair, f32[48,128]{1,0:T(8,128)S(1)} %fusion.sent, f32[48,128]{1,0:T(8,128)S(1)} %collective-permute-done.12.other, ...), custom_call_target="tpu_custom_call" | custom-call | flops 800000000 | tf_op jit(solution)/shard_map/finish/pallas_call | solution.py:920
  (19 shorter events, 0.1 us)
Async XLA Ops:
  0.6 5.5 %copy-start.3 = (s32[1,3,3,8192]{3,0,2,1:T(1,128)S(1)}, s32[1,3,3,8192]{3,0,2,1:T(1,128)}, u32[]{:S(2)}) copy-start(s32[1,3,3,8192]{3,0,2,1:T(1,128)} %param.10) | copy-start | bytes 884740
  0.6 5.5 %copy-start.4 = (f32[16384]{0:T(1024)S(1)}, f32[16384]{0:T(1024)}, u32[]{:S(2)}) copy-start(f32[16384]{0:T(1024)} %param.9) | copy-start | bytes 196612
  6.2 0.9 copy-start.8
  7.1 4.8 %copy-start.10 = (f32[288,128]{1,0:T(8,128)S(1)}, f32[288,128]{1,0:T(8,128)}, u32[]{:S(2)}) copy-start(f32[288,128]{1,0:T(8,128)} %get-tuple-element.26) | copy-start | bytes 442372
  10.6 11.0 %collective-permute-start.1 = (f32[288,128]{1,0:T(8,128)S(1)}, f32[288,128]{1,0:T(8,128)S(1)}, u32[]{:S(2)}, u32[]{:S(2)}) collective-permute-start(f32[288,128]{1,0:T(8,128)S(1)} %down.1), channel_id=1, source_target_pairs={{8,0},{16,8},{24,16},{9,1},{17,9},{25,17},{10,2},{18,10},{26,18},{... | collective-permute-start | bytes 442376 | tf_op jit(solution)/shard_map/ppermute | solution.py:848
  11.9 6.9 %copy-start = (s32[4,8,8,512]{3,2,1,0:T(8,128)S(1)}, s32[4,8,8,512]{3,2,1,0:T(8,128)}, u32[]{:S(2)}) copy-start(s32[4,8,8,512]{3,2,1,0:T(8,128)} %shift) | copy-start | bytes 1572868
  11.9 6.8 %copy-start.1 = (s32[4,8,8,512]{3,2,1,0:T(8,128)S(1)}, s32[4,8,8,512]{3,2,1,0:T(8,128)}, u32[]{:S(2)}) copy-start(s32[4,8,8,512]{3,2,1,0:T(8,128)} %bucket.1) | copy-start | bytes 1572868
  12.0 9.6 %collective-permute-start = (f32[288,128]{1,0:T(8,128)S(1)}, f32[288,128]{1,0:T(8,128)S(1)}, u32[]{:S(2)}, u32[]{:S(2)}) collective-permute-start(f32[288,128]{1,0:T(8,128)S(1)} %copy-done.10), channel_id=1, source_target_pairs={{0,8},{8,16},{16,24},{1,9},{9,17},{17,25},{2,10},{10,18},{18,26},{... | collective-permute-start | bytes 442376 | tf_op jit(solution)/shard_map/ppermute | solution.py:845
  18.8 2.8 %copy-start.9 = (f32[8,32,128]{2,1,0:T(8,128)S(1)}, f32[8,32,128]{2,1,0:T(8,128)}, u32[]{:S(2)}) copy-start(f32[8,32,128]{2,1,0:T(8,128)} %get-tuple-element.27.mixed.rigid) | copy-start | bytes 393220
  22.2 7.4 %collective-permute-start.2 = (f32[312,128]{1,0:T(8,128)S(1)}, f32[312,128]{1,0:T(8,128)S(1)}, u32[]{:S(2)}, u32[]{:S(2)}) collective-permute-start(f32[312,128]{1,0:T(8,128)S(1)} %get-tuple-element.31), channel_id=1, source_target_pairs={{0,1},{1,0},{2,3},{3,2},{4,5},{5,4},{6,7},{7,6},{8,9},{9,8},{10,11... | collective-permute-start | bytes 479240 | tf_op jit(solution)/shard_map/ppermute | solution.py:863
  29.6 7.1 %collective-permute-start.3 = (f32[312,128]{1,0:T(8,128)S(1)}, f32[312,128]{1,0:T(8,128)S(1)}, u32[]{:S(2)}, u32[]{:S(2)}) collective-permute-start(f32[312,128]{1,0:T(8,128)S(1)} %get-tuple-element.35), channel_id=1, source_target_pairs={{1,2},{2,1},{3,4},{4,3},{5,6},{6,5},{9,10},{10,9},{11,12},{12,11},... | collective-permute-start | bytes 479240 | tf_op jit(solution)/shard_map/ppermute | solution.py:869
  30.2 6.4 %copy-start.2 = (f32[4,8,8,512]{3,2,1,0:T(8,128)S(1)}, f32[4,8,8,512]{3,2,1,0:T(8,128)}, u32[]{:S(2)}) copy-start(f32[4,8,8,512]{3,2,1,0:T(8,128)} %factor.1) | copy-start | bytes 1572868
  44.1 5.5 %collective-permute-start.5 = (f32[5,32,128]{2,1,0:T(8,128)S(1)}, f32[5,32,128]{2,1,0:T(8,128)S(1)}, u32[]{:S(2)}, u32[]{:S(2)}) collective-permute-start(f32[5,32,128]{2,1,0:T(8,128)S(1)} %get-tuple-element.52), channel_id=1, source_target_pairs={{8,0},{16,8},{24,16},{9,1},{17,9},{25,17},{10,2},{18,10},{26,18},{... | collective-permute-start | bytes 245768 | tf_op jit(solution)/shard_map/ppermute | solution.py:784
  45.4 5.1 %collective-permute-start.4 = (f32[5,32,128]{2,1,0:T(8,128)S(1)}, f32[5,32,128]{2,1,0:T(8,128)S(1)}, u32[]{:S(2)}, u32[]{:S(2)}) collective-permute-start(f32[5,32,128]{2,1,0:T(8,128)S(1)} %get-tuple-element.53), channel_id=1, source_target_pairs={{0,8},{8,16},{16,24},{1,9},{9,17},{17,25},{2,10},{10,18},{18,26},{... | collective-permute-start | bytes 245768 | tf_op jit(solution)/shard_map/ppermute | solution.py:784
  51.0 11.9 %collective-permute-start.6 = (f32[240,128]{1,0:T(8,128)S(1)}, f32[240,128]{1,0:T(8,128)S(1)}, u32[]{:S(2)}, u32[]{:S(2)}) collective-permute-start(f32[240,128]{1,0:T(8,128)S(1)} %get-tuple-element.37), channel_id=1, source_target_pairs={{0,1},{1,0},{2,3},{3,2},{4,5},{5,4},{6,7},{7,6},{8,9},{9,8},{10,11... | collective-permute-start | bytes 368648 | tf_op jit(solution)/shard_map/ppermute | solution.py:802
  60.1 17.2 %copy-start.5 = (s32[1,3,3,128]{3,0,2,1:T(1,128)S(1)}, s32[1,3,3,128]{3,0,2,1:T(1,128)}, u32[]{:S(2)}) copy-start(s32[1,3,3,128]{3,0,2,1:T(1,128)} %param.15) | copy-start | bytes 13828
  60.1 17.2 %copy-start.7 = (s32[1,9]{1,0:T(1,128)S(1)}, s32[1,9]{1,0:T(1,128)}, u32[]{:S(2)}) copy-start(s32[1,9]{1,0:T(1,128)} %tally.1) | copy-start | bytes 112
  60.1 2.9 %collective-permute-start.7 = (f32[240,128]{1,0:T(8,128)S(1)}, f32[240,128]{1,0:T(8,128)S(1)}, u32[]{:S(2)}, u32[]{:S(2)}) collective-permute-start(f32[240,128]{1,0:T(8,128)S(1)} %get-tuple-element.38), channel_id=1, source_target_pairs={{1,2},{2,1},{3,4},{4,3},{5,6},{6,5},{9,10},{10,9},{11,12},{12,11},... | collective-permute-start | bytes 368648 | tf_op jit(solution)/shard_map/ppermute | solution.py:802
  69.4 13.2 %collective-permute-start.8 = (f32[8,128]{1,0:T(8,128)S(1)}, f32[8,128]{1,0:T(8,128)S(1)}, u32[]{:S(2)}, u32[]{:S(2)}) collective-permute-start(f32[8,128]{1,0:T(8,128)S(1)} %get-tuple-element.42), channel_id=1, source_target_pairs={{0,4},{1,5},{2,6},{3,7},{4,0},{5,1},{6,2},{7,3},{8,12},{9,13},{10,... | collective-permute-start | bytes 12296 | tf_op jit(solution)/shard_map/ppermute | solution.py:809
  77.3 17.6 %copy-start.6 = (s32[1,3,3,128]{3,0,2,1:T(1,128)S(1)}, s32[1,3,3,128]{3,0,2,1:T(1,128)}, u32[]{:S(2)}) copy-start(s32[1,3,3,128]{3,0,2,1:T(1,128)} %param.17) | copy-start | bytes 13828
  82.6 1.5 %collective-permute-start.9 = (f32[48,128]{1,0:T(8,128)S(1)}, f32[48,128]{1,0:T(8,128)S(1)}, u32[]{:S(2)}, u32[]{:S(2)}) collective-permute-start(f32[48,128]{1,0:T(8,128)S(1)} %get-tuple-element.50), channel_id=1, source_target_pairs={{0,8},{8,0},{16,24},{24,16},{1,9},{9,1},{17,25},{25,17},{2,10},{10... | collective-permute-start | bytes 73736 | tf_op jit(solution)/shard_map/ppermute | solution.py:816
  84.1 5.3 %collective-permute-start.10 = (f32[48,128]{1,0:T(8,128)S(1)}, f32[48,128]{1,0:T(8,128)S(1)}, u32[]{:S(2)}, u32[]{:S(2)}) collective-permute-start(f32[48,128]{1,0:T(8,128)S(1)} %fusion.1.sent), channel_id=1, source_target_pairs={{0,24},{8,16},{16,8},{24,0},{1,25},{9,17},{17,9},{25,1},{2,26},{10... | collective-permute-start | bytes 73736 | tf_op jit(solution)/shard_map/ppermute | solution.py:818
  90.0 3.9 %collective-permute-start.11 = (f32[48,128]{1,0:T(8,128)S(1)}, f32[48,128]{1,0:T(8,128)S(1)}, u32[]{:S(2)}, u32[]{:S(2)}) collective-permute-start(f32[48,128]{1,0:T(8,128)S(1)} %get-tuple-element.45), channel_id=1, source_target_pairs={{0,1},{1,0},{2,3},{3,2},{4,5},{5,4},{6,7},{7,6},{8,9},{9,8},{10,11... | collective-permute-start | bytes 73736 | tf_op jit(solution)/shard_map/ppermute | solution.py:917
  93.9 6.5 %collective-permute-start.12 = (f32[48,128]{1,0:T(8,128)S(1)}, f32[48,128]{1,0:T(8,128)S(1)}, u32[]{:S(2)}, u32[]{:S(2)}) collective-permute-start(f32[48,128]{1,0:T(8,128)S(1)} %fusion.sent), channel_id=1, source_target_pairs={{0,7},{1,2},{2,1},{3,4},{4,3},{5,6},{6,5},{7,0},{8,15},{9,10},{10,... | collective-permute-start | bytes 73736 | tf_op jit(solution)/shard_map/ppermute | solution.py:919

commit v4 on v3

--- a/solution.py
+++ b/solution.py
@@ -159,7 +159,7 @@
         return carry
 
     if not done:
-        lax.fori_loop(0, count // block, whole, 0)
+        lax.fori_loop(0, count // block, whole, 0, unroll=2)
     size = 2 * max(done, block)
     while size <= (until or count * SUB):
         span = min(size, count)
@@ -199,8 +199,8 @@
             for v, h in zip(spots, held): store(v, h)
             return carry
 
-        lax.fori_loop(0, (count // span) * (block // 2), top, 0, unroll=max(1, 8 // groups))
-        lax.fori_loop(0, count // block, finish, 0)
+        lax.fori_loop(0, (count // span) * (block // 2), top, 0, unroll=max(1, 16 // groups))
+        lax.fori_loop(0, count // block, finish, 0, unroll=2)
         size *= 2
 
 
@@ -231,7 +231,7 @@
                 keys[pl.ds(pl.multiple_of(v * SUB, SUB), SUB), :] = flat * (count * SUB) + (sub * count + v)
         return carry
 
-    lax.fori_loop(0, nx, build, 0)
+    lax.fori_loop(0, nx, build, 0, unroll=2)
     sort_rows([keys], 32, until=count)
 
 
@@ -305,36 +305,36 @@
     lax.fori_loop(0, rows // group, body, 0)
 
 
-def depart_kernel(heat_hbm, picks_hbm, rigid_hbm, up, mixed, heat, picks, rigid, arrived):
-    rows = picks.shape[0]
-    sources = (rigid_hbm, heat_hbm, picks_hbm.at[pl.ds(picks_hbm.shape[0] - rows, rows), :])
+def depart_kernel(heat_hbm, picks_hbm, rigid_hbm, up, heat, picks, rigid, arrived):
+    rows, narrow = picks.shape[0], rigid.shape[0]
+    sources = (rigid_hbm.at[pl.ds(rigid_hbm.shape[0] - narrow, narrow)], heat_hbm,
+               picks_hbm.at[pl.ds(picks_hbm.shape[0] - rows, rows), :])
     copies = [
         pltpu.make_async_copy(source, target, arrived.at[k])
         for k, (source, target) in enumerate(zip(sources, (rigid, heat, picks)))
     ]
     for copy in copies:
         copy.start()
-    nx, _, nz = rigid.shape
-    tiles = nz // LANES
-    narrow = REACH - 2
+    tiles = rigid.shape[2] // LANES
     copies[0].wait()
-    for x in range(nx):
-        values = mix([rigid[x, :, pl.ds(t * LANES, LANES)] for t in range(tiles)])
-        for t in range(tiles):
-            mixed[x, pl.ds(t * SUB, SUB), :] = values[t]
-            if x >= nx - narrow:
-                up[pl.ds(rows + ((x - nx + narrow) * tiles + t) * SUB, SUB), :] = values[t]
+    for x in range(narrow):
+        for t, value in enumerate(mix([rigid[x, :, pl.ds(t * LANES, LANES)] for t in range(tiles)])):
+            up[pl.ds(rows + (x * tiles + t) * SUB, SUB), :] = value
     copies[1].wait()
     copies[2].wait()
     slots_of(heat, picks, 0, up, rows)
 
 
-def depart_down_kernel(heat, picks, mixed, down):
+def depart_down_kernel(heat, picks, rigid, down, mixed):
     narrow = REACH - 2
-    tall = mixed.shape[1]
-    rows = down.shape[0] - narrow * tall
-    for x in range(narrow):
-        down[pl.ds(rows + x * tall, tall), :] = mixed[x]
+    nx, _, nz = rigid.shape
+    tiles = nz // LANES
+    rows = down.shape[0] - narrow * tiles * SUB
+    for x in range(nx):
+        for t, value in enumerate(mix([rigid[x, :, pl.ds(t * LANES, LANES)] for t in range(tiles)])):
+            mixed[x, pl.ds(t * SUB, SUB), :] = value
+            if x < narrow:
+                down[pl.ds(rows + (x * tiles + t) * SUB, SUB), :] = value
     slots_of(heat, picks, 0, down, rows)
 
 
@@ -429,7 +429,7 @@
             out[x, pl.ds(t * SUB, SUB), :] = total
         return carry
 
-    lax.fori_loop(0, nx, blend, 0)
+    lax.fori_loop(0, nx, blend, 0, unroll=2)
 
 
 def pack_kernel(place, low, own, high, pair, other):
@@ -521,7 +521,7 @@
                 u0[2, t, x, pl.ds(part * SUB, SUB), :] = scale * (along[t][1] - along[t][0])
         return carry
 
-    lax.fori_loop(1, nx + 2 * REACH - 1, load_row, 0)
+    lax.fori_loop(1, nx + 2 * REACH - 1, load_row, 0, unroll=2)
 
     def twice(ref, c, x, part):
         coefficient = (2.0 / HALF) * mask(x, part)
@@ -550,7 +550,7 @@
             return carry
 
         margin = ITERS - order
-        lax.fori_loop(REACH - margin, REACH + nx + margin, apply_row, 0)
+        lax.fori_loop(REACH - margin, REACH + nx + margin, apply_row, 0, unroll=2)
 
     def dots_row(x, carry):
         carry = list(carry)
@@ -567,7 +567,7 @@
                     basis[3 * j + c, pl.ds(pl.multiple_of(t * nx * SUB + x * SUB, SUB), SUB), :] = v[j]
         return tuple(carry)
 
-    totals = lax.fori_loop(0, nx, dots_row, tuple(zero for _ in range(8)))
+    totals = lax.fori_loop(0, nx, dots_row, tuple(zero for _ in range(8)), unroll=2)
     for k in range(8):
         sums[pl.ds(k, 1), :] = jnp.sum(totals[k], axis=0, keepdims=True)
 
@@ -616,7 +616,7 @@
         give(f, values)
         return carry
 
-    lax.fori_loop(0, fields, body, 0)
+    lax.fori_loop(0, fields, body, 0, unroll=3)
 
 
 def route_kernel(place, kept, pair_in, sent, other_in, keep, pair, other):
@@ -691,6 +691,20 @@
         direction = [r + ratio * d for r, d in zip(residual, direction)]
         rr = fresh
     return found
+
+
+def plain_kernel(basis, plain):
+    fields, nx, _, nz = plain.shape
+    tiles = nz // LANES
+
+    def row(x, carry):
+        for f in range(fields):
+            at = [pl.ds(pl.multiple_of(t * nx * SUB + x * SUB, SUB), SUB) for t in range(tiles)]
+            for t, value in enumerate(unmix([basis[f, k, :] for k in at])):
+                plain[f, x, :, pl.ds(t * LANES, LANES)] = value
+        return carry
+
+    lax.fori_loop(0, nx, row, 0)
 
 
 def hot_kernel(picks, row_hot, lane_hot):
@@ -756,15 +770,12 @@
 
     def row(x, carry):
         for c in range(3):
-            totals = []
             for t in range(tiles):
-                at = pl.ds(pl.multiple_of(t * nx * SUB + x * SUB, SUB), SUB)
-                total = wide[0] * basis[c, at, :]
+                at = pl.ds(t * LANES, LANES)
+                total = wide[0] * basis[c, x, :, at]
                 for j in range(1, 4):
-                    total = total + wide[j] * basis[3 * j + c, at, :]
-                totals.append(total)
-            for t, total in enumerate(unmix(totals)):
-                disp[c, x, :, pl.ds(t * LANES, LANES)] = total
+                    total = total + wide[j] * basis[3 * j + c, x, :, at]
+                disp[c, x, :, at] = total
         return carry
 
     half = nx // 2
@@ -815,7 +826,8 @@
     pair = pair if sums is None else lax.dynamic_update_slice(pair, sums, (0, 0))
     pair_in = lax.ppermute(pair, axis, even_odd(axis))
     sent = lax.dynamic_update_slice(other, pair[:SUB] + pair_in[:SUB], (0, 0))
-    return pair_in, sent, lax.ppermute(sent, axis, odd_even(axis, True))
+    other_in = lax.ppermute(sent, axis, odd_even(axis, True))
+    return pair_in, sent, other_in
 
 
 def on_device(heat_level, emitting, holder, bucket, factors, rigidity, boundary, tally, accepting):
@@ -834,17 +846,18 @@
     emit_rows = emitting.reshape(-1, LANES)
     dom_message = shape((ways * per + narrow * tiles * ny, LANES), f32)
     third = shape((ways * per, LANES), i32)
-    up, mixed = call(
-        depart_kernel, out_shape=(dom_message, shape((nx, tiles * ny, LANES), f32)), in_specs=[HBM] * 3,
-        out_specs=(VMEM,) * 2,
-        scratch_shapes=[pltpu.VMEM(heat.shape, f32), pltpu.VMEM(third.shape, i32), pltpu.VMEM(rigidity.shape, f32),
+    up = call(
+        depart_kernel, out_shape=dom_message, in_specs=[HBM] * 3, out_specs=VMEM,
+        scratch_shapes=[pltpu.VMEM(heat.shape, f32), pltpu.VMEM(third.shape, i32), pltpu.VMEM((narrow, ny, nz), f32),
                         pltpu.SemaphoreType.DMA((3,))],
         compiler_params=params(DEPART_MIB), cost_estimate=cost(5), name="depart",
     )(heat, emit_rows, rigidity)
     pairs_up = [(i, i + 1) for i in range(lax.axis_size("dom") - 1)]
     from_low = lax.ppermute(up, "dom", pairs_up)
-    down = call(depart_down_kernel, out_shape=dom_message, in_specs=[VMEM] * 3, out_specs=VMEM,
-                compiler_params=params(4), cost_estimate=cost(4), name="down")(heat, emit_rows, mixed)
+    down, mixed = call(
+        depart_down_kernel, out_shape=(dom_message, shape((nx, tiles * ny, LANES), f32)), in_specs=[VMEM] * 3,
+        out_specs=(VMEM,) * 2, compiler_params=params(4), cost_estimate=cost(4), name="down",
+    )(after(heat, up), emit_rows, rigidity)
     from_high = lax.ppermute(down, "dom", [(j, i) for i, j in pairs_up])
     near = call(near_kernel, out_shape=shape((ways * per, LANES), f32), in_specs=[VMEM] * 2, out_specs=VMEM,
                 compiler_params=params(4), cost_estimate=cost(4), name="near")(after(heat, down), emit_rows)
@@ -904,6 +917,8 @@
         out_specs=(VMEM,) * 3, scratch_shapes=[pltpu.VMEM((2 * SUB, LANES), i32), pltpu.VMEM((2 * SUB, LANES), f32)],
         compiler_params=params(6), cost_estimate=cost(4), name="surface",
     )(tally, place, basis, boundary.reshape(-1, 1, LANES))
+    plain = call(plain_kernel, out_shape=shape((3 * ITERS, nx, ny, nz), f32), in_specs=[VMEM], out_specs=VMEM,
+                 compiler_params=params(6), cost_estimate=cost(3), name="plain")(after(basis, pair))
     pair_in, sent, other_in = pair_hops(sums, pair, other, "dom")
     keep, pair, other = call(
         route_kernel, out_shape=(kept, message, message), in_specs=[SMEM] + [VMEM] * 4,
@@ -925,7 +940,7 @@
         scratch_shapes=[pltpu.VMEM((3, nx, ny, nz), f32), pltpu.VMEM((3, heat_level.shape[0]), f32),
                         pltpu.VMEM(heat.shape, f32), pltpu.SemaphoreType.DMA((3,))],
         compiler_params=params(8), cost_estimate=cost(2), name="finish",
-    )(place, keep, pair_in, sent, other_in, basis, row_hot, lane_hot)
+    )(place, keep, pair_in, sent, other_in, plain, row_hot, lane_hot)
 
 
 def solution(mesh):

time: 105 us -> 97.6 us (0.930)
  waiting for transfers between devices: 16.3 us -> 14 us
  starting transfers between devices: 36.7 us -> 34.7 us
  Pallas kernels: 49.1 us -> 47.5 us
    ppermute x2, waiting for transfers between devices: 5.5 us -> 0.66 us  [on_device(): pair_in = lax.ppermute(pair, 'slab', even_odd('slab'))]
    pallas_call x2 -> x3, Pallas kernels: 9.03 us -> 12.6 us  [the longest x1 5.25 us: on_device(): call(depart_kernel, out_shape=dom_message, in_specs=[HBM] * 3, out_specs=...]
    ppermute x2, waiting for transfers between devices: 0.89 us -> 3.85 us  [swap(): return (lax.ppermute(last, axis, up), lax.ppermute(leading, axis, down))]
    ppermute x1, starting transfers between devices: 3.82 us -> 1.65 us  [pair_hops(): other_in = lax.ppermute(sent, axis, odd_even(axis, True))]
    pallas_call x1, Pallas kernels: 6.47 us -> 4.39 us  [on_device(): call(krylov_kernel, out_shape=(shape((3 * ITERS, tiles * nx * ny, LANES),...]
    pallas_call x1, Pallas kernels: 3.76 us -> 2.52 us  [on_device(): call(finish_kernel, out_shape=(shape((3, nx, ny, nz), f32), shape((3, hea...]
  transfers between devices with their start and end apart: 13 -> 13, of which waited for: 7 -> 6; matrix products, arithmetic and copies ran while one was open for 0% -> 0% of each run, Pallas kernels for 20% -> 28%
where the time goes in v4:
time: 97.6 us; the launch traced here: 97.3 us
  Pallas kernels  47.5 us (49%)
  starting transfers between devices  34.7 us (36%)
  waiting for transfers between devices  14 us (14%)
    ppermute x1, starting transfers between devices, exchange(): lax.ppermute(pair, axis, even_odd(axis))  8.27 us
    ppermute x1, starting transfers between devices, far_hops(): lax.ppermute(sums, axis, [(i, (i + hop) % peers) for i in range(peers)])  7.59 us
    pallas_call x1, Pallas kernels, on_device(): call(pick_kernel, out_shape=shape((nx, tiles * ny, LANES), f32), in_specs...  6.53 us
    pallas_call x1, Pallas kernels, on_device(): call(early_kernel, out_shape=shape((count, LANES), f32), in_specs=[SMEM]...  6.38 us
    ppermute x2, starting transfers between devices, swap(): return (lax.ppermute(last, axis, up), lax.ppermute(leading, axis, down))  6.18 us
    pallas_call x1, Pallas kernels, on_device(): call(depart_kernel, out_shape=dom_message, in_specs=[HBM] * 3, out_specs=...  5.25 us
    ppermute x1, waiting for transfers between devices, on_device(): other_in = lax.ppermute(sent, 'slab', odd_even('slab', True))  4.97 us
    pallas_call x1, Pallas kernels, on_device(): call(functools.partial(surface_kernel, nz), out_shape=(kept, message, mes...  4.69 us
  transfers between devices with their start and end apart: 13, of which 6 were waited for; matrix products, arithmetic and copies ran while one was open for 0% of the time, Pallas kernels for 28%

profile of v4, /device:TPU:0, one launch (start us, length us, event | category | flops | bytes accessed | tf_op | source)
XLA Modules:
  0.0 97.3 jit_solution(10740197204916621919)
XLA Ops:
  0.7 5.2 %depart.1 = f32[288,128]{1,0:T(8,128)} custom-call(f32[128,128]{1,0:T(8,128)} %bitcast.14, s32[576,128]{1,0:T(8,128)} %bitcast.11, f32[8,8,512]{2,1,0:T(8,128)} %rigid.1), custom_call_target="tpu_custom_call" | custom-call | flops 2000000000 | tf_op jit(solution)/shard_map/depart/pallas_call | solution.py:849
  5.9 2.4 %collective-permute-start = (f32[288,128]{1,0:T(8,128)}, f32[288,128]{1,0:T(8,128)S(1)}, u32[]{:S(2)}, u32[]{:S(2)}) collective-permute-start(f32[288,128]{1,0:T(8,128)} %depart.1), channel_id=1, source_target_pairs={{0,8},{8,16},{16,24},{1,9},{9,17},{17,25},{2,10},{10,18},{18,26},{... | collective-permute-start | bytes 442376 | tf_op jit(solution)/shard_map/ppermute | solution.py:856
  8.4 3.9 %down.1 = (f32[288,128]{1,0:T(8,128)S(1)}, f32[8,32,128]{2,1,0:T(8,128)S(1)}) custom-call(f32[128,128]{1,0:T(8,128)S(1)} %bitcast.15, s32[576,128]{1,0:T(8,128)S(1)} %bitcast.12, f32[8,8,512]{2,1,0:T(8,128)S(1)} %copy-done.4), custom_call_target="tpu_custom_call" | custom-call | flops 1600000000 | tf_op jit(solution)/shard_map/down/pallas_call | solution.py:857
  12.2 0.0 copy-start
  12.2 0.0 copy-start.1
  12.2 1.4 %collective-permute-start.1 = (f32[288,128]{1,0:T(8,128)S(1)}, f32[288,128]{1,0:T(8,128)S(1)}, u32[]{:S(2)}, u32[]{:S(2)}) collective-permute-start(f32[288,128]{1,0:T(8,128)S(1)} %get-tuple-element.29), channel_id=1, source_target_pairs={{8,0},{16,8},{24,16},{9,1},{17,9},{25,17},{10,2},{18,10},{26,18},{... | collective-permute-start | bytes 442376 | tf_op jit(solution)/shard_map/ppermute | solution.py:861
  13.7 3.5 %near.1 = f32[192,128]{1,0:T(8,128)S(1)} custom-call(f32[128,128]{1,0:T(8,128)S(1)} %bitcast.16, s32[576,128]{1,0:T(8,128)S(1)} %bitcast.13), custom_call_target="tpu_custom_call" | custom-call | flops 1600000000 | tf_op jit(solution)/shard_map/near/pallas_call | solution.py:862
  17.2 0.1 stack.47.place.inside
  17.3 0.0 copy-done.1
  17.3 2.4 %plan.1.begun = s32[1024,128]{1,0:T(8,128)S(1)} custom-call(s32[7]{0:T(128)S(1)} %stack.47.place.inside, s32[4,8,8,512]{3,2,1,0:T(8,128)S(1)} %copy-done, s32[4,8,8,512]{3,2,1,0:T(8,128)S(1)} %copy-done.1), custom_call_target="tpu_custom_call" | custom-call | flops 1200000000 | tf_op jit(solution)/shard_map/plan/pallas_call | solution.py:866
  19.8 0.0 collective-permute-done.1.high.d_high
  19.8 0.0 collective-permute-done.low.d_low
  19.8 0.6 forward.1
  20.4 2.4 %collective-permute-start.2 = (f32[312,128]{1,0:T(8,128)S(1)}, f32[312,128]{1,0:T(8,128)S(1)}, u32[]{:S(2)}, u32[]{:S(2)}) collective-permute-start(f32[312,128]{1,0:T(8,128)S(1)} %get-tuple-element.34), channel_id=1, source_target_pairs={{0,1},{1,0},{2,3},{3,2},{4,5},{5,4},{6,7},{7,6},{8,9},{9,8},{10,11... | collective-permute-start | bytes 479240 | tf_op jit(solution)/shard_map/ppermute | solution.py:876
  22.7 2.6 %order.1 = (s32[1024,128]{1,0:T(8,128)S(1)}, s32[8,128]{1,0:T(8,128)S(1)}) custom-call(s32[7]{0:T(128)S(1)} %stack.47.place.inside, s32[1024,128]{1,0:T(8,128)S(1)} %plan.1.begun), custom_call_target="tpu_custom_call" | custom-call | flops 1200000000 | tf_op jit(solution)/shard_map/order/pallas_call | solution.py:877
  25.3 0.7 collective-permute-done.2.pair.d_pair
  26.0 0.7 collective-permute-start.3
  26.7 0.0 copy-start.2
  26.7 6.4 %early.1 = f32[1024,128]{1,0:T(8,128)S(1)} custom-call(s32[7]{0:T(128)S(1)} %stack.47.place.inside, f32[312,128]{1,0:T(8,128)S(1)} %collective-permute-done.2.pair.d_pair, f32[288,128]{1,0:T(8,128)S(1)} %collective-permute-done.low.d_low, f32[192,128]{1,0:T(8,128)S(1)} %near.1, f32[288,128]{1,0:T(8,128)S(1)} %collective-permute-done.1.high.d_high, ...), custom_call_target="tpu_custom_call" | custom-call | flops 1200000000 | tf_op jit(solution)/shard_map/early/pallas_call | solution.py:883
  33.1 0.0 collective-permute-done.3.other.d_other
  33.1 6.5 %pick.1.own = f32[8,32,128]{2,1,0:T(8,128)S(1)} custom-call(s32[7]{0:T(128)S(1)} %stack.47.place.inside, f32[312,128]{1,0:T(8,128)S(1)} %collective-permute-done.2.pair.d_pair, f32[312,128]{1,0:T(8,128)S(1)} %collective-permute-done.3.other.d_other, f32[288,128]{1,0:T(8,128)S(1)} %collective-permute-done.low.d_low, f32[192,128]{1,0:T(8,128)S(1)} %near.1, ...), custom_call_target="tpu_custom_call" | custom-call | flops 4800000000 | tf_op jit(solution)/shard_map/pick/pallas_call | solution.py:888
  39.6 4.9 %collective-permute-start.4 = (f32[5,32,128]{2,1,0:T(8,128)S(1)}, f32[5,32,128]{2,1,0:T(8,128)S(1)}, u32[]{:S(2)}, u32[]{:S(2)}) collective-permute-start(f32[5,32,128]{2,1,0:T(8,128)S(1)} %get-tuple-element.57), channel_id=1, source_target_pairs={{0,8},{8,16},{16,24},{1,9},{9,17},{17,25},{2,10},{10,18},{18,26},{... | collective-permute-start | bytes 245768 | tf_op jit(solution)/shard_map/ppermute | solution.py:795
  44.5 1.3 %collective-permute-start.5 = (f32[5,32,128]{2,1,0:T(8,128)S(1)}, f32[5,32,128]{2,1,0:T(8,128)S(1)}, u32[]{:S(2)}, u32[]{:S(2)}) collective-permute-start(f32[5,32,128]{2,1,0:T(8,128)S(1)} %get-tuple-element.56), channel_id=1, source_target_pairs={{8,0},{16,8},{24,16},{9,1},{17,9},{25,17},{10,2},{18,10},{26,18},{... | collective-permute-start | bytes 245768 | tf_op jit(solution)/shard_map/ppermute | solution.py:795
  45.8 0.0 collective-permute-done.4.low.p_low
  45.9 3.8 %collective-permute-done.5.high.p_high = f32[5,32,128]{2,1,0:T(8,128)S(1)} collective-permute-done((f32[5,32,128]{2,1,0:T(8,128)S(1)}, f32[5,32,128]{2,1,0:T(8,128)S(1)}, u32[]{:S(2)}, u32[]{:S(2)}) %collective-permute-start.5) | collective-permute-done | bytes 81952 | tf_op jit(solution)/shard_map/ppermute | solution.py:795
  49.7 0.6 pack.1
  50.3 8.3 %collective-permute-start.6 = (f32[240,128]{1,0:T(8,128)S(1)}, f32[240,128]{1,0:T(8,128)S(1)}, u32[]{:S(2)}, u32[]{:S(2)}) collective-permute-start(f32[240,128]{1,0:T(8,128)S(1)} %get-tuple-element.40), channel_id=1, source_target_pairs={{0,1},{1,0},{2,3},{3,2},{4,5},{5,4},{6,7},{7,6},{8,9},{9,8},{10,11... | collective-permute-start | bytes 368648 | tf_op jit(solution)/shard_map/ppermute | solution.py:813
  58.6 0.8 collective-permute-start.7
  59.4 2.1 %collective-permute-done.6.p_pair = f32[240,128]{1,0:T(8,128)S(1)} collective-permute-done((f32[240,128]{1,0:T(8,128)S(1)}, f32[240,128]{1,0:T(8,128)S(1)}, u32[]{:S(2)}, u32[]{:S(2)}) %collective-permute-start.6) | collective-permute-done | bytes 122912 | tf_op jit(solution)/shard_map/ppermute | solution.py:813
  61.4 0.0 collective-permute-done.7.p_other
  61.4 4.4 %krylov.1 = (f32[12,256,128]{2,1,0:T(8,128)S(1)}, f32[8,128]{1,0:T(8,128)S(1)}) custom-call(s32[7]{0:T(128)S(1)} %stack.47.place.inside, f32[8,32,128]{2,1,0:T(8,128)S(1)} %pick.1.own, f32[5,32,128]{2,1,0:T(8,128)S(1)} %collective-permute-done.4.low.p_low, f32[5,32,128]{2,1,0:T(8,128)S(1)} %collective-permute-done.5.high.p_high, ...), custom_call_target="tpu_custom_call" | custom-call | flops 2800000000 | tf_op jit(solution)/shard_map/krylov/pallas_call | solution.py:902
  65.8 7.6 %collective-permute-start.8 = (f32[8,128]{1,0:T(8,128)S(1)}, f32[8,128]{1,0:T(8,128)S(1)}, u32[]{:S(2)}, u32[]{:S(2)}) collective-permute-start(f32[8,128]{1,0:T(8,128)S(1)} %get-tuple-element.45), channel_id=1, source_target_pairs={{0,4},{1,5},{2,6},{3,7},{4,0},{5,1},{6,2},{7,3},{8,12},{9,13},{10,... | collective-permute-start | bytes 12296 | tf_op jit(solution)/shard_map/ppermute | solution.py:820
  73.4 4.7 %surface.1 = (f32[40,128]{1,0:T(8,128)S(1)}, f32[48,128]{1,0:T(8,128)S(1)}, f32[48,128]{1,0:T(8,128)S(1)}) custom-call(s32[1,9]{1,0:T(1,128)S(1)} %copy-done.8, s32[7]{0:T(128)S(1)} %stack.47.place.inside, f32[12,256,128]{2,1,0:T(8,128)S(1)} %get-tuple-element.50.basis, s32[9,1,128]{2,1,0:T(1,128)S(1)} %bitcast.17), custom_call_target="tpu_custom_call" | custom-call | flops 1600000000 | tf_op jit(solution)/shard_map/surface/pallas_call | solution.py:915
  78.1 0.0 collective-permute-done.8
  78.1 1.4 %collective-permute-start.9 = (f32[48,128]{1,0:T(8,128)S(1)}, f32[48,128]{1,0:T(8,128)S(1)}, u32[]{:S(2)}, u32[]{:S(2)}) collective-permute-start(f32[48,128]{1,0:T(8,128)S(1)} %get-tuple-element.54), channel_id=1, source_target_pairs={{0,8},{8,0},{16,24},{24,16},{1,9},{9,1},{17,25},{25,17},{2,10},{10... | collective-permute-start | bytes 73736 | tf_op jit(solution)/shard_map/ppermute | solution.py:827
  79.6 0.8 collective-permute-done.9.pair_in
  80.4 1.6 %collective-permute-start.10 = (f32[48,128]{1,0:T(8,128)S(1)}, f32[48,128]{1,0:T(8,128)S(1)}, u32[]{:S(2)}, u32[]{:S(2)}) collective-permute-start(f32[48,128]{1,0:T(8,128)S(1)} %fusion.1.sent), channel_id=1, source_target_pairs={{0,24},{8,16},{16,8},{24,0},{1,25},{9,17},{17,9},{25,1},{2,26},{10... | collective-permute-start | bytes 73736 | tf_op jit(solution)/shard_map/ppermute | solution.py:829
  82.1 1.6 %collective-permute-done.10.other_in = f32[48,128]{1,0:T(8,128)S(1)} collective-permute-done((f32[48,128]{1,0:T(8,128)S(1)}, f32[48,128]{1,0:T(8,128)S(1)}, u32[]{:S(2)}, u32[]{:S(2)}) %collective-permute-start.10) | collective-permute-done | bytes 24608 | tf_op jit(solution)/shard_map/ppermute | solution.py:829
  83.7 0.6 route.1
  84.3 0.0 copy-start.7
  84.3 0.4 collective-permute-start.11
  84.7 3.5 %plain.1.basis = f32[12,8,8,512]{3,2,1,0:T(8,128)S(1)} custom-call(f32[12,256,128]{2,1,0:T(8,128)S(1)} %get-tuple-element.50.basis), custom_call_target="tpu_custom_call" | custom-call | flops 1200000000 | tf_op jit(solution)/shard_map/plain/pallas_call | solution.py:920
  88.2 0.0 collective-permute-done.11.pair
  88.2 1.5 %collective-permute-start.12 = (f32[48,128]{1,0:T(8,128)S(1)}, f32[48,128]{1,0:T(8,128)S(1)}, u32[]{:S(2)}, u32[]{:S(2)}) collective-permute-start(f32[48,128]{1,0:T(8,128)S(1)} %fusion.sent), channel_id=1, source_target_pairs={{0,7},{1,2},{2,1},{3,4},{4,3},{5,6},{6,5},{7,0},{8,15},{9,10},{10,... | collective-permute-start | bytes 73736 | tf_op jit(solution)/shard_map/ppermute | solution.py:934
  89.7 0.0 copy-done.7
  89.7 0.1 hot.1
  89.9 5.0 %collective-permute-done.12.other = f32[48,128]{1,0:T(8,128)S(1)} collective-permute-done((f32[48,128]{1,0:T(8,128)S(1)}, f32[48,128]{1,0:T(8,128)S(1)}, u32[]{:S(2)}, u32[]{:S(2)}) %collective-permute-start.12) | collective-permute-done | bytes 24608 | tf_op jit(solution)/shard_map/ppermute | solution.py:934
  94.8 2.5 %finish.1 = (f32[3,8,8,512]{3,2,1,0:T(8,128)}, f32[3,16384]{1,0:T(4,128)}) custom-call(s32[7]{0:T(128)S(1)} %stack.47.place.inside, f32[40,128]{1,0:T(8,128)S(1)} %get-tuple-element.47.keep, f32[48,128]{1,0:T(8,128)S(1)} %collective-permute-done.11.pair, f32[48,128]{1,0:T(8,128)S(1)} %fusion.sent, f32[48,128]{1,0:T(8,128)S(1)} %collective-permute-done.12.other, ...), custom_call_target="tpu_custom_call" | custom-call | flops 800000000 | tf_op jit(solution)/shard_map/finish/pallas_call | solution.py:935
  (16 shorter events, 0.1 us)
Async XLA Ops:
  0.6 7.7 %copy-start.3 = (s32[1,3,3,8192]{3,0,2,1:T(1,128)S(1)}, s32[1,3,3,8192]{3,0,2,1:T(1,128)}, u32[]{:S(2)}) copy-start(s32[1,3,3,8192]{3,0,2,1:T(1,128)} %param.10) | copy-start | bytes 884740
  0.6 7.7 %copy-start.4 = (f32[8,8,512]{2,1,0:T(8,128)S(1)}, f32[8,8,512]{2,1,0:T(8,128)}, u32[]{:S(2)}) copy-start(f32[8,8,512]{2,1,0:T(8,128)} %rigid.1) | copy-start | bytes 393220
  0.6 7.7 %copy-start.5 = (f32[16384]{0:T(1024)S(1)}, f32[16384]{0:T(1024)}, u32[]{:S(2)}) copy-start(f32[16384]{0:T(1024)} %param.9) | copy-start | bytes 196612
  5.9 13.8 %collective-permute-start = (f32[288,128]{1,0:T(8,128)}, f32[288,128]{1,0:T(8,128)S(1)}, u32[]{:S(2)}, u32[]{:S(2)}) collective-permute-start(f32[288,128]{1,0:T(8,128)} %depart.1), channel_id=1, source_target_pairs={{0,8},{8,16},{16,24},{1,9},{9,17},{17,25},{2,10},{10,18},{18,26},{... | collective-permute-start | bytes 442376 | tf_op jit(solution)/shard_map/ppermute | solution.py:856
  12.2 5.1 %copy-start = (s32[4,8,8,512]{3,2,1,0:T(8,128)S(1)}, s32[4,8,8,512]{3,2,1,0:T(8,128)}, u32[]{:S(2)}) copy-start(s32[4,8,8,512]{3,2,1,0:T(8,128)} %shift) | copy-start | bytes 1572868
  12.2 5.1 %copy-start.1 = (s32[4,8,8,512]{3,2,1,0:T(8,128)S(1)}, s32[4,8,8,512]{3,2,1,0:T(8,128)}, u32[]{:S(2)}) copy-start(s32[4,8,8,512]{3,2,1,0:T(8,128)} %bucket.1) | copy-start | bytes 1572868
  12.2 7.5 %collective-permute-start.1 = (f32[288,128]{1,0:T(8,128)S(1)}, f32[288,128]{1,0:T(8,128)S(1)}, u32[]{:S(2)}, u32[]{:S(2)}) collective-permute-start(f32[288,128]{1,0:T(8,128)S(1)} %get-tuple-element.29), channel_id=1, source_target_pairs={{8,0},{16,8},{24,16},{9,1},{17,9},{25,17},{10,2},{18,10},{26,18},{... | collective-permute-start | bytes 442376 | tf_op jit(solution)/shard_map/ppermute | solution.py:861
  20.4 5.6 %collective-permute-start.2 = (f32[312,128]{1,0:T(8,128)S(1)}, f32[312,128]{1,0:T(8,128)S(1)}, u32[]{:S(2)}, u32[]{:S(2)}) collective-permute-start(f32[312,128]{1,0:T(8,128)S(1)} %get-tuple-element.34), channel_id=1, source_target_pairs={{0,1},{1,0},{2,3},{3,2},{4,5},{5,4},{6,7},{7,6},{8,9},{9,8},{10,11... | collective-permute-start | bytes 479240 | tf_op jit(solution)/shard_map/ppermute | solution.py:876
  26.0 7.1 %collective-permute-start.3 = (f32[312,128]{1,0:T(8,128)S(1)}, f32[312,128]{1,0:T(8,128)S(1)}, u32[]{:S(2)}, u32[]{:S(2)}) collective-permute-start(f32[312,128]{1,0:T(8,128)S(1)} %get-tuple-element.38), channel_id=1, source_target_pairs={{1,2},{2,1},{3,4},{4,3},{5,6},{6,5},{9,10},{10,9},{11,12},{12,11},... | collective-permute-start | bytes 479240 | tf_op jit(solution)/shard_map/ppermute | solution.py:882
  26.7 6.4 %copy-start.2 = (f32[4,8,8,512]{3,2,1,0:T(8,128)S(1)}, f32[4,8,8,512]{3,2,1,0:T(8,128)}, u32[]{:S(2)}) copy-start(f32[4,8,8,512]{3,2,1,0:T(8,128)} %factor.1) | copy-start | bytes 1572868
  39.6 6.2 %collective-permute-start.4 = (f32[5,32,128]{2,1,0:T(8,128)S(1)}, f32[5,32,128]{2,1,0:T(8,128)S(1)}, u32[]{:S(2)}, u32[]{:S(2)}) collective-permute-start(f32[5,32,128]{2,1,0:T(8,128)S(1)} %get-tuple-element.57), channel_id=1, source_target_pairs={{0,8},{8,16},{16,24},{1,9},{9,17},{17,25},{2,10},{10,18},{18,26},{... | collective-permute-start | bytes 245768 | tf_op jit(solution)/shard_map/ppermute | solution.py:795
  44.5 5.2 %collective-permute-start.5 = (f32[5,32,128]{2,1,0:T(8,128)S(1)}, f32[5,32,128]{2,1,0:T(8,128)S(1)}, u32[]{:S(2)}, u32[]{:S(2)}) collective-permute-start(f32[5,32,128]{2,1,0:T(8,128)S(1)} %get-tuple-element.56), channel_id=1, source_target_pairs={{8,0},{16,8},{24,16},{9,1},{17,9},{25,17},{10,2},{18,10},{26,18},{... | collective-permute-start | bytes 245768 | tf_op jit(solution)/shard_map/ppermute | solution.py:795
  50.3 11.1 %collective-permute-start.6 = (f32[240,128]{1,0:T(8,128)S(1)}, f32[240,128]{1,0:T(8,128)S(1)}, u32[]{:S(2)}, u32[]{:S(2)}) collective-permute-start(f32[240,128]{1,0:T(8,128)S(1)} %get-tuple-element.40), channel_id=1, source_target_pairs={{0,1},{1,0},{2,3},{3,2},{4,5},{5,4},{6,7},{7,6},{8,9},{9,8},{10,11... | collective-permute-start | bytes 368648 | tf_op jit(solution)/shard_map/ppermute | solution.py:813
  58.6 14.8 %copy-start.6 = (s32[1,3,3,128]{3,0,2,1:T(1,128)S(1)}, s32[1,3,3,128]{3,0,2,1:T(1,128)}, u32[]{:S(2)}) copy-start(s32[1,3,3,128]{3,0,2,1:T(1,128)} %param.15) | copy-start | bytes 13828
  58.6 14.8 %copy-start.8 = (s32[1,9]{1,0:T(1,128)S(1)}, s32[1,9]{1,0:T(1,128)}, u32[]{:S(2)}) copy-start(s32[1,9]{1,0:T(1,128)} %tally.1) | copy-start | bytes 112
  58.6 2.9 %collective-permute-start.7 = (f32[240,128]{1,0:T(8,128)S(1)}, f32[240,128]{1,0:T(8,128)S(1)}, u32[]{:S(2)}, u32[]{:S(2)}) collective-permute-start(f32[240,128]{1,0:T(8,128)S(1)} %get-tuple-element.41), channel_id=1, source_target_pairs={{1,2},{2,1},{3,4},{4,3},{5,6},{6,5},{9,10},{10,9},{11,12},{12,11},... | collective-permute-start | bytes 368648 | tf_op jit(solution)/shard_map/ppermute | solution.py:813
  65.8 12.3 %collective-permute-start.8 = (f32[8,128]{1,0:T(8,128)S(1)}, f32[8,128]{1,0:T(8,128)S(1)}, u32[]{:S(2)}, u32[]{:S(2)}) collective-permute-start(f32[8,128]{1,0:T(8,128)S(1)} %get-tuple-element.45), channel_id=1, source_target_pairs={{0,4},{1,5},{2,6},{3,7},{4,0},{5,1},{6,2},{7,3},{8,12},{9,13},{10,... | collective-permute-start | bytes 12296 | tf_op jit(solution)/shard_map/ppermute | solution.py:820
  78.1 2.3 %collective-permute-start.9 = (f32[48,128]{1,0:T(8,128)S(1)}, f32[48,128]{1,0:T(8,128)S(1)}, u32[]{:S(2)}, u32[]{:S(2)}) collective-permute-start(f32[48,128]{1,0:T(8,128)S(1)} %get-tuple-element.54), channel_id=1, source_target_pairs={{0,8},{8,0},{16,24},{24,16},{1,9},{9,1},{17,25},{25,17},{2,10},{10... | collective-permute-start | bytes 73736 | tf_op jit(solution)/shard_map/ppermute | solution.py:827
  80.4 3.3 %collective-permute-start.10 = (f32[48,128]{1,0:T(8,128)S(1)}, f32[48,128]{1,0:T(8,128)S(1)}, u32[]{:S(2)}, u32[]{:S(2)}) collective-permute-start(f32[48,128]{1,0:T(8,128)S(1)} %fusion.1.sent), channel_id=1, source_target_pairs={{0,24},{8,16},{16,8},{24,0},{1,25},{9,17},{17,9},{25,1},{2,26},{10... | collective-permute-start | bytes 73736 | tf_op jit(solution)/shard_map/ppermute | solution.py:829
  84.3 5.5 %copy-start.7 = (s32[1,3,3,128]{3,0,2,1:T(1,128)S(1)}, s32[1,3,3,128]{3,0,2,1:T(1,128)}, u32[]{:S(2)}) copy-start(s32[1,3,3,128]{3,0,2,1:T(1,128)} %param.17) | copy-start | bytes 13828
  84.3 3.9 %collective-permute-start.11 = (f32[48,128]{1,0:T(8,128)S(1)}, f32[48,128]{1,0:T(8,128)S(1)}, u32[]{:S(2)}, u32[]{:S(2)}) collective-permute-start(f32[48,128]{1,0:T(8,128)S(1)} %get-tuple-element.48), channel_id=1, source_target_pairs={{0,1},{1,0},{2,3},{3,2},{4,5},{5,4},{6,7},{7,6},{8,9},{9,8},{10,11... | collective-permute-start | bytes 73736 | tf_op jit(solution)/shard_map/ppermute | solution.py:932
  88.2 6.6 %collective-permute-start.12 = (f32[48,128]{1,0:T(8,128)S(1)}, f32[48,128]{1,0:T(8,128)S(1)}, u32[]{:S(2)}, u32[]{:S(2)}) collective-permute-start(f32[48,128]{1,0:T(8,128)S(1)} %fusion.sent), channel_id=1, source_target_pairs={{0,7},{1,2},{2,1},{3,4},{4,3},{5,6},{6,5},{7,0},{8,15},{9,10},{10,... | collective-permute-start | bytes 73736 | tf_op jit(solution)/shard_map/ppermute | solution.py:934

commit v5 on v4

--- a/solution.py
+++ b/solution.py
@@ -264,27 +264,30 @@
 def visit(table, keys, bounds, soon, before, store):
     count = keys.shape[0] // SUB
     pos_bits = int(math.log2(count * SUB))
-    depth = int(math.log2(CHUNK))
     per = count // SUB
 
     def body(s, carry):
         own = [keys[pl.ds(SUB * SUB * g + s, SUB, stride=SUB), :] for g in range(per)]
         start = [bounds[s, g] for g in range(per)]
 
-        def step(n, found):
+        def step(offset, chunk, found):
+            depth = int(math.log2(chunk))
             fresh = []
             for g in range(per):
                 lanes = (own[g] >> pos_bits) & (LANES - 1)
-                first = start[g] + n * CHUNK
+                first = start[g] + offset
                 rel = (own[g] >> (pos_bits + 7)) - first
                 bits = [((rel >> b) & 1) == 1 for b in range(depth)]
-                fresh.append(jnp.where((rel >> depth) == 0, lookup(table, first, CHUNK, lanes, bits), found[g]))
+                fresh.append(jnp.where((rel >> depth) == 0, lookup(table, first, chunk, lanes, bits), found[g]))
             return tuple(fresh)
 
         spots = [pl.ds(SUB * SUB * g + s, SUB, stride=SUB) for g in range(per)]
         least = 0 if soon else bounds[s, LANES - 2]
         most = bounds[s, LANES - 2 if soon else LANES - 1]
-        found = lax.fori_loop(least, most, step, tuple(before(at) for at in spots))
+        twos = (most - least) // 2
+        found = tuple(before(at) for at in spots)
+        found = lax.fori_loop(0, twos, lambda n, f: step((least + 2 * n) * CHUNK, 2 * CHUNK, f), found)
+        found = lax.fori_loop(least + 2 * twos, most, lambda n, f: step(n * CHUNK, CHUNK, f), found)
         for g, at in enumerate(spots):
             store(at, found[g], own[g] & (count * SUB - 1))
         return carry
@@ -302,7 +305,7 @@
             out[pl.ds(base + SUB * k, SUB), :] = found[k]
         return carry
 
-    lax.fori_loop(0, rows // group, body, 0)
+    lax.fori_loop(0, rows // group, body, 0, unroll=True)
 
 
 def depart_kernel(heat_hbm, picks_hbm, rigid_hbm, up, heat, picks, rigid, arrived):
@@ -521,7 +524,7 @@
                 u0[2, t, x, pl.ds(part * SUB, SUB), :] = scale * (along[t][1] - along[t][0])
         return carry
 
-    lax.fori_loop(1, nx + 2 * REACH - 1, load_row, 0, unroll=2)
+    lax.fori_loop(1, nx + 2 * REACH - 1, load_row, 0, unroll=4 if nx == SUB else 1)
 
     def twice(ref, c, x, part):
         coefficient = (2.0 / HALF) * mask(x, part)
@@ -550,7 +553,7 @@
             return carry
 
         margin = ITERS - order
-        lax.fori_loop(REACH - margin, REACH + nx + margin, apply_row, 0, unroll=2)
+        lax.fori_loop(REACH - margin, REACH + nx + margin, apply_row, 0, unroll=(2, 4, 5)[order - 1] if nx == SUB else 1)
 
     def dots_row(x, carry):
         carry = list(carry)
@@ -567,7 +570,7 @@
                     basis[3 * j + c, pl.ds(pl.multiple_of(t * nx * SUB + x * SUB, SUB), SUB), :] = v[j]
         return tuple(carry)
 
-    totals = lax.fori_loop(0, nx, dots_row, tuple(zero for _ in range(8)), unroll=2)
+    totals = lax.fori_loop(0, nx, dots_row, tuple(zero for _ in range(8)), unroll=4 if nx == SUB else 1)
     for k in range(8):
         sums[pl.ds(k, 1), :] = jnp.sum(totals[k], axis=0, keepdims=True)
 
@@ -616,7 +619,7 @@
         give(f, values)
         return carry
 
-    lax.fori_loop(0, fields, body, 0, unroll=3)
+    lax.fori_loop(0, fields, body, 0, unroll=4)
 
 
 def route_kernel(place, kept, pair_in, sent, other_in, keep, pair, other):
@@ -704,7 +707,7 @@
                 plain[f, x, :, pl.ds(t * LANES, LANES)] = value
         return carry
 
-    lax.fori_loop(0, nx, row, 0)
+    lax.fori_loop(0, nx, row, 0, unroll=2)
 
 
 def hot_kernel(picks, row_hot, lane_hot):
@@ -781,7 +784,7 @@
     half = nx // 2
     for k in range(2):
         at = pl.ds(k * half, half)
-        lax.fori_loop(k * half, (k + 1) * half, row, 0)
+        lax.fori_loop(k * half, (k + 1) * half, row, 0, unroll=2)
         copies.append(pltpu.make_async_copy(disp.at[:, at], disp_hbm.at[:, at], left.at[1 + k]))
         copies[-1].start()
     for copy in copies:

time: 97.6 us -> 95.9 us (0.983)
  starting transfers between devices: 34.7 us -> 33.4 us
  Pallas kernels: 47.5 us -> 46.2 us
  transfers between devices with their start and end apart: 13 -> 13, of which waited for: 6 -> 7; matrix products, arithmetic and copies ran while one was open for 0% -> 0% of each run, Pallas kernels for 28% -> 27%
where the time goes in v5:
time: 95.9 us; the launch traced here: 95.6 us
  Pallas kernels  46.2 us (48%)
  starting transfers between devices  33.4 us (35%)
  waiting for transfers between devices  14.7 us (15%)
  between operations  1.1 us (1%)
    ppermute x1, starting transfers between devices, exchange(): lax.ppermute(pair, axis, even_odd(axis))  7.69 us
    ppermute x1, starting transfers between devices, far_hops(): lax.ppermute(sums, axis, [(i, (i + hop) % peers) for i in range(peers)])  7.59 us
    pallas_call x1, Pallas kernels, on_device(): call(pick_kernel, out_shape=shape((nx, tiles * ny, LANES), f32), in_specs...  6.75 us
    pallas_call x1, Pallas kernels, on_device(): call(early_kernel, out_shape=shape((count, LANES), f32), in_specs=[SMEM]...  6.07 us
    ppermute x2, starting transfers between devices, swap(): return (lax.ppermute(last, axis, up), lax.ppermute(leading, axis, down))  5.83 us
    pallas_call x1, Pallas kernels, on_device(): call(depart_kernel, out_shape=dom_message, in_specs=[HBM] * 3, out_specs=...  5.1 us
    ppermute x1, waiting for transfers between devices, on_device(): other_in = lax.ppermute(sent, 'slab', odd_even('slab', True))  5.09 us
    pallas_call x1, Pallas kernels, on_device(): call(functools.partial(surface_kernel, nz), out_shape=(kept, message, mes...  4.64 us
  transfers between devices with their start and end apart: 13, of which 7 were waited for; matrix products, arithmetic and copies ran while one was open for 0% of the time, Pallas kernels for 27%

profile of v5, /device:TPU:0, one launch (start us, length us, event | category | flops | bytes accessed | tf_op | source)
XLA Modules:
  0.0 95.6 jit_solution(4246927254392528530)
XLA Ops:
  0.7 5.1 %depart.1 = f32[288,128]{1,0:T(8,128)} custom-call(f32[128,128]{1,0:T(8,128)} %bitcast.14, s32[576,128]{1,0:T(8,128)} %bitcast.11, f32[8,8,512]{2,1,0:T(8,128)} %rigid.1), custom_call_target="tpu_custom_call" | custom-call | flops 2000000000 | tf_op jit(solution)/shard_map/depart/pallas_call | solution.py:852
  5.8 2.4 %collective-permute-start = (f32[288,128]{1,0:T(8,128)}, f32[288,128]{1,0:T(8,128)S(1)}, u32[]{:S(2)}, u32[]{:S(2)}) collective-permute-start(f32[288,128]{1,0:T(8,128)} %depart.1), channel_id=1, source_target_pairs={{0,8},{8,16},{16,24},{1,9},{9,17},{17,25},{2,10},{10,18},{18,26},{... | collective-permute-start | bytes 442376 | tf_op jit(solution)/shard_map/ppermute | solution.py:859
  8.2 0.0 copy-done.3
  8.2 0.0 copy-done.4
  8.2 3.6 %down.1 = (f32[288,128]{1,0:T(8,128)S(1)}, f32[8,32,128]{2,1,0:T(8,128)S(1)}) custom-call(f32[128,128]{1,0:T(8,128)S(1)} %bitcast.15, s32[576,128]{1,0:T(8,128)S(1)} %bitcast.12, f32[8,8,512]{2,1,0:T(8,128)S(1)} %copy-done.4), custom_call_target="tpu_custom_call" | custom-call | flops 1600000000 | tf_op jit(solution)/shard_map/down/pallas_call | solution.py:860
  11.8 0.0 copy-start
  11.9 0.0 copy-start.1
  11.9 1.4 %collective-permute-start.1 = (f32[288,128]{1,0:T(8,128)S(1)}, f32[288,128]{1,0:T(8,128)S(1)}, u32[]{:S(2)}, u32[]{:S(2)}) collective-permute-start(f32[288,128]{1,0:T(8,128)S(1)} %get-tuple-element.29), channel_id=1, source_target_pairs={{8,0},{16,8},{24,16},{9,1},{17,9},{25,17},{10,2},{18,10},{26,18},{... | collective-permute-start | bytes 442376 | tf_op jit(solution)/shard_map/ppermute | solution.py:864
  13.3 3.4 %near.1 = f32[192,128]{1,0:T(8,128)S(1)} custom-call(f32[128,128]{1,0:T(8,128)S(1)} %bitcast.16, s32[576,128]{1,0:T(8,128)S(1)} %bitcast.13), custom_call_target="tpu_custom_call" | custom-call | flops 1600000000 | tf_op jit(solution)/shard_map/near/pallas_call | solution.py:865
  16.7 0.1 stack.47.place.inside
  16.8 2.4 %plan.1.begun = s32[1024,128]{1,0:T(8,128)S(1)} custom-call(s32[7]{0:T(128)S(1)} %stack.47.place.inside, s32[4,8,8,512]{3,2,1,0:T(8,128)S(1)} %copy-done, s32[4,8,8,512]{3,2,1,0:T(8,128)S(1)} %copy-done.1), custom_call_target="tpu_custom_call" | custom-call | flops 1200000000 | tf_op jit(solution)/shard_map/plan/pallas_call | solution.py:869
  19.2 0.0 collective-permute-done.1.high.d_high
  19.2 0.0 collective-permute-done.low.d_low
  19.2 0.6 forward.1
  19.8 2.4 %collective-permute-start.2 = (f32[312,128]{1,0:T(8,128)S(1)}, f32[312,128]{1,0:T(8,128)S(1)}, u32[]{:S(2)}, u32[]{:S(2)}) collective-permute-start(f32[312,128]{1,0:T(8,128)S(1)} %get-tuple-element.34), channel_id=1, source_target_pairs={{0,1},{1,0},{2,3},{3,2},{4,5},{5,4},{6,7},{7,6},{8,9},{9,8},{10,11... | collective-permute-start | bytes 479240 | tf_op jit(solution)/shard_map/ppermute | solution.py:879
  22.2 2.6 %order.1 = (s32[1024,128]{1,0:T(8,128)S(1)}, s32[8,128]{1,0:T(8,128)S(1)}) custom-call(s32[7]{0:T(128)S(1)} %stack.47.place.inside, s32[1024,128]{1,0:T(8,128)S(1)} %plan.1.begun), custom_call_target="tpu_custom_call" | custom-call | flops 1200000000 | tf_op jit(solution)/shard_map/order/pallas_call | solution.py:880
  24.8 0.7 collective-permute-done.2.pair.d_pair
  25.5 0.7 collective-permute-start.3
  26.1 0.0 copy-start.2
  26.1 6.1 %early.1 = f32[1024,128]{1,0:T(8,128)S(1)} custom-call(s32[7]{0:T(128)S(1)} %stack.47.place.inside, f32[312,128]{1,0:T(8,128)S(1)} %collective-permute-done.2.pair.d_pair, f32[288,128]{1,0:T(8,128)S(1)} %collective-permute-done.low.d_low, f32[192,128]{1,0:T(8,128)S(1)} %near.1, f32[288,128]{1,0:T(8,128)S(1)} %collective-permute-done.1.high.d_high, ...), custom_call_target="tpu_custom_call" | custom-call | flops 1200000000 | tf_op jit(solution)/shard_map/early/pallas_call | solution.py:886
  32.2 0.0 collective-permute-done.3.other.d_other
  32.2 6.8 %pick.1.own = f32[8,32,128]{2,1,0:T(8,128)S(1)} custom-call(s32[7]{0:T(128)S(1)} %stack.47.place.inside, f32[312,128]{1,0:T(8,128)S(1)} %collective-permute-done.2.pair.d_pair, f32[312,128]{1,0:T(8,128)S(1)} %collective-permute-done.3.other.d_other, f32[288,128]{1,0:T(8,128)S(1)} %collective-permute-done.low.d_low, f32[192,128]{1,0:T(8,128)S(1)} %near.1, ...), custom_call_target="tpu_custom_call" | custom-call | flops 4800000000 | tf_op jit(solution)/shard_map/pick/pallas_call | solution.py:891
  39.0 4.5 %collective-permute-start.4 = (f32[5,32,128]{2,1,0:T(8,128)S(1)}, f32[5,32,128]{2,1,0:T(8,128)S(1)}, u32[]{:S(2)}, u32[]{:S(2)}) collective-permute-start(f32[5,32,128]{2,1,0:T(8,128)S(1)} %get-tuple-element.57), channel_id=1, source_target_pairs={{0,8},{8,16},{16,24},{1,9},{9,17},{17,25},{2,10},{10,18},{18,26},{... | collective-permute-start | bytes 245768 | tf_op jit(solution)/shard_map/ppermute | solution.py:798
  43.6 1.3 %collective-permute-start.5 = (f32[5,32,128]{2,1,0:T(8,128)S(1)}, f32[5,32,128]{2,1,0:T(8,128)S(1)}, u32[]{:S(2)}, u32[]{:S(2)}) collective-permute-start(f32[5,32,128]{2,1,0:T(8,128)S(1)} %get-tuple-element.56), channel_id=1, source_target_pairs={{8,0},{16,8},{24,16},{9,1},{17,9},{25,17},{10,2},{18,10},{26,18},{... | collective-permute-start | bytes 245768 | tf_op jit(solution)/shard_map/ppermute | solution.py:798
  44.9 0.0 collective-permute-done.4.low.p_low
  44.9 4.0 %collective-permute-done.5.high.p_high = f32[5,32,128]{2,1,0:T(8,128)S(1)} collective-permute-done((f32[5,32,128]{2,1,0:T(8,128)S(1)}, f32[5,32,128]{2,1,0:T(8,128)S(1)}, u32[]{:S(2)}, u32[]{:S(2)}) %collective-permute-start.5) | collective-permute-done | bytes 81952 | tf_op jit(solution)/shard_map/ppermute | solution.py:798
  48.9 0.6 pack.1
  49.5 7.7 %collective-permute-start.6 = (f32[240,128]{1,0:T(8,128)S(1)}, f32[240,128]{1,0:T(8,128)S(1)}, u32[]{:S(2)}, u32[]{:S(2)}) collective-permute-start(f32[240,128]{1,0:T(8,128)S(1)} %get-tuple-element.40), channel_id=1, source_target_pairs={{0,1},{1,0},{2,3},{3,2},{4,5},{5,4},{6,7},{7,6},{8,9},{9,8},{10,11... | collective-permute-start | bytes 368648 | tf_op jit(solution)/shard_map/ppermute | solution.py:816
  57.1 0.8 collective-permute-start.7
  57.9 2.1 %collective-permute-done.6.p_pair = f32[240,128]{1,0:T(8,128)S(1)} collective-permute-done((f32[240,128]{1,0:T(8,128)S(1)}, f32[240,128]{1,0:T(8,128)S(1)}, u32[]{:S(2)}, u32[]{:S(2)}) %collective-permute-start.6) | collective-permute-done | bytes 122912 | tf_op jit(solution)/shard_map/ppermute | solution.py:816
  60.0 0.0 collective-permute-done.7.p_other
  60.0 4.1 %krylov.1 = (f32[12,256,128]{2,1,0:T(8,128)S(1)}, f32[8,128]{1,0:T(8,128)S(1)}) custom-call(s32[7]{0:T(128)S(1)} %stack.47.place.inside, f32[8,32,128]{2,1,0:T(8,128)S(1)} %pick.1.own, f32[5,32,128]{2,1,0:T(8,128)S(1)} %collective-permute-done.4.low.p_low, f32[5,32,128]{2,1,0:T(8,128)S(1)} %collective-permute-done.5.high.p_high, ...), custom_call_target="tpu_custom_call" | custom-call | flops 2800000000 | tf_op jit(solution)/shard_map/krylov/pallas_call | solution.py:905
  64.1 7.6 %collective-permute-start.8 = (f32[8,128]{1,0:T(8,128)S(1)}, f32[8,128]{1,0:T(8,128)S(1)}, u32[]{:S(2)}, u32[]{:S(2)}) collective-permute-start(f32[8,128]{1,0:T(8,128)S(1)} %get-tuple-element.45), channel_id=1, source_target_pairs={{0,4},{1,5},{2,6},{3,7},{4,0},{5,1},{6,2},{7,3},{8,12},{9,13},{10,... | collective-permute-start | bytes 12296 | tf_op jit(solution)/shard_map/ppermute | solution.py:823
  71.7 4.6 %surface.1 = (f32[40,128]{1,0:T(8,128)S(1)}, f32[48,128]{1,0:T(8,128)S(1)}, f32[48,128]{1,0:T(8,128)S(1)}) custom-call(s32[1,9]{1,0:T(1,128)S(1)} %copy-done.8, s32[7]{0:T(128)S(1)} %stack.47.place.inside, f32[12,256,128]{2,1,0:T(8,128)S(1)} %get-tuple-element.50.basis, s32[9,1,128]{2,1,0:T(1,128)S(1)} %bitcast.17), custom_call_target="tpu_custom_call" | custom-call | flops 1600000000 | tf_op jit(solution)/shard_map/surface/pallas_call | solution.py:918
  76.4 0.0 collective-permute-done.8
  76.4 1.4 %collective-permute-start.9 = (f32[48,128]{1,0:T(8,128)S(1)}, f32[48,128]{1,0:T(8,128)S(1)}, u32[]{:S(2)}, u32[]{:S(2)}) collective-permute-start(f32[48,128]{1,0:T(8,128)S(1)} %get-tuple-element.54), channel_id=1, source_target_pairs={{0,8},{8,0},{16,24},{24,16},{1,9},{9,1},{17,25},{25,17},{2,10},{10... | collective-permute-start | bytes 73736 | tf_op jit(solution)/shard_map/ppermute | solution.py:830
  77.8 0.8 collective-permute-done.9.pair_in
  78.7 1.6 %collective-permute-start.10 = (f32[48,128]{1,0:T(8,128)S(1)}, f32[48,128]{1,0:T(8,128)S(1)}, u32[]{:S(2)}, u32[]{:S(2)}) collective-permute-start(f32[48,128]{1,0:T(8,128)S(1)} %fusion.1.sent), channel_id=1, source_target_pairs={{0,24},{8,16},{16,8},{24,0},{1,25},{9,17},{17,9},{25,1},{2,26},{10... | collective-permute-start | bytes 73736 | tf_op jit(solution)/shard_map/ppermute | solution.py:832
  80.3 1.6 %collective-permute-done.10.other_in = f32[48,128]{1,0:T(8,128)S(1)} collective-permute-done((f32[48,128]{1,0:T(8,128)S(1)}, f32[48,128]{1,0:T(8,128)S(1)}, u32[]{:S(2)}, u32[]{:S(2)}) %collective-permute-start.10) | collective-permute-done | bytes 24608 | tf_op jit(solution)/shard_map/ppermute | solution.py:832
  81.9 0.6 route.1
  82.5 0.0 copy-start.7
  82.5 0.3 collective-permute-start.11
  82.8 3.2 %plain.1.basis = f32[12,8,8,512]{3,2,1,0:T(8,128)S(1)} custom-call(f32[12,256,128]{2,1,0:T(8,128)S(1)} %get-tuple-element.50.basis), custom_call_target="tpu_custom_call" | custom-call | flops 1200000000 | tf_op jit(solution)/shard_map/plain/pallas_call | solution.py:923
  86.0 0.5 collective-permute-done.11.pair
  86.4 1.3 %collective-permute-start.12 = (f32[48,128]{1,0:T(8,128)S(1)}, f32[48,128]{1,0:T(8,128)S(1)}, u32[]{:S(2)}, u32[]{:S(2)}) collective-permute-start(f32[48,128]{1,0:T(8,128)S(1)} %fusion.sent), channel_id=1, source_target_pairs={{0,7},{1,2},{2,1},{3,4},{4,3},{5,6},{6,5},{7,0},{8,15},{9,10},{10,... | collective-permute-start | bytes 73736 | tf_op jit(solution)/shard_map/ppermute | solution.py:937
  87.7 0.1 hot.1
  87.9 5.1 %collective-permute-done.12.other = f32[48,128]{1,0:T(8,128)S(1)} collective-permute-done((f32[48,128]{1,0:T(8,128)S(1)}, f32[48,128]{1,0:T(8,128)S(1)}, u32[]{:S(2)}, u32[]{:S(2)}) %collective-permute-start.12) | collective-permute-done | bytes 24608 | tf_op jit(solution)/shard_map/ppermute | solution.py:937
  93.0 2.5 %finish.1 = (f32[3,8,8,512]{3,2,1,0:T(8,128)}, f32[3,16384]{1,0:T(4,128)}) custom-call(s32[7]{0:T(128)S(1)} %stack.47.place.inside, f32[40,128]{1,0:T(8,128)S(1)} %get-tuple-element.47.keep, f32[48,128]{1,0:T(8,128)S(1)} %collective-permute-done.11.pair, f32[48,128]{1,0:T(8,128)S(1)} %fusion.sent, f32[48,128]{1,0:T(8,128)S(1)} %collective-permute-done.12.other, ...), custom_call_target="tpu_custom_call" | custom-call | flops 800000000 | tf_op jit(solution)/shard_map/finish/pallas_call | solution.py:938
  (16 shorter events, 0.1 us)
Async XLA Ops:
  0.6 7.6 %copy-start.3 = (s32[1,3,3,8192]{3,0,2,1:T(1,128)S(1)}, s32[1,3,3,8192]{3,0,2,1:T(1,128)}, u32[]{:S(2)}) copy-start(s32[1,3,3,8192]{3,0,2,1:T(1,128)} %param.10) | copy-start | bytes 884740
  0.6 7.6 %copy-start.4 = (f32[8,8,512]{2,1,0:T(8,128)S(1)}, f32[8,8,512]{2,1,0:T(8,128)}, u32[]{:S(2)}) copy-start(f32[8,8,512]{2,1,0:T(8,128)} %rigid.1) | copy-start | bytes 393220
  0.6 7.6 %copy-start.5 = (f32[16384]{0:T(1024)S(1)}, f32[16384]{0:T(1024)}, u32[]{:S(2)}) copy-start(f32[16384]{0:T(1024)} %param.9) | copy-start | bytes 196612
  5.8 13.5 %collective-permute-start = (f32[288,128]{1,0:T(8,128)}, f32[288,128]{1,0:T(8,128)S(1)}, u32[]{:S(2)}, u32[]{:S(2)}) collective-permute-start(f32[288,128]{1,0:T(8,128)} %depart.1), channel_id=1, source_target_pairs={{0,8},{8,16},{16,24},{1,9},{9,17},{17,25},{2,10},{10,18},{18,26},{... | collective-permute-start | bytes 442376 | tf_op jit(solution)/shard_map/ppermute | solution.py:859
  11.8 5.0 %copy-start = (s32[4,8,8,512]{3,2,1,0:T(8,128)S(1)}, s32[4,8,8,512]{3,2,1,0:T(8,128)}, u32[]{:S(2)}) copy-start(s32[4,8,8,512]{3,2,1,0:T(8,128)} %shift) | copy-start | bytes 1572868
  11.9 4.9 %copy-start.1 = (s32[4,8,8,512]{3,2,1,0:T(8,128)S(1)}, s32[4,8,8,512]{3,2,1,0:T(8,128)}, u32[]{:S(2)}) copy-start(s32[4,8,8,512]{3,2,1,0:T(8,128)} %bucket.1) | copy-start | bytes 1572868
  11.9 7.4 %collective-permute-start.1 = (f32[288,128]{1,0:T(8,128)S(1)}, f32[288,128]{1,0:T(8,128)S(1)}, u32[]{:S(2)}, u32[]{:S(2)}) collective-permute-start(f32[288,128]{1,0:T(8,128)S(1)} %get-tuple-element.29), channel_id=1, source_target_pairs={{8,0},{16,8},{24,16},{9,1},{17,9},{25,17},{10,2},{18,10},{26,18},{... | collective-permute-start | bytes 442376 | tf_op jit(solution)/shard_map/ppermute | solution.py:864
  19.8 5.6 %collective-permute-start.2 = (f32[312,128]{1,0:T(8,128)S(1)}, f32[312,128]{1,0:T(8,128)S(1)}, u32[]{:S(2)}, u32[]{:S(2)}) collective-permute-start(f32[312,128]{1,0:T(8,128)S(1)} %get-tuple-element.34), channel_id=1, source_target_pairs={{0,1},{1,0},{2,3},{3,2},{4,5},{5,4},{6,7},{7,6},{8,9},{9,8},{10,11... | collective-permute-start | bytes 479240 | tf_op jit(solution)/shard_map/ppermute | solution.py:879
  25.5 6.8 %collective-permute-start.3 = (f32[312,128]{1,0:T(8,128)S(1)}, f32[312,128]{1,0:T(8,128)S(1)}, u32[]{:S(2)}, u32[]{:S(2)}) collective-permute-start(f32[312,128]{1,0:T(8,128)S(1)} %get-tuple-element.38), channel_id=1, source_target_pairs={{1,2},{2,1},{3,4},{4,3},{5,6},{6,5},{9,10},{10,9},{11,12},{12,11},... | collective-permute-start | bytes 479240 | tf_op jit(solution)/shard_map/ppermute | solution.py:885
  26.1 6.1 %copy-start.2 = (f32[4,8,8,512]{3,2,1,0:T(8,128)S(1)}, f32[4,8,8,512]{3,2,1,0:T(8,128)}, u32[]{:S(2)}) copy-start(f32[4,8,8,512]{3,2,1,0:T(8,128)} %factor.1) | copy-start | bytes 1572868
  39.0 5.9 %collective-permute-start.4 = (f32[5,32,128]{2,1,0:T(8,128)S(1)}, f32[5,32,128]{2,1,0:T(8,128)S(1)}, u32[]{:S(2)}, u32[]{:S(2)}) collective-permute-start(f32[5,32,128]{2,1,0:T(8,128)S(1)} %get-tuple-element.57), channel_id=1, source_target_pairs={{0,8},{8,16},{16,24},{1,9},{9,17},{17,25},{2,10},{10,18},{18,26},{... | collective-permute-start | bytes 245768 | tf_op jit(solution)/shard_map/ppermute | solution.py:798
  43.6 5.3 %collective-permute-start.5 = (f32[5,32,128]{2,1,0:T(8,128)S(1)}, f32[5,32,128]{2,1,0:T(8,128)S(1)}, u32[]{:S(2)}, u32[]{:S(2)}) collective-permute-start(f32[5,32,128]{2,1,0:T(8,128)S(1)} %get-tuple-element.56), channel_id=1, source_target_pairs={{8,0},{16,8},{24,16},{9,1},{17,9},{25,17},{10,2},{18,10},{26,18},{... | collective-permute-start | bytes 245768 | tf_op jit(solution)/shard_map/ppermute | solution.py:798
  49.5 10.5 %collective-permute-start.6 = (f32[240,128]{1,0:T(8,128)S(1)}, f32[240,128]{1,0:T(8,128)S(1)}, u32[]{:S(2)}, u32[]{:S(2)}) collective-permute-start(f32[240,128]{1,0:T(8,128)S(1)} %get-tuple-element.40), channel_id=1, source_target_pairs={{0,1},{1,0},{2,3},{3,2},{4,5},{5,4},{6,7},{7,6},{8,9},{9,8},{10,11... | collective-permute-start | bytes 368648 | tf_op jit(solution)/shard_map/ppermute | solution.py:816
  57.1 14.6 %copy-start.6 = (s32[1,3,3,128]{3,0,2,1:T(1,128)S(1)}, s32[1,3,3,128]{3,0,2,1:T(1,128)}, u32[]{:S(2)}) copy-start(s32[1,3,3,128]{3,0,2,1:T(1,128)} %param.15) | copy-start | bytes 13828
  57.1 14.6 %copy-start.8 = (s32[1,9]{1,0:T(1,128)S(1)}, s32[1,9]{1,0:T(1,128)}, u32[]{:S(2)}) copy-start(s32[1,9]{1,0:T(1,128)} %tally.1) | copy-start | bytes 112
  57.1 2.9 %collective-permute-start.7 = (f32[240,128]{1,0:T(8,128)S(1)}, f32[240,128]{1,0:T(8,128)S(1)}, u32[]{:S(2)}, u32[]{:S(2)}) collective-permute-start(f32[240,128]{1,0:T(8,128)S(1)} %get-tuple-element.41), channel_id=1, source_target_pairs={{1,2},{2,1},{3,4},{4,3},{5,6},{6,5},{9,10},{10,9},{11,12},{12,11},... | collective-permute-start | bytes 368648 | tf_op jit(solution)/shard_map/ppermute | solution.py:816
  64.1 12.2 %collective-permute-start.8 = (f32[8,128]{1,0:T(8,128)S(1)}, f32[8,128]{1,0:T(8,128)S(1)}, u32[]{:S(2)}, u32[]{:S(2)}) collective-permute-start(f32[8,128]{1,0:T(8,128)S(1)} %get-tuple-element.45), channel_id=1, source_target_pairs={{0,4},{1,5},{2,6},{3,7},{4,0},{5,1},{6,2},{7,3},{8,12},{9,13},{10,... | collective-permute-start | bytes 12296 | tf_op jit(solution)/shard_map/ppermute | solution.py:823
  76.4 2.3 %collective-permute-start.9 = (f32[48,128]{1,0:T(8,128)S(1)}, f32[48,128]{1,0:T(8,128)S(1)}, u32[]{:S(2)}, u32[]{:S(2)}) collective-permute-start(f32[48,128]{1,0:T(8,128)S(1)} %get-tuple-element.54), channel_id=1, source_target_pairs={{0,8},{8,0},{16,24},{24,16},{1,9},{9,1},{17,25},{25,17},{2,10},{10... | collective-permute-start | bytes 73736 | tf_op jit(solution)/shard_map/ppermute | solution.py:830
  78.7 3.3 %collective-permute-start.10 = (f32[48,128]{1,0:T(8,128)S(1)}, f32[48,128]{1,0:T(8,128)S(1)}, u32[]{:S(2)}, u32[]{:S(2)}) collective-permute-start(f32[48,128]{1,0:T(8,128)S(1)} %fusion.1.sent), channel_id=1, source_target_pairs={{0,24},{8,16},{16,8},{24,0},{1,25},{9,17},{17,9},{25,1},{2,26},{10... | collective-permute-start | bytes 73736 | tf_op jit(solution)/shard_map/ppermute | solution.py:832
  82.5 5.2 %copy-start.7 = (s32[1,3,3,128]{3,0,2,1:T(1,128)S(1)}, s32[1,3,3,128]{3,0,2,1:T(1,128)}, u32[]{:S(2)}) copy-start(s32[1,3,3,128]{3,0,2,1:T(1,128)} %param.17) | copy-start | bytes 13828
  82.5 3.9 %collective-permute-start.11 = (f32[48,128]{1,0:T(8,128)S(1)}, f32[48,128]{1,0:T(8,128)S(1)}, u32[]{:S(2)}, u32[]{:S(2)}) collective-permute-start(f32[48,128]{1,0:T(8,128)S(1)} %get-tuple-element.48), channel_id=1, source_target_pairs={{0,1},{1,0},{2,3},{3,2},{4,5},{5,4},{6,7},{7,6},{8,9},{9,8},{10,11... | collective-permute-start | bytes 73736 | tf_op jit(solution)/shard_map/ppermute | solution.py:935
  86.4 6.5 %collective-permute-start.12 = (f32[48,128]{1,0:T(8,128)S(1)}, f32[48,128]{1,0:T(8,128)S(1)}, u32[]{:S(2)}, u32[]{:S(2)}) collective-permute-start(f32[48,128]{1,0:T(8,128)S(1)} %fusion.sent), channel_id=1, source_target_pairs={{0,7},{1,2},{2,1},{3,4},{4,3},{5,6},{6,5},{7,0},{8,15},{9,10},{10,... | collective-permute-start | bytes 73736 | tf_op jit(solution)/shard_map/ppermute | solution.py:937
